TPU v7x, 32 devices: a whole 2x2x4 slice. The times are simulated.
32 devices in a mesh: gx: 8 (over y, x, core), yz: 4 (over z).
Axes of the slice: x: 2, y: 2, z: 4, core: 2. Of those that a mesh axis runs over, the one named last changes fastest.
Arguments:
- vel: float32 [3, 48, 192, 1024], P(None, 'gx', 'yz'), may hold values from -6 to 6
- q_old: float32 [3, 48, 192, 1024], P(None, 'gx', None, 'yz'), may hold values from -6 to 6
- pressure_guess: float32 [48, 192, 1024], P('gx', None, 'yz'), may hold values from -6 to 6
- shear_shift: int32 [1], replicated, may hold values from 0 to 1023
Outputs:
- vel_next: float32 [3, 48, 192, 1024], P(None, 'gx', 'yz')
- q_next: float32 [3, 48, 192, 1024], P(None, 'gx', None, 'yz')
- pressure: float32 [48, 192, 1024], P('gx', None, 'yz')
All inputs are finite; a program needn't handle non-finite values.
Results may differ from a plain program's by a relative error of at most 0.00013.
Values sent between devices are 32-bit elements; how exact they have to be, the bound alone decides.
No kernel may reach another device: no remote copies, remote signals or barrier semaphores. Data moves between devices by JAX's collectives and lax.ppermute only.
A program may use at most 128 MiB of HBM per device.

v0:
```python
import math

import jax
import jax.numpy as jnp
from jax import lax
from jax.experimental import pallas as pl
from jax.experimental.pallas import tpu as pltpu
from jax.sharding import PartitionSpec as P


SWEEPS = 2
viscosity = 0.05
time_step = 0.2
keep_weight = -5.0 / 9.0
section_weight = 15.0 / 16.0
shear_param = 1.5
fraction = 0.375
f32 = jnp.float32
bf16 = jnp.bfloat16
COST_SCALE = 250_000_000


def params(mib, n=1):
    return pltpu.CompilerParams(
        vmem_limit_bytes=mib * 1024 * 1024, dimension_semantics=("arbitrary",) * n
    )


def cost(us):
    return pl.CostEstimate(flops=int(us * COST_SCALE), bytes_accessed=0, transcendentals=0)


def split_const(matrix):
    high = lax.reduce_precision(matrix, 8, 7)
    return high.astype(bf16), (matrix - high).astype(bf16)


def split_value(value):
    high = value.astype(bf16)
    return high, (value - high.astype(f32)).astype(bf16)


def dot3(a, b, contract=((1,), (0,))):
    dims = (contract, ((), ()))

    def one(x, y):
        return lax.dot_general(x, y, dims, preferred_element_type=f32)

    return one(a[0], b[0]) + one(a[0], b[1]) + one(a[1], b[0])


def full_spec(shape):
    zeros = (0,) * len(shape)
    return pl.BlockSpec(shape, lambda *_: zeros)


def lane_sign(half):
    lanes = lax.broadcasted_iota(jnp.int32, (1, 2 * half), 1)
    return jnp.where(lanes < half, -1.0, 1.0).astype(f32)


def rot(value, half):
    return pltpu.roll(value, half, axis=1) * lane_sign(half)


def y_matrix(width_y, modes, weights):
    step = 32
    count, half = modes.shape
    k = jnp.concatenate([modes, modes], axis=1).reshape(1, -1)
    phase = jnp.concatenate([jnp.zeros((count, half)), jnp.ones((count, half))], axis=1)
    phase = (0.5 * math.pi * phase).reshape(1, -1).astype(f32)
    unit = 2.0 * math.pi / width_y
    a = jnp.arange(width_y // step, dtype=jnp.int32)[:, None] * step
    b = jnp.arange(step, dtype=jnp.int32)[:, None]
    angle_a = unit * (a * k % width_y).astype(f32)
    angle_b = unit * (b * k % width_y).astype(f32) + phase
    w = jnp.concatenate([weights, weights], axis=1).reshape(1, -1) / math.sqrt(width_y)
    ca, sa = jnp.cos(angle_a) * w, jnp.sin(angle_a) * w
    cb, sb = jnp.cos(angle_b), jnp.sin(angle_b)
    ca, sa, cb, sb = lax.optimization_barrier((ca, sa, cb, sb))
    full = ca[:, None, :] * cb[None] - sa[:, None, :] * sb[None]
    return split_const(full.reshape(width_y, -1))


def z_angles(depth_z, rows_m, cols_z):
    return (
        2.0
        * math.pi
        / depth_z
        * (rows_m[:, None] * cols_z[None, :] % depth_z).astype(f32)
    )


def spectra_body(comp, omega, half, jobs, comps, n_out, bg_ref, *rest):
    vels = dict(zip(comps, rest))
    rest = rest[len(comps) :]
    ui, u0, u1, u2 = vels[comp], vels.get(0), vels.get(1), vels.get(2)
    has_w = any("w" in want for want in jobs)
    has_c = any("c" in want for want in jobs)
    if has_w:
        n_h = 2 if comp == 0 else 4
        halos, rest = rest[:n_h], rest[n_h:]
    mats, rest = rest[: 3 * len(jobs)], rest[3 * len(jobs) :]
    outs, buf = rest[:-1], rest[-1]
    _, X, Rz, NY = ui.shape
    d1 = (0.0, 45.0 / 60.0, -9.0 / 60.0, 1.0 / 60.0)
    d2 = (-490.0 / 180.0, 270.0 / 180.0, -27.0 / 180.0, 2.0 / 180.0)
    step = min(512, NY)
    base = 1 if has_c else 0

    def pick(i, at, rows, cols):
        if 0 <= at < X:
            return vels[i][0, at, rows, cols]
        ref = halos[(0 if i == 0 else 2) + (0 if at < 0 else 1)]
        return ref[0, at + 3 if at < 0 else at - X, rows, cols]

    def tile(r, carry):
        rows = pl.ds(pl.multiple_of(r * 8, 8), 8)
        for x in range(X):
            for at in range(0, NY, step):
                cols = slice(at, at + step)
                u = ui[0, x, rows, cols]
                if has_c:
                    buf[0, x, rows, cols] = -u2[0, x, rows, cols] * u
                buf[base, x, rows, cols] = u
                if has_w:
                    acc = (viscosity * d2[0]) * u
                    for o in (1, 2, 3):
                        up = pick(comp, x + o, rows, cols)
                        dn = pick(comp, x - o, rows, cols)
                        if comp == 0:
                            xp, xm = up, dn
                        else:
                            xp = pick(0, x + o, rows, cols)
                            xm = pick(0, x - o, rows, cols)
                        acc = acc + (viscosity * d2[o]) * (up + dn)
                        acc = acc - d1[o] * (xp * up - xm * dn)
                    if comp == 0:
                        acc = acc + (2.0 * omega) * u1[0, x, rows, cols]
                    if comp == 1:
                        acc = acc - ((2.0 - shear_param) * omega) * u0[0, x, rows, cols]
                    buf[base + 1, x, rows, cols] = acc
                    buf[base + 2, x, rows, cols] = -(u1[0, x, rows, cols] + bg_ref[x]) * u
        return carry

    lax.fori_loop(0, Rz // 8, tile, 0)
    M = X * Rz
    wide = 2 * half
    for n, want in enumerate(jobs):
        lo = 0 if "c" in want else base
        hi = base + (3 if "w" in want else 1)
        lhs = buf[lo:hi].reshape((hi - lo) * M, NY)
        res = dot3(split_value(lhs), (mats[3 * n][...], mats[3 * n + 1][...]))
        vec_ref = mats[3 * n + 2]
        u_at = (base - lo) * M
        at = 0
        for out in outs[n * n_out : (n + 1) * n_out]:
            for j in range(out.shape[-1] // wide):
                cols = slice(at, at + wide)
                own = slice(j * wide, (j + 1) * wide)
                yu = res[u_at : u_at + M, cols]
                if "c" in want:
                    out[0, :, :, own] = yu.reshape(X, Rz, wide)
                    out[1, :, :, own] = res[:M, cols].reshape(X, Rz, wide)
                if "w" in want:
                    k = u_at + M
                    ky = vec_ref[0:1, cols]
                    w = (
                        res[k : k + M, cols]
                        + ky * rot(res[k + M : k + 2 * M, cols], half)
                        - (viscosity * ky * ky) * yu
                    )
                    out[len(want) - 1, :, :, own] = w.reshape(X, Rz, wide)
                at += wide


def spectra_call(comp, jobs, vel, ghost, background, omega, mats, widths, half, us):
    _, X, Rz, NY = vel.shape
    has_w = any("w" in want for want in jobs)
    has_c = any("c" in want for want in jobs)
    comps = sorted({comp} | ({2} if has_c else set()) | ({0, 1} if has_w else set()))
    plane = lambda i: pl.BlockSpec((1, X, Rz, NY), lambda *_: (i, 0, 0, 0))
    halos, halo_specs = [], []
    if has_w:
        halos = list(ghost[0]) + (list(ghost[1]) if comp else [])
        block = (1,) + halos[0].shape[1:]
        halo_specs = [pl.BlockSpec(block, lambda *_: (0, 0, 0, 0))] * 2
        if comp:
            halo_specs += [pl.BlockSpec(block, lambda *_: (comp - 1, 0, 0, 0))] * 2
    count = (2 if has_c else 1) + (2 if has_w else 0)
    flat = [a for m in mats for a in m]
    shapes = [(len(want), X, Rz, w) for want in jobs for w in widths]
    return pl.pallas_call(
        lambda *refs: spectra_body(comp, omega, half, jobs, comps, len(widths), *refs),
        grid=(1,),
        in_specs=[pl.BlockSpec(memory_space=pltpu.SMEM)]
        + [plane(c) for c in comps]
        + halo_specs
        + [full_spec(a.shape) for a in flat],
        out_specs=[full_spec(shape) for shape in shapes],
        out_shape=[jax.ShapeDtypeStruct(shape, f32) for shape in shapes],
        scratch_shapes=[pltpu.VMEM((count, X, Rz, NY), f32)],
        compiler_params=params(50),
        cost_estimate=cost(us),
        name="spectra",
    )(background, *([vel] * len(comps)), *halos, *flat)


def z_body(counts, n_t, half, mh_ref, ml_ref, *rest):
    n_in = len(counts)
    ins, outs, buf = rest[:n_in], rest[n_in : n_in + n_t], rest[-1]
    _, X, Rz, _ = ins[0].shape
    wide = 2 * half
    depth = outs[0].shape[1]
    for t in range(n_t):
        own = slice(t * wide, (t + 1) * wide)
        at = 0
        for ref, count in zip(ins, counts):
            for f in range(count):
                for x in range(X):
                    col = (t * X + x) * wide
                    buf[at : at + Rz, col : col + wide] = ref[f, x, :, own]
                at += Rz
    res = dot3((mh_ref[...], ml_ref[...]), split_value(buf[...]))
    for t in range(n_t):
        for x in range(X):
            col = (t * X + x) * wide
            cols = slice(col, col + wide)
            outs[t][x] = res[:depth, cols] + rot(res[depth:, cols], half)


def z_call(m_pair, ins, n_t, half):
    flat = [a for source in ins for a in source]
    counts = [a.shape[0] for a in flat]
    _, X, Rz, _ = flat[0].shape
    depth = m_pair[0].shape[0] // 2
    return pl.pallas_call(
        lambda *refs: z_body(counts, n_t, half, *refs),
        out_shape=[jax.ShapeDtypeStruct((X, depth, 2 * half), f32)] * n_t,
        scratch_shapes=[pltpu.VMEM((sum(counts) * Rz, n_t * X * 2 * half), f32)],
        compiler_params=params(24, 0),
        cost_estimate=cost(4),
        name="zforward",
    )(*m_pair, *flat)


def shear_body(meta, up, down, up_out, down_out):
    NY = up.shape[-1]
    shift = meta[0]

    def one(flag, ref, out, by, by_next):
        @pl.when(flag == 1)
        def _():
            v = ref[0, 0]
            out[0, 0] = (1.0 - fraction) * pltpu.roll(v, by, 1) + fraction * pltpu.roll(v, by_next, 1)

        @pl.when(flag == 0)
        def _():
            out[0, 0] = ref[0, 0]

    one(meta[1], up, up_out, (NY - shift) % NY, (2 * NY - shift - 1) % NY)
    one(meta[2], down, down_out, shift % NY, (shift + 1) % NY)


def shear_call(meta, up, down):
    n, w, Rz, NY = up.shape
    spec = pl.BlockSpec((1, 1, Rz, NY), lambda i, x: (i, x, 0, 0))
    return pl.pallas_call(
        shear_body,
        grid=(n, w),
        in_specs=[pl.BlockSpec(memory_space=pltpu.SMEM), spec, spec],
        out_specs=[spec, spec],
        out_shape=[jax.ShapeDtypeStruct(up.shape, f32)] * 2,
        compiler_params=params(16, 2),
        cost_estimate=cost(3),
        name="shear",
    )(meta, up, down)


def blocks_of(depth):
    return 4 if depth % 32 == 0 else 1


def row_block(lead, rows, wide):
    zeros = (0,) * len(lead)
    return pl.BlockSpec(tuple(lead) + (rows, wide), lambda b: zeros + (b, 0))


def add_parts(parts, x, rows):
    v = parts[0][x, rows]
    for p in parts[1:]:
        v = v + p[x, rows]
    return v


def prep_body(n_part, half, vec_ref, kz_ref, *rest):
    parts = [rest[i * n_part : (i + 1) * n_part] for i in range(3)]
    up, down = rest[3 * n_part :]
    X, depth = parts[0][0].shape[:2]
    ky = vec_ref[0:1]

    def tile(r, carry):
        rows = pl.ds(pl.multiple_of(r * 8, 8), 8)
        kz = kz_ref[rows]
        for x in range(X):
            if x < 3 or x >= X - 3:
                t = add_parts(parts[0], x, rows)
                if x < 3:
                    down[x, rows] = t
                if x >= X - 3:
                    up[x - X + 3, rows] = t
            if x < 2 or x >= X - 2:
                d = rot(ky * add_parts(parts[1], x, rows) + kz * add_parts(parts[2], x, rows), half)
                if x < 2:
                    down[3 + x, rows] = d
                if x >= X - 2:
                    up[3 + x - X + 2, rows] = d
        return carry

    lax.fori_loop(0, depth // 8, tile, 0)


def prep_call(parts, vec, kz, half):
    X, depth, wide = parts[0][0].shape
    n = len(parts[0])
    nb = blocks_of(depth)
    rows = depth // nb
    flat = [a for p in parts for a in p]
    return pl.pallas_call(
        lambda *refs: prep_body(n, half, *refs),
        grid=(nb,),
        in_specs=[full_spec(vec.shape), row_block((), rows, wide)]
        + [row_block((X,), rows, wide)] * len(flat),
        out_specs=[row_block((5,), rows, wide)] * 2,
        out_shape=[jax.ShapeDtypeStruct((5, depth, wide), f32)] * 2,
        compiler_params=params(24),
        cost_estimate=cost(4),
        name="prep",
    )(vec, kz, *flat)


def take_chunk(ref, lead, rows, chunk, half):
    total = ref.shape[-1]
    if total == 2 * half:
        return ref[lead + (rows,)]
    wide = 2 * half
    assert total == 2 * wide
    re = ref[lead + (rows, slice(0, wide))]
    im = ref[lead + (rows, slice(wide, total))]
    low = lax.broadcasted_iota(jnp.int32, (1, wide), 1) < half
    if chunk == 0:
        return jnp.where(low, re, pltpu.roll(im, half, axis=1))
    return jnp.where(low, pltpu.roll(re, half, axis=1), im)


def solve_body(chunk, half, n_slot, n_part, nb, vec_ref, kz_ref, inv_ref, mh_ref, ml_ref, fl, fr, p0, p0l, p0r, q_old, *rest):
    parts = [rest[i * n_part : (i + 1) * n_part] for i in range(3)]
    rest = rest[3 * n_part :]
    q_out, p_out = rest[:2]
    outs, buf = rest[2:-1], rest[-1]
    X, depth = p_out.shape[:2]
    wide = 2 * half
    ky = vec_ref[0:1]
    cl, sl = vec_ref[1:2], vec_ref[2:3]
    cr, sr = vec_ref[3:4], vec_ref[4:5]
    step = pl.program_id(0)

    def left(v):
        return v * cl + rot(v, half) * sl

    def right(v):
        return v * cr + rot(v, half) * sr

    def tile(r, carry):
        rows = pl.ds(pl.multiple_of(r * 8, 8), 8)
        whole = pl.ds(pl.multiple_of(step * depth + r * 8, 8), 8)
        kz = kz_ref[rows]
        inv = inv_ref[rows]
        tx, ty, tz, dd, pp = {}, {}, {}, {}, {}
        for x in range(X):
            tx[x] = add_parts(parts[0], x, rows)
            ty[x] = add_parts(parts[1], x, rows)
            tz[x] = add_parts(parts[2], x, rows)
            dd[x] = rot(ky * ty[x] + kz * tz[x], half)
            pp[x] = take_chunk(p0, (x,), rows, chunk, half)
        for o in range(3):
            tx[o - 3] = left(fl[o, rows])
            tx[X + o] = right(fr[o, rows])
            pp[o - 3] = left(take_chunk(p0l, (o,), rows, chunk, half))
            pp[X + o] = right(take_chunk(p0r, (o,), rows, chunk, half))
        for o in range(2):
            dd[o - 2] = left(fl[3 + o, rows])
            dd[X + o] = right(fr[3 + o, rows])
        div = {x: 0.5 * (tx[x + 1] - tx[x - 1]) + dd[x] for x in range(-2, X + 2)}
        for sweep in range(SWEEPS):
            reach = SWEEPS - sweep
            pp = {
                x: (pp[x + 1] + pp[x - 1] - div[x]) * inv
                for x in range(-reach, X + reach)
            }
        for x in range(X):
            p = pp[x]
            p_out[x, rows] = p
            ip = rot(p, half)
            grad = (0.5 * (pp[x + 1] - pp[x - 1]), ky * ip, kz * ip)
            for i, now in enumerate((tx[x], ty[x], tz[x])):
                old = take_chunk(q_old, (i, x), rows, chunk, half)
                q = keep_weight * old + time_step * (now - grad[i])
                q_out[i, x, rows] = q
                buf[i, whole, x * wide : (x + 1) * wide] = q
        return carry

    lax.fori_loop(0, depth // 8, tile, 0)

    @pl.when(step == nb - 1)
    def _():
        total = depth * nb
        Rz = total // n_slot
        mats = (mh_ref[...], ml_ref[...])
        for i in range(3):
            res = dot3(mats, split_value(buf[i]))
            for x in range(X):
                cols = slice(x * wide, (x + 1) * wide)
                h = res[:total, cols] + rot(res[total:, cols], half)
                for s in range(n_slot):
                    piece = h[s * Rz : (s + 1) * Rz]
                    if len(outs) == n_slot:
                        outs[s][i, x] = piece
                    else:
                        outs[i * n_slot + s][0, x] = piece


def solve_call(chunk, half, n_slot, split, vec, kz, inv, m_pair, parts, fl, fr, p0, p0l, p0r, q_old):
    X, depth, wide = parts[0][0].shape
    nb = blocks_of(depth)
    rows = depth // nb
    n = len(parts[0])
    flat = [a for p in parts for a in p]
    packed = p0.shape[-1]
    lead = 1 if split else 3
    n_h = n_slot * (3 if split else 1)
    h_shape = (lead, X, depth // n_slot, wide)
    out = pl.pallas_call(
        lambda *refs: solve_body(chunk, half, n_slot, n, nb, *refs),
        grid=(nb,),
        in_specs=[
            full_spec(vec.shape),
            row_block((), rows, wide),
            row_block((), rows, wide),
            full_spec(m_pair[0].shape),
            full_spec(m_pair[1].shape),
            row_block((5,), rows, wide),
            row_block((5,), rows, wide),
            row_block((X,), rows, packed),
            row_block((3,), rows, packed),
            row_block((3,), rows, packed),
            row_block((3, X), rows, packed),
        ]
        + [row_block((X,), rows, wide)] * len(flat),
        out_specs=[row_block((3, X), rows, wide), row_block((X,), rows, wide)]
        + [full_spec(h_shape)] * n_h,
        out_shape=[
            jax.ShapeDtypeStruct((3, X, depth, wide), f32),
            jax.ShapeDtypeStruct((X, depth, wide), f32),
        ]
        + [jax.ShapeDtypeStruct(h_shape, f32)] * n_h,
        scratch_shapes=[pltpu.VMEM((3, depth, X * wide), f32)],
        compiler_params=params(40),
        cost_estimate=cost(10),
        name="solve",
    )(vec, kz, inv, *m_pair, fl, fr, p0, p0l, p0r, q_old, *flat)
    q, p, hs = out[0], out[1], list(out[2:])
    if split:
        return q, p, [hs[i * n_slot : (i + 1) * n_slot] for i in range(3)]
    return q, p, [hs]


def back_body(n_slot, base_ref, gh_ref, gl_ref, *rest):
    hs, out = rest[:n_slot], rest[-1]
    _, X, Rz, wide = hs[0].shape
    lhs = jnp.concatenate([h[...].reshape(X * Rz, wide) for h in hs], axis=1)
    res = dot3(split_value(lhs), (gh_ref[...], gl_ref[...]), ((1,), (1,)))
    out[...] = base_ref[...] + section_weight * res.reshape(out.shape)


def back_call(base, g_pair, hs, comp):
    _, X, Rz, NY = base.shape
    wide = hs[0].shape[-1]
    if comp is None:
        grid, at = (3,), lambda i: (i, 0, 0, 0)
        h_at = at
    else:
        grid, at = (1,), lambda i: (comp, 0, 0, 0)
        h_at = lambda i: (0, 0, 0, 0)
    return pl.pallas_call(
        lambda *refs: back_body(len(hs), *refs),
        grid=grid,
        in_specs=[pl.BlockSpec((1, X, Rz, NY), at), full_spec(g_pair[0].shape), full_spec(g_pair[1].shape)]
        + [pl.BlockSpec((1, X, Rz, wide), h_at)] * len(hs),
        out_specs=pl.BlockSpec((1, X, Rz, NY), at),
        out_shape=jax.ShapeDtypeStruct(base.shape, f32),
        input_output_aliases={} if comp is None else {0: 0},
        compiler_params=params(32),
        cost_estimate=cost(7),
        name="back",
    )(base, *g_pair, *hs)


def pack_body(half, a_ref, b_ref, out):
    wide = 2 * half
    low = lax.broadcasted_iota(jnp.int32, (1, wide), 1) < half
    for n in range(a_ref.shape[0]):
        a, b = a_ref[n], b_ref[n]
        out[n, :, 0:wide] = jnp.where(low, a, pltpu.roll(b, half, axis=1))
        out[n, :, wide : 2 * wide] = jnp.where(low, pltpu.roll(a, half, axis=1), b)


def pack_call(chunks, half):
    if len(chunks) == 1:
        return chunks[0]
    a, b = chunks
    lead, (depth, wide) = a.shape[:-2], a.shape[-2:]
    n = math.prod(lead)
    per = 3 if n % 3 == 0 else 1
    spec = lambda w: pl.BlockSpec((per, depth, w), lambda i: (i, 0, 0))
    out = pl.pallas_call(
        lambda *refs: pack_body(half, *refs),
        grid=(n // per,),
        in_specs=[spec(wide), spec(wide)],
        out_specs=spec(2 * wide),
        out_shape=jax.ShapeDtypeStruct((n, depth, 2 * wide), f32),
        compiler_params=params(16),
        cost_estimate=cost(5),
        name="pack",
    )(a.reshape(n, depth, wide), b.reshape(n, depth, wide))
    return out.reshape(lead + (depth, 2 * wide))


def ring(axis, shift):
    count = lax.axis_size(axis)
    return [(i, (i + shift) % count) for i in range(count)]


def after(value, *deps):
    return lax.optimization_barrier((value,) + deps)[0]


def local(vel, q_old, pressure_guess, shear_shift):
    X, Rz, NY = vel.shape[1:]
    depth = q_old.shape[2]
    G = lax.axis_size("yz")
    L = NY // (2 * G)
    half = 64 if L % 64 == 0 else L
    J = L // half
    wide = 2 * half
    g = lax.axis_index("yz")
    slab = lax.axis_index("gx")
    slabs = lax.axis_size("gx")
    total_x = X * slabs
    offset = shear_shift[0]
    omega = 2.0 / total_x
    paired = G == 4
    first, last = slab == 0, slab == slabs - 1

    if paired:
        slot_groups = jnp.stack([g, G - 1 - g, g ^ 1, G - 1 - (g ^ 1)])
        sources = jnp.stack([g, g ^ 1])
        n_t = 2
    else:
        slot_groups = (g + jnp.arange(G, dtype=jnp.int32)) % G
        sources = (g - jnp.arange(G, dtype=jnp.int32)) % G
        n_t = 1
    back_groups = (g - jnp.arange(G, dtype=jnp.int32)) % G
    widths = [n_t * wide] * (2 if paired else G)

    def modes_of(groups, j):
        return groups[:, None] * L + j * half + jnp.arange(half, dtype=jnp.int32)[None, :]

    unit_y = 2.0 * math.pi / NY

    def twice(a):
        return jnp.concatenate([a, a], axis=-1).reshape(1, -1)

    m = jnp.arange(depth, dtype=jnp.int32)
    signed = jnp.where(m < depth // 2, m, m - depth)
    kz1 = 2.0 * math.pi / depth * signed.astype(f32)
    kz = jnp.broadcast_to(kz1[:, None], (depth, wide))
    zloc = jnp.arange(Rz, dtype=jnp.int32)
    norm_z = 1.0 / math.sqrt(depth)
    kc = kz1[:, None]
    n_src = sources.shape[0]
    three = (n_src, 3, Rz)
    z_cols = jnp.broadcast_to((sources[:, None] * Rz + zloc[None, :])[:, None], three).reshape(-1)
    field = jnp.broadcast_to(jnp.arange(3, dtype=jnp.int32)[None, :, None], three).reshape(1, -1)
    ang = z_angles(depth, m, z_cols)
    cz, sz = jnp.cos(ang) * norm_z, jnp.sin(ang) * norm_z
    gain = jnp.where(field == 0, -viscosity * kc * kc, jnp.where(field == 1, kc, 1.0))
    real = gain * jnp.where(field == 1, sz, cz)
    imag = gain * jnp.where(field == 1, cz, -sz)
    m_fwd = split_const(jnp.concatenate([real, imag], axis=0))
    dest = (g + jnp.arange(G, dtype=jnp.int32)) % G
    z_rows = (dest[:, None] * Rz + zloc[None, :]).reshape(-1)
    ang_b = z_angles(depth, z_rows, m)
    m_inv = split_const(
        jnp.concatenate([jnp.cos(ang_b) * norm_z, jnp.sin(ang_b) * norm_z], axis=0)
    )
    xpos = (slab * X + jnp.arange(X, dtype=jnp.int32)).astype(f32) + 0.5 - total_x / 2.0
    background = -shear_param * omega * xpos

    f_pairs, kys = [], []
    for j in range(J):
        modes = modes_of(slot_groups, j)
        f_pairs.append(y_matrix(NY, modes, jnp.ones(modes.shape, f32)))
        kys.append(twice(unit_y * modes.astype(f32)))

    swap = [(i, i ^ 1) for i in range(G)]
    cross = [(i, G - 1 - i) for i in range(G)]

    def scatter(pieces):
        if paired:
            return [pieces[0], lax.ppermute(pieces[1], "yz", swap)]
        return [pieces[0]] + [
            lax.ppermute(pieces[s], "yz", ring("yz", s)) for s in range(1, len(pieces))
        ]

    token = []

    def chained(value):
        return after(value, *token) if token else value

    def mark(*arrays):
        token[:] = arrays

    def gather_z(sent):
        ins = [list(source) for source in zip(*sent)]
        got = z_call((chained(m_fwd[0]), m_fwd[1]), ins, n_t, half)
        mark(got[-1])
        if paired:
            return [got[0], lax.ppermute(got[1], "yz", cross)]
        return [got[0]]

    ghost = {}
    sends, parts, faces, solved = {}, {}, {}, {}
    meta = jnp.stack([offset, first.astype(jnp.int32), last.astype(jnp.int32)])

    def vel_halo(n, lo, hi):
        v = chained(vel)
        ghost[n] = (
            lax.ppermute(v[lo:hi, X - 3 :], "gx", ring("gx", 1)),
            lax.ppermute(v[lo:hi, :3], "gx", ring("gx", -1)),
        )

    def shear(n):
        ghost[n] = shear_call(chained(meta), *ghost[n])
        mark(*ghost[n])

    def spectra(i, *jobs, us=8):
        flat = spectra_call(
            i, [want for _, want in jobs], vel, ghost, chained(background), omega,
            [f_pairs[j] + (kys[j],) for j, _ in jobs], widths, half, us,
        )
        mark(flat[-1])
        n = len(widths)
        for at, (j, _) in enumerate(jobs):
            sends.setdefault((i, j), []).append(scatter(flat[at * n : (at + 1) * n]))

    def forward_z(i, j):
        parts[i, j] = gather_z(sends[i, j])

    p_halo = []

    def vectors(j):
        own = modes_of(g[None], j)
        ky = twice(unit_y * own.astype(f32))
        edge = unit_y * ((own * offset % NY).astype(f32) + fraction * own.astype(f32))
        ec, es = twice(jnp.cos(edge)), twice(jnp.sin(edge))
        vec = jnp.concatenate(
            [
                ky,
                jnp.where(first, ec, 1.0),
                jnp.where(first, es, 0.0),
                jnp.where(last, ec, 1.0),
                jnp.where(last, -es, 0.0),
                jnp.zeros((3, wide), f32),
            ],
            axis=0,
        )
        return vec, 1.0 / (2.0 + ky * ky + kz * kz)

    def prep(j):
        vec, inv = vectors(j)
        mine = [parts[i, j] for i in range(3)]
        up, down = prep_call(mine, chained(vec), kz, half)
        mark(up, down)
        faces[j] = (
            vec,
            inv,
            mine,
            lax.ppermute(up, "gx", ring("gx", 1)),
            lax.ppermute(down, "gx", ring("gx", -1)),
        )

    def solve(j, split):
        vec, inv, mine, fl, fr = faces[j]
        q, p, groups = solve_call(
            j, half, G, split, chained(vec), kz, inv, m_inv, mine, fl, fr,
            pressure_guess, p_halo[0], p_halo[1], q_old,
        )
        mark(q)
        solved[j] = (q, p, groups)

    def give_back(j):
        out = []
        for hs in solved[j][2]:
            got = [hs[0]]
            for s in range(1, G):
                got.append(lax.ppermute(hs[s], "yz", ring("yz", s)))
            out.append(got)
        return out

    def back_matrix(j):
        back_modes = modes_of(back_groups, j)
        weights = jnp.where(back_modes == 0, 1.0, 2.0).astype(f32)
        return y_matrix(NY, back_modes, weights)

    def guess_halo():
        guess = chained(pressure_guess)
        p_halo.append(lax.ppermute(guess[X - 3 :], "gx", ring("gx", 1)))
        p_halo.append(lax.ppermute(guess[:3], "gx", ring("gx", -1)))

    if J == 2:
        vel_halo(0, 0, 1)
        spectra(0, (0, "uc"), us=6)
        vel_halo(1, 1, 3)
        spectra(1, (0, "uc"), us=6)
        shear(0)
        spectra(0, (0, "w"))
        spectra(2, (0, "uc"), us=6)
        guess_halo()
        forward_z(0, 0)
        shear(1)
        spectra(1, (0, "w"))
        spectra(2, (0, "w"))
        forward_z(1, 0)
        spectra(0, (1, "ucw"))
        forward_z(2, 0)
        spectra(1, (1, "ucw"))
        forward_z(0, 1)
        spectra(2, (1, "ucw"))
        prep(0)
        forward_z(1, 1)
        solve(0, False)
        forward_z(2, 1)
        q, p, groups = solved[0]
        solved[0] = (q, p, [[chained(h) for h in hs] for hs in groups])
        got = give_back(0)
        prep(1)
        solve(1, False)
        got1 = give_back(1)
        base = chained(vel)
        result = back_call(base, back_matrix(0), got[0], None)
        result = back_call(result, back_matrix(1), got1[0], None)
    else:
        if J > 2:
            raise NotImplementedError
        guess_halo()
        vel_halo(0, 0, 1)
        vel_halo(1, 1, 3)
        shear(0)
        shear(1)
        result = vel
        for j in range(J):
            for i in range(3):
                spectra(i, (j, "ucw"))
                forward_z(i, j)
            prep(j)
            solve(j, False)
            result = back_call(result, back_matrix(j), give_back(j)[0], None)
    q_parts = [solved[j][0] for j in range(J)]
    p_parts = [solved[j][1] for j in range(J)]
    return result, pack_call(q_parts, half), pack_call(p_parts, half)


def solution(mesh):
    placed = (P(None, "gx", "yz", None), P(None, "gx", None, "yz"), P("gx", None, "yz"), P())
    return jax.shard_map(
        local,
        mesh=mesh,
        in_specs=placed,
        out_specs=(P(None, "gx", "yz", None), P(None, "gx", None, "yz"), P("gx", None, "yz")),
        check_vma=False,
    )
```

profile of v0, /device:TPU:8, one launch (start us, length us, event | category | flops | bytes accessed | tf_op | source)
XLA Modules:
  0.0 376.3 jit_solution(5726576005362081179)
XLA Ops:
  0.6 2.4 fusion.84
  3.1 2.6 collective-permute-start.1
  7.2 2.9 fusion.56
  14.7 4.9 %spectra.9 = (f32[2,6,48,256]{3,2,1,0:T(8,128)S(1)}, f32[2,6,48,256]{3,2,1,0:T(8,128)}) custom-call(f32[6]{0:T(128)S(1)} %add_multiply_fusion.2.refs_0_, f32[3,6,48,1024]{3,2,1,0:T(8,128)} %refs_0_, f32[3,6,48,1024]{3,2,1,0:T(8,128)} %refs_0_, bf16[1024,512]{1,0:T(8,128)(2,1)S(1)} %copy-done.4, bf16[1024,512]{1,0:T(8,128)(2,1)S(1)} %copy-done.2, ...), custom_call_target="tpu_custom_call" | custom-call | flops 1500000000 | tf_op jit(solution)/shard_map/spectra/pallas_call | solution.py:193
  21.1 3.1 collective-permute-start.5
  25.0 4.7 %spectra.10 = (f32[2,6,48,256]{3,2,1,0:T(8,128)S(1)}, f32[2,6,48,256]{3,2,1,0:T(8,128)}) custom-call(f32[6]{0:T(128)S(1)} %add_multiply_fusion.2.refs_0_, f32[3,6,48,1024]{3,2,1,0:T(8,128)} %refs_0_, f32[3,6,48,1024]{3,2,1,0:T(8,128)} %refs_0_, bf16[1024,512]{1,0:T(8,128)(2,1)S(1)} %copy-done.4, bf16[1024,512]{1,0:T(8,128)(2,1)S(1)} %copy-done.2, ...), custom_call_target="tpu_custom_call" | custom-call | flops 1500000000 | tf_op jit(solution)/shard_map/spectra/pallas_call | solution.py:193
  38.6 2.9 fusion.1
  43.6 2.6 shear.2
  46.2 5.9 %spectra.11 = (f32[1,6,48,256]{3,2,1,0:T(8,128)S(1)}, f32[1,6,48,256]{3,2,1,0:T(8,128)S(1)}) custom-call(f32[6]{0:T(128)S(1)} %add_multiply_fusion.2.refs_0_, f32[3,6,48,1024]{3,2,1,0:T(8,128)} %refs_0_, f32[3,6,48,1024]{3,2,1,0:T(8,128)} %refs_0_, f32[1,3,48,1024]{3,2,1,0:T(8,128)S(1)} %get-tuple-element.104.refs_3_.refs_4_, ...), custom_call_target="tpu_custom_call" | custom-call | flops 2000000000 | tf_op jit(solution)/shard_map/spectra/pallas_call | solution.py:193
  52.5 3.7 spectra.12
  58.1 6.2 %collective-permute-done.3.refs_5_ = f32[1,6,48,256]{3,2,1,0:T(8,128)S(1)} collective-permute-done((f32[1,6,48,256]{3,2,1,0:T(8,128)S(1)}, f32[1,6,48,256]{3,2,1,0:T(8,128)S(1)}, u32[]{:S(2)}, u32[]{:S(2)}) %collective-permute-start.3) | collective-permute-done | bytes 294944 | tf_op jit(solution)/shard_map/ppermute | solution.py:621
  64.3 4.1 %zforward.6 = (f32[6,192,128]{2,1,0:T(8,128)S(1)}, f32[6,192,128]{2,1,0:T(8,128)}) custom-call(bf16[384,288]{1,0:T(8,128)(2,1)S(1)} %get-tuple-element.155.refs_0_, bf16[384,288]{1,0:T(8,128)(2,1)S(1)} %get-tuple-element.205.refs_1_, f32[2,6,48,256]{3,2,1,0:T(8,128)S(1)} %copy-done.41, f32[1,6,48,256]{3,2,1,0:T(8,128)S(1)} %get-tuple-element.112.refs_3_, ...), custom_call_target="tpu_custom_call" | custom-call | flops 1000000000 | tf_op jit(solution)/shard_map/zforward/pallas_call | solution.py:237
  68.4 4.1 %shear.3 = (f32[2,3,48,1024]{3,2,1,0:T(8,128)S(1)}, f32[2,3,48,1024]{3,2,1,0:T(8,128)S(1)}) custom-call(s32[3]{0:T(128)S(1)} %pad_add_fusion.meta, f32[2,3,48,1024]{3,2,1,0:T(8,128)S(1)} %collective-permute-done.4.up, f32[2,3,48,1024]{3,2,1,0:T(8,128)} %collective-permute-done.5.down), custom_call_target="tpu_custom_call" | custom-call | flops 750000000 | tf_op jit(solution)/shard_map/shear/pallas_call | solution.py:268
  74.6 6.3 %spectra.13 = (f32[1,6,48,256]{3,2,1,0:T(8,128)S(1)}, f32[1,6,48,256]{3,2,1,0:T(8,128)S(1)}) custom-call(f32[6]{0:T(128)S(1)} %add_multiply_fusion.2.refs_0_, f32[3,6,48,1024]{3,2,1,0:T(8,128)} %refs_0_, f32[3,6,48,1024]{3,2,1,0:T(8,128)} %refs_0_, f32[1,3,48,1024]{3,2,1,0:T(8,128)S(1)} %get-tuple-element.104.refs_3_.refs_4_, ...), custom_call_target="tpu_custom_call" | custom-call | flops 2000000000 | tf_op jit(solution)/shard_map/spectra/pallas_call | solution.py:193
  83.0 6.4 %spectra.14 = (f32[1,6,48,256]{3,2,1,0:T(8,128)S(1)}, f32[1,6,48,256]{3,2,1,0:T(8,128)S(1)}) custom-call(f32[6]{0:T(128)S(1)} %add_multiply_fusion.2.refs_0_, f32[3,6,48,1024]{3,2,1,0:T(8,128)} %refs_0_, f32[3,6,48,1024]{3,2,1,0:T(8,128)} %refs_0_, f32[3,6,48,1024]{3,2,1,0:T(8,128)} %refs_0_, f32[1,3,48,1024]{3,2,1,0:T(8,128)S(1)} %get-tuple-element.104.refs_3_.refs_4_, ...), custom_call_target="tpu_custom_call" | custom-call | flops 2000000000 | tf_op jit(solution)/shard_map/spectra/pallas_call | solution.py:193
  90.1 3.0 zforward.7
  94.0 8.4 %spectra.15 = (f32[3,6,48,256]{3,2,1,0:T(8,128)S(1)}, f32[3,6,48,256]{3,2,1,0:T(8,128)}) custom-call(f32[6]{0:T(128)S(1)} %add_multiply_fusion.2.refs_0_, f32[3,6,48,1024]{3,2,1,0:T(8,128)} %refs_0_, f32[3,6,48,1024]{3,2,1,0:T(8,128)} %refs_0_, f32[3,6,48,1024]{3,2,1,0:T(8,128)} %refs_0_, f32[1,3,48,1024]{3,2,1,0:T(8,128)S(1)} %get-tuple-element.104.refs_3_.refs_4_, ...), custom_call_target="tpu_custom_call" | custom-call | flops 2000000000 | tf_op jit(solution)/shard_map/spectra/pallas_call | solution.py:193
  102.4 2.5 collective-permute-start.10
  104.9 3.0 zforward.8
  108.7 9.1 %spectra.16 = (f32[3,6,48,256]{3,2,1,0:T(8,128)S(1)}, f32[3,6,48,256]{3,2,1,0:T(8,128)}) custom-call(f32[6]{0:T(128)S(1)} %add_multiply_fusion.2.refs_0_, f32[3,6,48,1024]{3,2,1,0:T(8,128)} %refs_0_, f32[3,6,48,1024]{3,2,1,0:T(8,128)} %refs_0_, f32[3,6,48,1024]{3,2,1,0:T(8,128)} %refs_0_, f32[1,3,48,1024]{3,2,1,0:T(8,128)S(1)} %get-tuple-element.104.refs_3_.refs_4_, ...), custom_call_target="tpu_custom_call" | custom-call | flops 2000000000 | tf_op jit(solution)/shard_map/spectra/pallas_call | solution.py:193
  118.9 2.7 collective-permute-start.11
  125.1 4.1 %zforward.9 = (f32[6,192,128]{2,1,0:T(8,128)S(1)}, f32[6,192,128]{2,1,0:T(8,128)}) custom-call(bf16[384,288]{1,0:T(8,128)(2,1)S(1)} %copy-done.31, bf16[384,288]{1,0:T(8,128)(2,1)S(1)} %copy-done.29, f32[3,6,48,256]{3,2,1,0:T(8,128)S(1)} %copy-done.35, f32[3,6,48,256]{3,2,1,0:T(8,128)} %collective-permute-done.10.refs_3_), custom_call_target="tpu_custom_call" | custom-call | flops 1000000000 | tf_op jit(solution)/shard_map/zforward/pallas_call | solution.py:237
  130.1 7.9 %spectra.17 = (f32[3,6,48,256]{3,2,1,0:T(8,128)S(1)}, f32[3,6,48,256]{3,2,1,0:T(8,128)S(1)}) custom-call(f32[6]{0:T(128)S(1)} %add_multiply_fusion.2.refs_0_, f32[3,6,48,1024]{3,2,1,0:T(8,128)} %refs_0_, f32[3,6,48,1024]{3,2,1,0:T(8,128)} %refs_0_, f32[3,6,48,1024]{3,2,1,0:T(8,128)} %refs_0_, f32[1,3,48,1024]{3,2,1,0:T(8,128)S(1)} %get-tuple-element.104.refs_3_.refs_4_, ...), custom_call_target="tpu_custom_call" | custom-call | flops 2000000000 | tf_op jit(solution)/shard_map/spectra/pallas_call | solution.py:193
  138.0 2.3 collective-permute-done.11.refs_3_.refs_12_
  140.4 43.8 %collective-permute-done.13.refs_7_.refs_16_ = f32[6,192,128]{2,1,0:T(8,128)} collective-permute-done((f32[6,192,128]{2,1,0:T(8,128)}, f32[6,192,128]{2,1,0:T(8,128)}, u32[]{:S(2)}, u32[]{:S(2)}) %collective-permute-start.13) | collective-permute-done | bytes 589856 | tf_op jit(solution)/shard_map/ppermute | solution.py:639
  184.1 6.3 %collective-permute-done.12.refs_5_.refs_14_ = f32[6,192,128]{2,1,0:T(8,128)} collective-permute-done((f32[6,192,128]{2,1,0:T(8,128)}, f32[6,192,128]{2,1,0:T(8,128)}, u32[]{:S(2)}, u32[]{:S(2)}) %collective-permute-start.12) | collective-permute-done | bytes 589856 | tf_op jit(solution)/shard_map/ppermute | solution.py:639
  190.6 3.9 %prep.2 = (f32[5,192,128]{2,1,0:T(8,128)S(1)}, f32[5,192,128]{2,1,0:T(8,128)S(1)}) custom-call(f32[8,128]{1,0:T(8,128)S(1)} %concatenate.163.refs_0_, f32[192,128]{1,0:T(8,128)S(1)} %broadcast_in_dim.164.refs_1_, f32[6,192,128]{2,1,0:T(8,128)S(1)} %copy-done.14, f32[6,192,128]{2,1,0:T(8,128)} %collective-permute-done.11.refs_3_.refs_12_, ...), custom_call_target="tpu_custom_call" | custom-call | flops 1000000000 | tf_op jit(solution)/shard_map/prep/pallas_call | solution.py:329
  194.5 2.6 collective-permute-start.16
  197.4 4.1 %zforward.10 = (f32[6,192,128]{2,1,0:T(8,128)S(1)}, f32[6,192,128]{2,1,0:T(8,128)}) custom-call(bf16[384,288]{1,0:T(8,128)(2,1)S(1)} %copy-done.31, bf16[384,288]{1,0:T(8,128)(2,1)S(1)} %copy-done.29, f32[3,6,48,256]{3,2,1,0:T(8,128)S(1)} %copy-done.33, f32[3,6,48,256]{3,2,1,0:T(8,128)} %collective-permute-done.14.refs_3_), custom_call_target="tpu_custom_call" | custom-call | flops 1000000000 | tf_op jit(solution)/shard_map/zforward/pallas_call | solution.py:237
  204.7 2.2 collective-permute-done.16.refs_6_
  206.9 9.5 %solve.2 = (f32[3,6,192,128]{3,2,1,0:T(8,128)S(1)}, f32[6,192,128]{2,1,0:T(8,128)S(1)}, f32[3,6,48,128]{3,2,1,0:T(8,128)S(1)}, f32[3,6,48,128]{3,2,1,0:T(8,128)S...) custom-call(f32[8,128]{1,0:T(8,128)S(1)} %concatenate.163.refs_0_, ...), custom_call_target="tpu_custom_call" | custom-call | flops 2500000000 | tf_op jit(solution)/shard_map/solve/pallas_call | solution.py:443
  217.7 3.0 zforward.11
  223.9 26.3 %collective-permute-done.21.refs_5_.refs_14_ = f32[6,192,128]{2,1,0:T(8,128)} collective-permute-done((f32[6,192,128]{2,1,0:T(8,128)}, f32[6,192,128]{2,1,0:T(8,128)}, u32[]{:S(2)}, u32[]{:S(2)}) %collective-permute-start.21) | collective-permute-done | bytes 589856 | tf_op jit(solution)/shard_map/ppermute | solution.py:639
  250.2 21.7 %collective-permute-done.20.refs_3_.refs_12_ = f32[6,192,128]{2,1,0:T(8,128)} collective-permute-done((f32[6,192,128]{2,1,0:T(8,128)}, f32[6,192,128]{2,1,0:T(8,128)}, u32[]{:S(2)}, u32[]{:S(2)}) %collective-permute-start.20) | collective-permute-done | bytes 589856 | tf_op jit(solution)/shard_map/ppermute | solution.py:639
  271.8 12.6 %collective-permute-done.22.refs_7_.refs_16_ = f32[6,192,128]{2,1,0:T(8,128)} collective-permute-done((f32[6,192,128]{2,1,0:T(8,128)}, f32[6,192,128]{2,1,0:T(8,128)}, u32[]{:S(2)}, u32[]{:S(2)}) %collective-permute-start.22) | collective-permute-done | bytes 589856 | tf_op jit(solution)/shard_map/ppermute | solution.py:639
  285.5 3.8 %prep.3 = (f32[5,192,128]{2,1,0:T(8,128)S(1)}, f32[5,192,128]{2,1,0:T(8,128)S(1)}) custom-call(f32[8,128]{1,0:T(8,128)S(1)} %concatenate.156.refs_0_, f32[192,128]{1,0:T(8,128)S(1)} %broadcast_in_dim.164.refs_1_, f32[6,192,128]{2,1,0:T(8,128)S(1)} %copy-done.16, f32[6,192,128]{2,1,0:T(8,128)} %collective-permute-done.20.refs_3_.refs_12_, ...), custom_call_target="tpu_custom_call" | custom-call | flops 1000000000 | tf_op jit(solution)/shard_map/prep/pallas_call | solution.py:329
  289.6 2.5 collective-permute-start.24
  293.5 3.4 collective-permute-start.26
  296.9 5.6 %collective-permute-done.23.refs_5_ = f32[5,192,128]{2,1,0:T(8,128)S(1)} collective-permute-done((f32[5,192,128]{2,1,0:T(8,128)S(1)}, f32[5,192,128]{2,1,0:T(8,128)S(1)}, u32[]{:S(2)}, u32[]{:S(2)}) %collective-permute-start.23) | collective-permute-done | bytes 491552 | tf_op jit(solution)/shard_map/ppermute | solution.py:699
  302.5 9.3 %solve.3 = (f32[3,6,192,128]{3,2,1,0:T(8,128)S(1)}, f32[6,192,128]{2,1,0:T(8,128)S(1)}, f32[3,6,48,128]{3,2,1,0:T(8,128)S(1)}, f32[3,6,48,128]{3,2,1,0:T(8,128)S...) custom-call(f32[8,128]{1,0:T(8,128)S(1)} %concatenate.156.refs_0_, ...), custom_call_target="tpu_custom_call" | custom-call | flops 2500000000 | tf_op jit(solution)/shard_map/solve/pallas_call | solution.py:443
  311.8 2.5 collective-permute-start.28
  318.1 3.3 pack.2
  321.5 3.7 collective-permute-done.25.refs_4_
  325.2 3.4 back.2.refs_0_
  328.6 24.8 %collective-permute-done.28.refs_4_ = f32[3,6,48,128]{3,2,1,0:T(8,128)S(1)} collective-permute-done((f32[3,6,48,128]{3,2,1,0:T(8,128)S(1)}, f32[3,6,48,128]{3,2,1,0:T(8,128)S(1)}, u32[]{:S(2)}, u32[]{:S(2)}) %collective-permute-start.28) | collective-permute-done | bytes 442400 | tf_op jit(solution)/shard_map/ppermute | solution.py:717
  353.3 9.4 %collective-permute-done.29.refs_5_ = f32[3,6,48,128]{3,2,1,0:T(8,128)S(1)} collective-permute-done((f32[3,6,48,128]{3,2,1,0:T(8,128)S(1)}, f32[3,6,48,128]{3,2,1,0:T(8,128)S(1)}, u32[]{:S(2)}, u32[]{:S(2)}) %collective-permute-start.29) | collective-permute-done | bytes 442400 | tf_op jit(solution)/shard_map/ppermute | solution.py:717
  362.7 8.9 %collective-permute-done.30.refs_6_ = f32[3,6,48,128]{3,2,1,0:T(8,128)S(1)} collective-permute-done((f32[3,6,48,128]{3,2,1,0:T(8,128)S(1)}, f32[3,6,48,128]{3,2,1,0:T(8,128)S(1)}, u32[]{:S(2)}, u32[]{:S(2)}) %collective-permute-start.30) | collective-permute-done | bytes 442400 | tf_op jit(solution)/shard_map/ppermute | solution.py:717
  371.6 4.4 %back.3 = f32[3,6,48,1024]{3,2,1,0:T(8,128)} custom-call(f32[3,6,48,1024]{3,2,1,0:T(8,128)S(1)} %back.2.refs_0_, bf16[1024,512]{1,0:T(8,128)(2,1)S(1)} %get-tuple-element.196.refs_1_, bf16[1024,512]{1,0:T(8,128)(2,1)S(1)} %get-tuple-element.195.refs_2_, f32[3,6,48,128]{3,2,1,0:T(8,128)S(1)} %get-tuple-element.183.refs_3_, ...), custom_call_target="tpu_custom_call" | custom-call | flops 1750000000 | tf_op jit(solution)/shard_map/back/pallas_call | solution.py:495
  (248 shorter events, 46.9 us)
Async XLA Ops:
  3.1 38.5 %collective-permute-start = (f32[1,3,48,1024]{3,2,1,0:T(8,128)}, f32[1,3,48,1024]{3,2,1,0:T(8,128)}, u32[]{:S(2)}, u32[]{:S(2)}) collective-permute-start(f32[1,3,48,1024]{3,2,1,0:T(8,128)} %get-tuple-element.194), channel_id=1, source_target_pairs={{0,4},{4,8},{8,12},{12,16},{16,20},{20,24},{24,28},{28,0},{1,5},{5... | collective-permute-start | bytes 1769480 | tf_op jit(solution)/shard_map/ppermute | solution.py:649
  3.1 40.5 %collective-permute-start.1 = (f32[1,3,48,1024]{3,2,1,0:T(8,128)}, f32[1,3,48,1024]{3,2,1,0:T(8,128)}, u32[]{:S(2)}, u32[]{:S(2)}) collective-permute-start(f32[1,3,48,1024]{3,2,1,0:T(8,128)} %get-tuple-element.193), channel_id=1, source_target_pairs={{0,28},{4,0},{8,4},{12,8},{16,12},{20,16},{24,20},{28,24},{1,29},{... | collective-permute-start | bytes 1769480 | tf_op jit(solution)/shard_map/ppermute | solution.py:650
  19.5 36.6 %collective-permute-start.2 = (f32[2,6,48,256]{3,2,1,0:T(8,128)}, f32[2,6,48,256]{3,2,1,0:T(8,128)}, u32[]{:S(2)}, u32[]{:S(2)}) collective-permute-start(f32[2,6,48,256]{3,2,1,0:T(8,128)} %get-tuple-element.100), channel_id=1, source_target_pairs={{0,1},{1,0},{2,3},{3,2},{4,5},{5,4},{6,7},{7,6},{8,9},{9,8},{10,11... | collective-permute-start | bytes 1769480 | tf_op jit(solution)/shard_map/ppermute | solution.py:621
  21.1 47.3 %collective-permute-start.4 = (f32[2,3,48,1024]{3,2,1,0:T(8,128)}, f32[2,3,48,1024]{3,2,1,0:T(8,128)S(1)}, u32[]{:S(2)}, u32[]{:S(2)}) collective-permute-start(f32[2,3,48,1024]{3,2,1,0:T(8,128)} %get-tuple-element.192), channel_id=1, source_target_pairs={{0,4},{4,8},{8,12},{12,16},{16,20},{20,24},{24,28},{28,0},{1,5},{5... | collective-permute-start | bytes 3538952 | tf_op jit(solution)/shard_map/ppermute | solution.py:649
  21.1 47.3 %collective-permute-start.5 = (f32[2,3,48,1024]{3,2,1,0:T(8,128)}, f32[2,3,48,1024]{3,2,1,0:T(8,128)}, u32[]{:S(2)}, u32[]{:S(2)}) collective-permute-start(f32[2,3,48,1024]{3,2,1,0:T(8,128)} %get-tuple-element.191), channel_id=1, source_target_pairs={{0,28},{4,0},{8,4},{12,8},{16,12},{20,16},{24,20},{28,24},{1,29},{... | collective-permute-start | bytes 3538952 | tf_op jit(solution)/shard_map/ppermute | solution.py:650
  41.5 48.1 %collective-permute-start.6 = (f32[2,6,48,256]{3,2,1,0:T(8,128)}, f32[2,6,48,256]{3,2,1,0:T(8,128)S(1)}, u32[]{:S(2)}, u32[]{:S(2)}) collective-permute-start(f32[2,6,48,256]{3,2,1,0:T(8,128)} %get-tuple-element.102), channel_id=1, source_target_pairs={{0,1},{1,0},{2,3},{3,2},{4,5},{5,4},{6,7},{7,6},{8,9},{9,8},{10,11... | collective-permute-start | bytes 1769480 | tf_op jit(solution)/shard_map/ppermute | solution.py:621
  52.1 12.2 %collective-permute-start.3 = (f32[1,6,48,256]{3,2,1,0:T(8,128)S(1)}, f32[1,6,48,256]{3,2,1,0:T(8,128)S(1)}, u32[]{:S(2)}, u32[]{:S(2)}) collective-permute-start(f32[1,6,48,256]{3,2,1,0:T(8,128)S(1)} %get-tuple-element.107), channel_id=1, source_target_pairs={{0,1},{1,0},{2,3},{3,2},{4,5},{5,4},{6,7},{7,6},{8,9},{9,8},{10,11... | collective-permute-start | bytes 884744 | tf_op jit(solution)/shard_map/ppermute | solution.py:621
  52.4 52.4 %copy-start.28 = (bf16[384,288]{1,0:T(8,128)(2,1)}, bf16[384,288]{1,0:T(8,128)(2,1)S(1)}, u32[]{:S(2)}) copy-start(bf16[384,288]{1,0:T(8,128)(2,1)S(1)} %get-tuple-element.205.refs_1_) | copy-start | bytes 663556
  52.4 52.4 %copy-start.30 = (bf16[384,288]{1,0:T(8,128)(2,1)}, bf16[384,288]{1,0:T(8,128)(2,1)S(1)}, u32[]{:S(2)}) copy-start(bf16[384,288]{1,0:T(8,128)(2,1)S(1)} %get-tuple-element.155.refs_0_) | copy-start | bytes 663556
  52.4 11.9 %copy-start.41 = (f32[2,6,48,256]{3,2,1,0:T(8,128)S(1)}, f32[2,6,48,256]{3,2,1,0:T(8,128)}, u32[]{:S(2)}) copy-start(f32[2,6,48,256]{3,2,1,0:T(8,128)} %copy-done.40) | copy-start | bytes 1769476
  56.2 48.7 %collective-permute-start.8 = (f32[2,6,48,256]{3,2,1,0:T(8,128)S(1)}, f32[2,6,48,256]{3,2,1,0:T(8,128)S(1)}, u32[]{:S(2)}, u32[]{:S(2)}) collective-permute-start(f32[2,6,48,256]{3,2,1,0:T(8,128)S(1)} %get-tuple-element.109), channel_id=1, source_target_pairs={{0,1},{1,0},{2,3},{3,2},{4,5},{5,4},{6,7},{7,6},{8,9},{9,8},{10,11... | collective-permute-start | bytes 1769480 | tf_op jit(solution)/shard_map/ppermute | solution.py:621
  80.9 9.2 %collective-permute-start.7 = (f32[1,6,48,256]{3,2,1,0:T(8,128)S(1)}, f32[1,6,48,256]{3,2,1,0:T(8,128)S(1)}, u32[]{:S(2)}, u32[]{:S(2)}) collective-permute-start(f32[1,6,48,256]{3,2,1,0:T(8,128)S(1)} %get-tuple-element.119), channel_id=1, source_target_pairs={{0,1},{1,0},{2,3},{3,2},{4,5},{5,4},{6,7},{7,6},{8,9},{9,8},{10,11... | collective-permute-start | bytes 884744 | tf_op jit(solution)/shard_map/ppermute | solution.py:621
  89.4 15.4 %collective-permute-start.9 = (f32[1,6,48,256]{3,2,1,0:T(8,128)S(1)}, f32[1,6,48,256]{3,2,1,0:T(8,128)S(1)}, u32[]{:S(2)}, u32[]{:S(2)}) collective-permute-start(f32[1,6,48,256]{3,2,1,0:T(8,128)S(1)} %get-tuple-element.121), channel_id=1, source_target_pairs={{0,1},{1,0},{2,3},{3,2},{4,5},{5,4},{6,7},{7,6},{8,9},{9,8},{10,11... | collective-permute-start | bytes 884744 | tf_op jit(solution)/shard_map/ppermute | solution.py:621
  102.4 21.5 %collective-permute-start.10 = (f32[3,6,48,256]{3,2,1,0:T(8,128)}, f32[3,6,48,256]{3,2,1,0:T(8,128)}, u32[]{:S(2)}, u32[]{:S(2)}) collective-permute-start(f32[3,6,48,256]{3,2,1,0:T(8,128)} %get-tuple-element.131), channel_id=1, source_target_pairs={{0,1},{1,0},{2,3},{3,2},{4,5},{5,4},{6,7},{7,6},{8,9},{9,8},{10,11... | collective-permute-start | bytes 2654216 | tf_op jit(solution)/shard_map/ppermute | solution.py:621
  108.7 15.0 %copy-start.65 = (f32[1,128]{1,0:T(1,128)S(1)}, f32[1,128]{1,0:T(1,128)}, u32[]{:S(2)}) copy-start(f32[1,128]{1,0:T(1,128)} %get-tuple-element.245) | copy-start | bytes 1540
  108.7 15.0 %copy-start.66 = (f32[1,128]{1,0:T(1,128)S(1)}, f32[1,128]{1,0:T(1,128)}, u32[]{:S(2)}) copy-start(f32[1,128]{1,0:T(1,128)} %get-tuple-element.246) | copy-start | bytes 1540
  108.7 15.0 %copy-start.67 = (f32[1,128]{1,0:T(1,128)S(1)}, f32[1,128]{1,0:T(1,128)}, u32[]{:S(2)}) copy-start(f32[1,128]{1,0:T(1,128)} %get-tuple-element.247) | copy-start | bytes 1540
  108.7 15.0 %copy-start.68 = (f32[1,128]{1,0:T(1,128)S(1)}, f32[1,128]{1,0:T(1,128)}, u32[]{:S(2)}) copy-start(f32[1,128]{1,0:T(1,128)} %get-tuple-element.248) | copy-start | bytes 1540
  108.7 15.0 %copy-start.8 = (f32[6,192,256]{2,1,0:T(8,128)S(1)}, f32[6,192,256]{2,1,0:T(8,128)}, u32[]{:S(2)}) copy-start(f32[6,192,256]{2,1,0:T(8,128)} %refs_7_.3) | copy-start | bytes 3538948
  118.8 75.8 %collective-permute-start.14 = (f32[3,6,48,256]{3,2,1,0:T(8,128)}, f32[3,6,48,256]{3,2,1,0:T(8,128)}, u32[]{:S(2)}, u32[]{:S(2)}) collective-permute-start(f32[3,6,48,256]{3,2,1,0:T(8,128)} %get-tuple-element.137), channel_id=1, source_target_pairs={{0,1},{1,0},{2,3},{3,2},{4,5},{5,4},{6,7},{7,6},{8,9},{9,8},{10,11... | collective-permute-start | bytes 2654216 | tf_op jit(solution)/shard_map/ppermute | solution.py:621
  118.9 21.5 %collective-permute-start.11 = (f32[6,192,128]{2,1,0:T(8,128)}, f32[6,192,128]{2,1,0:T(8,128)}, u32[]{:S(2)}, u32[]{:S(2)}) collective-permute-start(f32[6,192,128]{2,1,0:T(8,128)} %get-tuple-element.113), channel_id=1, source_target_pairs={{0,3},{1,2},{2,1},{3,0},{4,7},{5,6},{6,5},{7,4},{8,11},{9,10},{10,... | collective-permute-start | bytes 1769480 | tf_op jit(solution)/shard_map/ppermute | solution.py:639
  121.6 62.5 %collective-permute-start.13 = (f32[6,192,128]{2,1,0:T(8,128)}, f32[6,192,128]{2,1,0:T(8,128)}, u32[]{:S(2)}, u32[]{:S(2)}) collective-permute-start(f32[6,192,128]{2,1,0:T(8,128)} %get-tuple-element.135), channel_id=1, source_target_pairs={{0,3},{1,2},{2,1},{3,0},{4,7},{5,6},{6,5},{7,4},{8,11},{9,10},{10,... | collective-permute-start | bytes 1769480 | tf_op jit(solution)/shard_map/ppermute | solution.py:639
  121.7 68.8 %collective-permute-start.12 = (f32[6,192,128]{2,1,0:T(8,128)}, f32[6,192,128]{2,1,0:T(8,128)}, u32[]{:S(2)}, u32[]{:S(2)}) collective-permute-start(f32[6,192,128]{2,1,0:T(8,128)} %get-tuple-element.125), channel_id=1, source_target_pairs={{0,3},{1,2},{2,1},{3,0},{4,7},{5,6},{6,5},{7,4},{8,11},{9,10},{10,... | collective-permute-start | bytes 1769480 | tf_op jit(solution)/shard_map/ppermute | solution.py:639
  123.9 78.4 %collective-permute-start.17 = (f32[3,192,256]{2,1,0:T(8,128)S(1)}, f32[3,192,256]{2,1,0:T(8,128)S(1)}, u32[]{:S(2)}, u32[]{:S(2)}) collective-permute-start(f32[3,192,256]{2,1,0:T(8,128)S(1)} %get-tuple-element.204), channel_id=1, source_target_pairs={{0,4},{4,8},{8,12},{12,16},{16,20},{20,24},{24,28},{28,0},{1,5},{5... | collective-permute-start | bytes 1769480 | tf_op jit(solution)/shard_map/ppermute | solution.py:728
  130.1 60.5 %copy-start.14 = (f32[6,192,128]{2,1,0:T(8,128)S(1)}, f32[6,192,128]{2,1,0:T(8,128)}, u32[]{:S(2)}) copy-start(f32[6,192,128]{2,1,0:T(8,128)} %copy-done.13) | copy-start | bytes 1769476
  130.1 60.5 %copy-start.18 = (f32[6,192,128]{2,1,0:T(8,128)S(1)}, f32[6,192,128]{2,1,0:T(8,128)}, u32[]{:S(2)}) copy-start(f32[6,192,128]{2,1,0:T(8,128)} %copy-done.17) | copy-start | bytes 1769476
  130.1 60.5 %copy-start.20 = (f32[6,192,128]{2,1,0:T(8,128)S(1)}, f32[6,192,128]{2,1,0:T(8,128)}, u32[]{:S(2)}) copy-start(f32[6,192,128]{2,1,0:T(8,128)} %copy-done.19) | copy-start | bytes 1769476
  138.0 59.2 %copy-start.50 = (f32[192,192]{1,0:T(8,128)S(1)}, f32[192,192]{1,0:T(8,128)}, u32[]{:S(2)}) copy-start(f32[192,192]{1,0:T(8,128)} %get-tuple-element.243) | copy-start | bytes 442372
  138.0 59.2 %copy-start.51 = (f32[192,192]{1,0:T(8,128)S(1)}, f32[192,192]{1,0:T(8,128)}, u32[]{:S(2)}) copy-start(f32[192,192]{1,0:T(8,128)} %get-tuple-element.244) | copy-start | bytes 442372
  140.4 63.7 %collective-permute-start.18 = (f32[3,192,256]{2,1,0:T(8,128)S(1)}, f32[3,192,256]{2,1,0:T(8,128)S(1)}, u32[]{:S(2)}, u32[]{:S(2)}) collective-permute-start(f32[3,192,256]{2,1,0:T(8,128)S(1)} %get-tuple-element.203), channel_id=1, source_target_pairs={{0,28},{4,0},{8,4},{12,8},{16,12},{20,16},{24,20},{28,24},{1,29},{... | collective-permute-start | bytes 1769480 | tf_op jit(solution)/shard_map/ppermute | solution.py:729
  184.1 33.6 %collective-permute-start.19 = (f32[3,6,48,256]{3,2,1,0:T(8,128)S(1)}, f32[3,6,48,256]{3,2,1,0:T(8,128)S(1)}, u32[]{:S(2)}, u32[]{:S(2)}) collective-permute-start(f32[3,6,48,256]{3,2,1,0:T(8,128)S(1)} %get-tuple-element.142), channel_id=1, source_target_pairs={{0,1},{1,0},{2,3},{3,2},{4,5},{5,4},{6,7},{7,6},{8,9},{9,8},{10,11... | collective-permute-start | bytes 2654216 | tf_op jit(solution)/shard_map/ppermute | solution.py:621
  194.5 10.3 %collective-permute-start.15 = (f32[5,192,128]{2,1,0:T(8,128)S(1)}, f32[5,192,128]{2,1,0:T(8,128)S(1)}, u32[]{:S(2)}, u32[]{:S(2)}) collective-permute-start(f32[5,192,128]{2,1,0:T(8,128)S(1)} %get-tuple-element.147), channel_id=1, source_target_pairs={{0,4},{4,8},{8,12},{12,16},{16,20},{20,24},{24,28},{28,0},{1,5},{5... | collective-permute-start | bytes 1474568 | tf_op jit(solution)/shard_map/ppermute | solution.py:699
  194.5 12.4 %collective-permute-start.16 = (f32[5,192,128]{2,1,0:T(8,128)S(1)}, f32[5,192,128]{2,1,0:T(8,128)S(1)}, u32[]{:S(2)}, u32[]{:S(2)}) collective-permute-start(f32[5,192,128]{2,1,0:T(8,128)S(1)} %get-tuple-element.148), channel_id=1, source_target_pairs={{0,28},{4,0},{8,4},{12,8},{16,12},{20,16},{24,20},{28,24},{1,29},{... | collective-permute-start | bytes 1474568 | tf_op jit(solution)/shard_map/ppermute | solution.py:700
  202.3 14.1 %copy-start.9 = (f32[3,192,256]{2,1,0:T(8,128)}, f32[3,192,256]{2,1,0:T(8,128)S(1)}, u32[]{:S(2)}) copy-start(f32[3,192,256]{2,1,0:T(8,128)S(1)} %collective-permute-done.17.refs_8_) | copy-start | bytes 1769476
  202.3 47.8 %collective-permute-start.21 = (f32[6,192,128]{2,1,0:T(8,128)}, f32[6,192,128]{2,1,0:T(8,128)}, u32[]{:S(2)}, u32[]{:S(2)}) collective-permute-start(f32[6,192,128]{2,1,0:T(8,128)} %get-tuple-element.151), channel_id=1, source_target_pairs={{0,3},{1,2},{2,1},{3,0},{4,7},{5,6},{6,5},{7,4},{8,11},{9,10},{10,... | collective-permute-start | bytes 1769480 | tf_op jit(solution)/shard_map/ppermute | solution.py:639
  204.1 67.7 %collective-permute-start.20 = (f32[6,192,128]{2,1,0:T(8,128)}, f32[6,192,128]{2,1,0:T(8,128)}, u32[]{:S(2)}, u32[]{:S(2)}) collective-permute-start(f32[6,192,128]{2,1,0:T(8,128)} %get-tuple-element.140), channel_id=1, source_target_pairs={{0,3},{1,2},{2,1},{3,0},{4,7},{5,6},{6,5},{7,4},{8,11},{9,10},{10,... | collective-permute-start | bytes 1769480 | tf_op jit(solution)/shard_map/ppermute | solution.py:639
  221.5 63.0 %copy-start.16 = (f32[6,192,128]{2,1,0:T(8,128)S(1)}, f32[6,192,128]{2,1,0:T(8,128)}, u32[]{:S(2)}) copy-start(f32[6,192,128]{2,1,0:T(8,128)} %copy-done.15) | copy-start | bytes 1769476
  221.5 63.0 %collective-permute-start.22 = (f32[6,192,128]{2,1,0:T(8,128)}, f32[6,192,128]{2,1,0:T(8,128)}, u32[]{:S(2)}, u32[]{:S(2)}) collective-permute-start(f32[6,192,128]{2,1,0:T(8,128)} %get-tuple-element.157), channel_id=1, source_target_pairs={{0,3},{1,2},{2,1},{3,0},{4,7},{5,6},{6,5},{7,4},{8,11},{9,10},{10,... | collective-permute-start | bytes 1769480 | tf_op jit(solution)/shard_map/ppermute | solution.py:639
  223.5 60.9 %copy-start.25 = (f32[6,192,128]{2,1,0:T(8,128)S(1)}, f32[6,192,128]{2,1,0:T(8,128)}, u32[]{:S(2)}) copy-start(f32[6,192,128]{2,1,0:T(8,128)} %copy-done.24) | copy-start | bytes 1769476
  289.3 13.2 %collective-permute-start.23 = (f32[5,192,128]{2,1,0:T(8,128)S(1)}, f32[5,192,128]{2,1,0:T(8,128)S(1)}, u32[]{:S(2)}, u32[]{:S(2)}) collective-permute-start(f32[5,192,128]{2,1,0:T(8,128)S(1)} %get-tuple-element.162), channel_id=1, source_target_pairs={{0,4},{4,8},{8,12},{12,16},{16,20},{20,24},{24,28},{28,0},{1,5},{5... | collective-permute-start | bytes 1474568 | tf_op jit(solution)/shard_map/ppermute | solution.py:699
  289.6 12.9 %collective-permute-start.24 = (f32[5,192,128]{2,1,0:T(8,128)S(1)}, f32[5,192,128]{2,1,0:T(8,128)S(1)}, u32[]{:S(2)}, u32[]{:S(2)}) collective-permute-start(f32[5,192,128]{2,1,0:T(8,128)S(1)} %get-tuple-element.163), channel_id=1, source_target_pairs={{0,28},{4,0},{8,4},{12,8},{16,12},{20,16},{24,20},{28,24},{1,29},{... | collective-permute-start | bytes 1474568 | tf_op jit(solution)/shard_map/ppermute | solution.py:700
  292.5 10.1 %copy-start.10 = (f32[3,192,256]{2,1,0:T(8,128)S(1)}, f32[3,192,256]{2,1,0:T(8,128)}, u32[]{:S(2)}) copy-start(f32[3,192,256]{2,1,0:T(8,128)} %copy-done.9) | copy-start | bytes 1769476
  292.5 21.8 %collective-permute-start.27 = (f32[3,6,48,128]{3,2,1,0:T(8,128)S(1)}, f32[3,6,48,128]{3,2,1,0:T(8,128)S(1)}, u32[]{:S(2)}, u32[]{:S(2)}) collective-permute-start(f32[3,6,48,128]{3,2,1,0:T(8,128)S(1)} %copy-done.47), channel_id=1, source_target_pairs={{0,3},{1,0},{2,1},{3,2},{4,7},{5,4},{6,5},{7,6},{8,11},{9,8},{10,9... | collective-permute-start | bytes 1327112 | tf_op jit(solution)/shard_map/ppermute | solution.py:717
  293.5 28.0 %collective-permute-start.26 = (f32[3,6,48,128]{3,2,1,0:T(8,128)S(1)}, f32[3,6,48,128]{3,2,1,0:T(8,128)S(1)}, u32[]{:S(2)}, u32[]{:S(2)}) collective-permute-start(f32[3,6,48,128]{3,2,1,0:T(8,128)S(1)} %copy-done.45), channel_id=1, source_target_pairs={{0,2},{1,3},{2,0},{3,1},{4,6},{5,7},{6,4},{7,5},{8,10},{9,11},{10,... | collective-permute-start | bytes 1327112 | tf_op jit(solution)/shard_map/ppermute | solution.py:717
  296.9 28.2 %collective-permute-start.25 = (f32[3,6,48,128]{3,2,1,0:T(8,128)S(1)}, f32[3,6,48,128]{3,2,1,0:T(8,128)S(1)}, u32[]{:S(2)}, u32[]{:S(2)}) collective-permute-start(f32[3,6,48,128]{3,2,1,0:T(8,128)S(1)} %copy-done.43), channel_id=1, source_target_pairs={{0,1},{1,2},{2,3},{3,0},{4,5},{5,6},{6,7},{7,4},{8,9},{9,10},{10,1... | collective-permute-start | bytes 1327112 | tf_op jit(solution)/shard_map/ppermute | solution.py:717
  311.8 41.5 %collective-permute-start.28 = (f32[3,6,48,128]{3,2,1,0:T(8,128)S(1)}, f32[3,6,48,128]{3,2,1,0:T(8,128)S(1)}, u32[]{:S(2)}, u32[]{:S(2)}) collective-permute-start(f32[3,6,48,128]{3,2,1,0:T(8,128)S(1)} %get-tuple-element.184), channel_id=1, source_target_pairs={{0,1},{1,2},{2,3},{3,0},{4,5},{5,6},{6,7},{7,4},{8,9},{9,10},{10,1... | collective-permute-start | bytes 1327112 | tf_op jit(solution)/shard_map/ppermute | solution.py:717
  314.3 48.4 %collective-permute-start.29 = (f32[3,6,48,128]{3,2,1,0:T(8,128)S(1)}, f32[3,6,48,128]{3,2,1,0:T(8,128)S(1)}, u32[]{:S(2)}, u32[]{:S(2)}) collective-permute-start(f32[3,6,48,128]{3,2,1,0:T(8,128)S(1)} %get-tuple-element.185), channel_id=1, source_target_pairs={{0,2},{1,3},{2,0},{3,1},{4,6},{5,7},{6,4},{7,5},{8,10},{9,11},{10,... | collective-permute-start | bytes 1327112 | tf_op jit(solution)/shard_map/ppermute | solution.py:717
  314.3 57.3 %collective-permute-start.30 = (f32[3,6,48,128]{3,2,1,0:T(8,128)S(1)}, f32[3,6,48,128]{3,2,1,0:T(8,128)S(1)}, u32[]{:S(2)}, u32[]{:S(2)}) collective-permute-start(f32[3,6,48,128]{3,2,1,0:T(8,128)S(1)} %get-tuple-element.186), channel_id=1, source_target_pairs={{0,3},{1,0},{2,1},{3,2},{4,7},{5,4},{6,5},{7,6},{8,11},{9,8},{10,9... | collective-permute-start | bytes 1327112 | tf_op jit(solution)/shard_map/ppermute | solution.py:717
  (54 other events, 227.6 us)
where the time goes:
time: 380 us; the launch traced here: 376 us
  waiting for transfers between devices  175 us (46%)
  Pallas kernels  124 us (33%)
  starting transfers between devices  36.3 us (10%)
  local copies, waits for them, and re-layouts  19.7 us (5%)
  other arithmetic  19 us (5%)
    ppermute x6, waiting for transfers between devices, gather_z(): return [got[0], lax.ppermute(got[1], 'yz', cross)]  113 us
    pallas_call x9, Pallas kernels, spectra_call(): pl.pallas_call(lambda *refs: spectra_body(comp, omega, half, jobs, comps,...  57.4 us
    ppermute x6, waiting for transfers between devices, give_back(): got.append(lax.ppermute(hs[s], 'yz', ring('yz', s)))  46.7 us
    pallas_call x6, Pallas kernels, z_call(): pl.pallas_call(lambda *refs: z_body(counts, n_t, half, *refs), out_shape=...  21.4 us
    pallas_call x2, Pallas kernels, solve_call(): pl.pallas_call(lambda *refs: solve_body(chunk, half, n_slot, n, nb, *refs...  18.7 us
    unnamed x142, local copies, waits for them, and re-layouts  15.1 us
    ppermute x9, starting transfers between devices, scatter(): return [pieces[0], lax.ppermute(pieces[1], 'yz', swap)]  8.92 us
    ppermute x6, starting transfers between devices, gather_z(): return [got[0], lax.ppermute(got[1], 'yz', cross)]  8.51 us
  transfers between devices with their start and end apart: 31, of which 15 were waited for; matrix products, arithmetic and copies ran while one was open for 6% of the time, Pallas kernels for 31%

commit v1 on v0

--- a/solution.py
+++ b/solution.py
@@ -2,6 +2,7 @@
 
 import jax
 import jax.numpy as jnp
+import numpy as np
 from jax import lax
 from jax.experimental import pallas as pl
 from jax.experimental.pallas import tpu as pltpu
@@ -31,8 +32,10 @@
 
 
 def split_const(matrix):
-    high = lax.reduce_precision(matrix, 8, 7)
-    return high.astype(bf16), (matrix - high).astype(bf16)
+    exact = matrix.astype(np.float32)
+    high = exact.astype(jnp.bfloat16)
+    low = (exact - high.astype(np.float32)).astype(jnp.bfloat16)
+    return jnp.asarray(high), jnp.asarray(low)
 
 
 def split_value(value):
@@ -63,35 +66,35 @@
     return pltpu.roll(value, half, axis=1) * lane_sign(half)
 
 
-def y_matrix(width_y, modes, weights):
-    step = 32
-    count, half = modes.shape
-    k = jnp.concatenate([modes, modes], axis=1).reshape(1, -1)
-    phase = jnp.concatenate([jnp.zeros((count, half)), jnp.ones((count, half))], axis=1)
-    phase = (0.5 * math.pi * phase).reshape(1, -1).astype(f32)
-    unit = 2.0 * math.pi / width_y
-    a = jnp.arange(width_y // step, dtype=jnp.int32)[:, None] * step
-    b = jnp.arange(step, dtype=jnp.int32)[:, None]
-    angle_a = unit * (a * k % width_y).astype(f32)
-    angle_b = unit * (b * k % width_y).astype(f32) + phase
-    w = jnp.concatenate([weights, weights], axis=1).reshape(1, -1) / math.sqrt(width_y)
-    ca, sa = jnp.cos(angle_a) * w, jnp.sin(angle_a) * w
-    cb, sb = jnp.cos(angle_b), jnp.sin(angle_b)
-    ca, sa, cb, sb = lax.optimization_barrier((ca, sa, cb, sb))
-    full = ca[:, None, :] * cb[None] - sa[:, None, :] * sb[None]
-    return split_const(full.reshape(width_y, -1))
-
-
-def z_angles(depth_z, rows_m, cols_z):
-    return (
-        2.0
-        * math.pi
-        / depth_z
-        * (rows_m[:, None] * cols_z[None, :] % depth_z).astype(f32)
-    )
-
-
-def spectra_body(comp, omega, half, jobs, comps, n_out, bg_ref, *rest):
+def y_matrix(width_y, modes):
+    angle = 2.0 * np.pi / width_y * (np.arange(width_y)[:, None, None] * modes[None] % width_y)
+    full = np.concatenate([np.cos(angle), -np.sin(angle)], axis=2)
+    return split_const(full.reshape(width_y, -1) / math.sqrt(width_y))
+
+
+def z_forward_matrix(depth, rows, sources):
+    m = np.arange(depth)
+    kz = (2.0 * np.pi / depth * np.where(m < depth // 2, m, m - depth))[:, None]
+    blocks = []
+    for source in sources:
+        z = source * rows + np.arange(rows)
+        wave = np.exp(-2j * np.pi / depth * (m[:, None] * z[None, :] % depth))
+        blocks += [-viscosity * kz * kz * wave, 1j * kz * wave, wave]
+    full = np.concatenate(blocks, axis=1) / math.sqrt(depth)
+    return np.concatenate([full.real, full.imag], axis=0)
+
+
+def z_inverse_matrix(depth):
+    m = np.arange(depth)
+    full = np.exp(2j * np.pi / depth * (m[:, None] * m[None, :] % depth)) / math.sqrt(depth)
+    return split_const(np.concatenate([full.real, full.imag], axis=0))
+
+
+def block_at(index, size):
+    return pl.ds(pl.multiple_of(index * size, size), size)
+
+
+def spectra_body(comp, omega, half, jobs, comps, n_out, ids, bg_ref, *rest):
     vels = dict(zip(comps, rest))
     rest = rest[len(comps) :]
     ui, u0, u1, u2 = vels[comp], vels.get(0), vels.get(1), vels.get(2)
@@ -101,7 +104,7 @@
         n_h = 2 if comp == 0 else 4
         halos, rest = rest[:n_h], rest[n_h:]
     mats, rest = rest[: 3 * len(jobs)], rest[3 * len(jobs) :]
-    outs, buf = rest[:-1], rest[-1]
+    outs, (buf, res) = rest[:-2], rest[-2:]
     _, X, Rz, NY = ui.shape
     d1 = (0.0, 45.0 / 60.0, -9.0 / 60.0, 1.0 / 60.0)
     d2 = (-490.0 / 180.0, 270.0 / 180.0, -27.0 / 180.0, 2.0 / 180.0)
@@ -115,66 +118,68 @@
         return ref[0, at + 3 if at < 0 else at - X, rows, cols]
 
     def tile(r, carry):
-        rows = pl.ds(pl.multiple_of(r * 8, 8), 8)
+        rows = pl.ds(pl.multiple_of(r // (NY // step) * 8, 8), 8)
+        cols = pl.ds(pl.multiple_of(r % (NY // step) * step, step), step)
         for x in range(X):
-            for at in range(0, NY, step):
-                cols = slice(at, at + step)
-                u = ui[0, x, rows, cols]
-                if has_c:
-                    buf[0, x, rows, cols] = -u2[0, x, rows, cols] * u
-                buf[base, x, rows, cols] = u
-                if has_w:
-                    acc = (viscosity * d2[0]) * u
-                    for o in (1, 2, 3):
-                        up = pick(comp, x + o, rows, cols)
-                        dn = pick(comp, x - o, rows, cols)
-                        if comp == 0:
-                            xp, xm = up, dn
-                        else:
-                            xp = pick(0, x + o, rows, cols)
-                            xm = pick(0, x - o, rows, cols)
-                        acc = acc + (viscosity * d2[o]) * (up + dn)
-                        acc = acc - d1[o] * (xp * up - xm * dn)
+            u = ui[0, x, rows, cols]
+            if has_c:
+                buf[0, x, rows, cols] = -u2[0, x, rows, cols] * u
+            buf[base, x, rows, cols] = u
+            if has_w:
+                acc = (viscosity * d2[0]) * u
+                for o in (1, 2, 3):
+                    up = pick(comp, x + o, rows, cols)
+                    dn = pick(comp, x - o, rows, cols)
                     if comp == 0:
-                        acc = acc + (2.0 * omega) * u1[0, x, rows, cols]
-                    if comp == 1:
-                        acc = acc - ((2.0 - shear_param) * omega) * u0[0, x, rows, cols]
-                    buf[base + 1, x, rows, cols] = acc
-                    buf[base + 2, x, rows, cols] = -(u1[0, x, rows, cols] + bg_ref[x]) * u
+                        xp, xm = up, dn
+                    else:
+                        xp = pick(0, x + o, rows, cols)
+                        xm = pick(0, x - o, rows, cols)
+                    acc = acc + (viscosity * d2[o]) * (up + dn)
+                    acc = acc - d1[o] * (xp * up - xm * dn)
+                if comp == 0:
+                    acc = acc + (2.0 * omega) * u1[0, x, rows, cols]
+                if comp == 1:
+                    acc = acc - ((2.0 - shear_param) * omega) * u0[0, x, rows, cols]
+                buf[base + 1, x, rows, cols] = acc
+                buf[base + 2, x, rows, cols] = -(u1[0, x, rows, cols] + bg_ref[x]) * u
         return carry
 
-    lax.fori_loop(0, Rz // 8, tile, 0)
+    lax.fori_loop(0, Rz // 8 * (NY // step), tile, 0)
     M = X * Rz
     wide = 2 * half
     for n, want in enumerate(jobs):
         lo = 0 if "c" in want else base
         hi = base + (3 if "w" in want else 1)
-        lhs = buf[lo:hi].reshape((hi - lo) * M, NY)
-        res = dot3(split_value(lhs), (mats[3 * n][...], mats[3 * n + 1][...]))
-        vec_ref = mats[3 * n + 2]
-        u_at = (base - lo) * M
-        at = 0
+        high, low, vec_ref = mats[3 * n : 3 * n + 3]
+
+        def product(f, carry):
+            lhs = split_value(buf[f].reshape(M, NY))
+            res[f] = dot3(lhs, (high[...], low[...]))
+            return carry
+
+        lax.fori_loop(lo, hi, product, 0)
+        slot = 0
         for out in outs[n * n_out : (n + 1) * n_out]:
             for j in range(out.shape[-1] // wide):
-                cols = slice(at, at + wide)
+                cols = block_at(ids[slot], wide)
                 own = slice(j * wide, (j + 1) * wide)
-                yu = res[u_at : u_at + M, cols]
+                yu = res[base, :, cols]
                 if "c" in want:
                     out[0, :, :, own] = yu.reshape(X, Rz, wide)
-                    out[1, :, :, own] = res[:M, cols].reshape(X, Rz, wide)
+                    out[1, :, :, own] = res[0, :, cols].reshape(X, Rz, wide)
                 if "w" in want:
-                    k = u_at + M
                     ky = vec_ref[0:1, cols]
                     w = (
-                        res[k : k + M, cols]
-                        + ky * rot(res[k + M : k + 2 * M, cols], half)
+                        res[base + 1, :, cols]
+                        + ky * rot(res[base + 2, :, cols], half)
                         - (viscosity * ky * ky) * yu
                     )
                     out[len(want) - 1, :, :, own] = w.reshape(X, Rz, wide)
-                at += wide
-
-
-def spectra_call(comp, jobs, vel, ghost, background, omega, mats, widths, half, us):
+                slot += 1
+
+
+def spectra_call(comp, jobs, vel, ghost, ids, background, omega, mats, widths, half, us):
     _, X, Rz, NY = vel.shape
     has_w = any("w" in want for want in jobs)
     has_c = any("c" in want for want in jobs)
@@ -193,20 +198,23 @@
     return pl.pallas_call(
         lambda *refs: spectra_body(comp, omega, half, jobs, comps, len(widths), *refs),
         grid=(1,),
-        in_specs=[pl.BlockSpec(memory_space=pltpu.SMEM)]
+        in_specs=[pl.BlockSpec(memory_space=pltpu.SMEM)] * 2
         + [plane(c) for c in comps]
         + halo_specs
         + [full_spec(a.shape) for a in flat],
         out_specs=[full_spec(shape) for shape in shapes],
         out_shape=[jax.ShapeDtypeStruct(shape, f32) for shape in shapes],
-        scratch_shapes=[pltpu.VMEM((count, X, Rz, NY), f32)],
+        scratch_shapes=[
+            pltpu.VMEM((count, X, Rz, NY), f32),
+            pltpu.VMEM((count, X * Rz, sum(widths)), f32),
+        ],
         compiler_params=params(50),
         cost_estimate=cost(us),
         name="spectra",
-    )(background, *([vel] * len(comps)), *halos, *flat)
-
-
-def z_body(counts, n_t, half, mh_ref, ml_ref, *rest):
+    )(ids, background, *([vel] * len(comps)), *halos, *flat)
+
+
+def z_body(counts, first_id, n_t, half, ids, mh_ref, ml_ref, *rest):
     n_in = len(counts)
     ins, outs, buf = rest[:n_in], rest[n_in : n_in + n_t], rest[-1]
     _, X, Rz, _ = ins[0].shape
@@ -214,13 +222,14 @@
     depth = outs[0].shape[1]
     for t in range(n_t):
         own = slice(t * wide, (t + 1) * wide)
-        at = 0
+        n = 0
         for ref, count in zip(ins, counts):
             for f in range(count):
+                rows = block_at(ids[first_id + n // 3] * 3 + n % 3, Rz)
                 for x in range(X):
                     col = (t * X + x) * wide
-                    buf[at : at + Rz, col : col + wide] = ref[f, x, :, own]
-                at += Rz
+                    buf[rows, col : col + wide] = ref[f, x, :, own]
+                n += 1
     res = dot3((mh_ref[...], ml_ref[...]), split_value(buf[...]))
     for t in range(n_t):
         for x in range(X):
@@ -229,19 +238,21 @@
             outs[t][x] = res[:depth, cols] + rot(res[depth:, cols], half)
 
 
-def z_call(m_pair, ins, n_t, half):
+def z_call(m_pair, ids, first_id, ins, n_t, half):
     flat = [a for source in ins for a in source]
     counts = [a.shape[0] for a in flat]
     _, X, Rz, _ = flat[0].shape
     depth = m_pair[0].shape[0] // 2
     return pl.pallas_call(
-        lambda *refs: z_body(counts, n_t, half, *refs),
+        lambda *refs: z_body(counts, first_id, n_t, half, *refs),
+        in_specs=[pl.BlockSpec(memory_space=pltpu.SMEM)]
+        + [pl.BlockSpec(memory_space=pltpu.VMEM)] * (2 + len(flat)),
         out_shape=[jax.ShapeDtypeStruct((X, depth, 2 * half), f32)] * n_t,
         scratch_shapes=[pltpu.VMEM((sum(counts) * Rz, n_t * X * 2 * half), f32)],
         compiler_params=params(24, 0),
         cost_estimate=cost(4),
         name="zforward",
-    )(*m_pair, *flat)
+    )(ids, *m_pair, *flat)
 
 
 def shear_body(meta, up, down, up_out, down_out):
@@ -293,9 +304,16 @@
     return v
 
 
-def prep_body(n_part, half, vec_ref, kz_ref, *rest):
-    parts = [rest[i * n_part : (i + 1) * n_part] for i in range(3)]
-    up, down = rest[3 * n_part :]
+def cut(refs, counts):
+    out, at = [], 0
+    for n in counts:
+        out.append(refs[at : at + n])
+        at += n
+    return out, refs[at:]
+
+
+def prep_body(counts, half, vec_ref, kz_ref, *rest):
+    parts, (up, down) = cut(rest, counts)
     X, depth = parts[0][0].shape[:2]
     ky = vec_ref[0:1]
 
@@ -322,7 +340,7 @@
 
 def prep_call(parts, vec, kz, half):
     X, depth, wide = parts[0][0].shape
-    n = len(parts[0])
+    n = [len(p) for p in parts]
     nb = blocks_of(depth)
     rows = depth // nb
     flat = [a for p in parts for a in p]
@@ -353,9 +371,8 @@
     return jnp.where(low, pltpu.roll(re, half, axis=1), im)
 
 
-def solve_body(chunk, half, n_slot, n_part, nb, vec_ref, kz_ref, inv_ref, mh_ref, ml_ref, fl, fr, p0, p0l, p0r, q_old, *rest):
-    parts = [rest[i * n_part : (i + 1) * n_part] for i in range(3)]
-    rest = rest[3 * n_part :]
+def solve_body(chunk, half, n_slot, counts, nb, ids, vec_ref, kz_ref, inv_ref, mh_ref, ml_ref, fl, fr, p0, p0l, p0r, q_old, *rest):
+    parts, rest = cut(rest, counts)
     q_out, p_out = rest[:2]
     outs, buf = rest[2:-1], rest[-1]
     X, depth = p_out.shape[:2]
@@ -421,29 +438,27 @@
             res = dot3(mats, split_value(buf[i]))
             for x in range(X):
                 cols = slice(x * wide, (x + 1) * wide)
-                h = res[:total, cols] + rot(res[total:, cols], half)
-                for s in range(n_slot):
-                    piece = h[s * Rz : (s + 1) * Rz]
-                    if len(outs) == n_slot:
-                        outs[s][i, x] = piece
-                    else:
-                        outs[i * n_slot + s][0, x] = piece
-
-
-def solve_call(chunk, half, n_slot, split, vec, kz, inv, m_pair, parts, fl, fr, p0, p0l, p0r, q_old):
+                buf[i, :, cols] = (res[:total, cols] + rot(res[total:, cols], half)) * vec_ref[5:6]
+            for s in range(n_slot):
+                rows = block_at(ids[2 * n_slot + 2 + s], Rz)
+                for x in range(X):
+                    outs[s][i, x] = buf[i, rows, x * wide : (x + 1) * wide]
+
+
+def solve_call(chunk, half, n_slot, ids, vec, kz, inv, m_pair, parts, fl, fr, p0, p0l, p0r, q_old):
     X, depth, wide = parts[0][0].shape
     nb = blocks_of(depth)
     rows = depth // nb
-    n = len(parts[0])
+    n = [len(p) for p in parts]
     flat = [a for p in parts for a in p]
     packed = p0.shape[-1]
-    lead = 1 if split else 3
-    n_h = n_slot * (3 if split else 1)
-    h_shape = (lead, X, depth // n_slot, wide)
+    n_h = n_slot
+    h_shape = (3, X, depth // n_slot, wide)
     out = pl.pallas_call(
         lambda *refs: solve_body(chunk, half, n_slot, n, nb, *refs),
         grid=(nb,),
         in_specs=[
+            pl.BlockSpec(memory_space=pltpu.SMEM),
             full_spec(vec.shape),
             row_block((), rows, wide),
             row_block((), rows, wide),
@@ -468,42 +483,40 @@
         compiler_params=params(40),
         cost_estimate=cost(10),
         name="solve",
-    )(vec, kz, inv, *m_pair, fl, fr, p0, p0l, p0r, q_old, *flat)
-    q, p, hs = out[0], out[1], list(out[2:])
-    if split:
-        return q, p, [hs[i * n_slot : (i + 1) * n_slot] for i in range(3)]
-    return q, p, [hs]
-
-
-def back_body(n_slot, base_ref, gh_ref, gl_ref, *rest):
-    hs, out = rest[:n_slot], rest[-1]
+    )(ids, vec, kz, inv, *m_pair, fl, fr, p0, p0l, p0r, q_old, *flat)
+    return out[0], out[1], [list(out[2:])]
+
+
+def back_body(n_slot, ids, base_ref, gh_ref, gl_ref, *rest):
+    hs, (out, buf) = rest[:n_slot], rest[n_slot:]
     _, X, Rz, wide = hs[0].shape
-    lhs = jnp.concatenate([h[...].reshape(X * Rz, wide) for h in hs], axis=1)
-    res = dot3(split_value(lhs), (gh_ref[...], gl_ref[...]), ((1,), (1,)))
+    for s, h in enumerate(hs):
+        buf[:, block_at(ids[3 * n_slot + 2 + s], wide)] = h[...].reshape(X * Rz, wide)
+    res = dot3(split_value(buf[...]), (gh_ref[...], gl_ref[...]), ((1,), (1,)))
     out[...] = base_ref[...] + section_weight * res.reshape(out.shape)
 
 
-def back_call(base, g_pair, hs, comp):
+def back_call(base, g_pair, ids, hs):
     _, X, Rz, NY = base.shape
     wide = hs[0].shape[-1]
-    if comp is None:
-        grid, at = (3,), lambda i: (i, 0, 0, 0)
-        h_at = at
-    else:
-        grid, at = (1,), lambda i: (comp, 0, 0, 0)
-        h_at = lambda i: (0, 0, 0, 0)
+    plane = lambda w: pl.BlockSpec((1, X, Rz, w), lambda i: (i, 0, 0, 0))
     return pl.pallas_call(
         lambda *refs: back_body(len(hs), *refs),
-        grid=grid,
-        in_specs=[pl.BlockSpec((1, X, Rz, NY), at), full_spec(g_pair[0].shape), full_spec(g_pair[1].shape)]
-        + [pl.BlockSpec((1, X, Rz, wide), h_at)] * len(hs),
-        out_specs=pl.BlockSpec((1, X, Rz, NY), at),
+        grid=(3,),
+        in_specs=[
+            pl.BlockSpec(memory_space=pltpu.SMEM),
+            plane(NY),
+            full_spec(g_pair[0].shape),
+            full_spec(g_pair[1].shape),
+        ]
+        + [plane(wide)] * len(hs),
+        out_specs=plane(NY),
         out_shape=jax.ShapeDtypeStruct(base.shape, f32),
-        input_output_aliases={} if comp is None else {0: 0},
+        scratch_shapes=[pltpu.VMEM((X * Rz, len(hs) * wide), f32)],
         compiler_params=params(32),
         cost_estimate=cost(7),
         name="back",
-    )(base, *g_pair, *hs)
+    )(ids, base, *g_pair, *hs)
 
 
 def pack_body(half, a_ref, b_ref, out):
@@ -564,14 +577,11 @@
 
     if paired:
         slot_groups = jnp.stack([g, G - 1 - g, g ^ 1, G - 1 - (g ^ 1)])
-        sources = jnp.stack([g, g ^ 1])
-        n_t = 2
+        slot_sources = slot_groups
     else:
         slot_groups = (g + jnp.arange(G, dtype=jnp.int32)) % G
-        sources = (g - jnp.arange(G, dtype=jnp.int32)) % G
-        n_t = 1
+        slot_sources = (g - jnp.arange(G, dtype=jnp.int32)) % G
     back_groups = (g - jnp.arange(G, dtype=jnp.int32)) % G
-    widths = [n_t * wide] * (2 if paired else G)
 
     def modes_of(groups, j):
         return groups[:, None] * L + j * half + jnp.arange(half, dtype=jnp.int32)[None, :]
@@ -585,43 +595,44 @@
     signed = jnp.where(m < depth // 2, m, m - depth)
     kz1 = 2.0 * math.pi / depth * signed.astype(f32)
     kz = jnp.broadcast_to(kz1[:, None], (depth, wide))
-    zloc = jnp.arange(Rz, dtype=jnp.int32)
-    norm_z = 1.0 / math.sqrt(depth)
-    kc = kz1[:, None]
-    n_src = sources.shape[0]
-    three = (n_src, 3, Rz)
-    z_cols = jnp.broadcast_to((sources[:, None] * Rz + zloc[None, :])[:, None], three).reshape(-1)
-    field = jnp.broadcast_to(jnp.arange(3, dtype=jnp.int32)[None, :, None], three).reshape(1, -1)
-    ang = z_angles(depth, m, z_cols)
-    cz, sz = jnp.cos(ang) * norm_z, jnp.sin(ang) * norm_z
-    gain = jnp.where(field == 0, -viscosity * kc * kc, jnp.where(field == 1, kc, 1.0))
-    real = gain * jnp.where(field == 1, sz, cz)
-    imag = gain * jnp.where(field == 1, cz, -sz)
-    m_fwd = split_const(jnp.concatenate([real, imag], axis=0))
+    m_inv = z_inverse_matrix(depth)
+    m_direct = split_const(z_forward_matrix(depth, Rz, range(G)))
+    pair_at = jnp.stack([g % 2, 1 - g % 2])
+    if paired:
+        halves = [split_const(z_forward_matrix(depth, Rz, (n, n + 1))) for n in (0, 2)]
+        m_pair = [jnp.where(g < 2, low, high) for low, high in zip(*halves)]
     dest = (g + jnp.arange(G, dtype=jnp.int32)) % G
-    z_rows = (dest[:, None] * Rz + zloc[None, :]).reshape(-1)
-    ang_b = z_angles(depth, z_rows, m)
-    m_inv = split_const(
-        jnp.concatenate([jnp.cos(ang_b) * norm_z, jnp.sin(ang_b) * norm_z], axis=0)
-    )
+    ids = jnp.concatenate([slot_groups, slot_sources, pair_at, dest, back_groups])
     xpos = (slab * X + jnp.arange(X, dtype=jnp.int32)).astype(f32) + 0.5 - total_x / 2.0
     background = -shear_param * omega * xpos
 
     f_pairs, kys = [], []
     for j in range(J):
-        modes = modes_of(slot_groups, j)
-        f_pairs.append(y_matrix(NY, modes, jnp.ones(modes.shape, f32)))
-        kys.append(twice(unit_y * modes.astype(f32)))
+        modes = np.arange(G)[:, None] * L + j * half + np.arange(half)[None, :]
+        f_pairs.append(y_matrix(NY, modes))
+        both = np.concatenate([modes, modes], axis=1).reshape(1, -1)
+        kys.append(jnp.asarray((unit_y * both).astype(np.float32)))
 
     swap = [(i, i ^ 1) for i in range(G)]
     cross = [(i, G - 1 - i) for i in range(G)]
-
-    def scatter(pieces):
-        if paired:
-            return [pieces[0], lax.ppermute(pieces[1], "yz", swap)]
-        return [pieces[0]] + [
-            lax.ppermute(pieces[s], "yz", ring("yz", s)) for s in range(1, len(pieces))
-        ]
+    if paired:
+        slot_perms = [None, cross, swap, ring("yz", 2)]
+    else:
+        slot_perms = [ring("yz", s) for s in range(G)]
+
+    def direct(j):
+        return not paired or j == 0
+
+    def widths_of(j):
+        return [wide] * G if direct(j) else [2 * wide] * 2
+
+    def scatter(pieces, j):
+        perms = slot_perms if direct(j) else [None, swap]
+        order = [2, 3, 1] if paired and direct(j) else range(1, len(pieces))
+        out = [pieces[0]] + [None] * (len(pieces) - 1)
+        for s in order:
+            out[s] = lax.ppermute(pieces[s], "yz", perms[s])
+        return out
 
     token = []
 
@@ -631,13 +642,16 @@
     def mark(*arrays):
         token[:] = arrays
 
-    def gather_z(sent):
+    def gather_z(sent, j):
         ins = [list(source) for source in zip(*sent)]
-        got = z_call((chained(m_fwd[0]), m_fwd[1]), ins, n_t, half)
+        whole_z = direct(j)
+        mats = m_direct if whole_z else m_pair
+        first_id = G if whole_z else 2 * G
+        got = z_call((chained(mats[0]), mats[1]), ids, first_id, ins, 1 if whole_z else 2, half)
         mark(got[-1])
-        if paired:
-            return [got[0], lax.ppermute(got[1], "yz", cross)]
-        return [got[0]]
+        if whole_z:
+            return [got[0]]
+        return [got[0], lax.ppermute(got[1], "yz", cross)]
 
     ghost = {}
     sends, parts, faces, solved = {}, {}, {}, {}
@@ -655,17 +669,18 @@
         mark(*ghost[n])
 
     def spectra(i, *jobs, us=8):
+        widths = widths_of(jobs[0][0])
         flat = spectra_call(
-            i, [want for _, want in jobs], vel, ghost, chained(background), omega,
+            i, [want for _, want in jobs], vel, ghost, ids, chained(background), omega,
             [f_pairs[j] + (kys[j],) for j, _ in jobs], widths, half, us,
         )
         mark(flat[-1])
         n = len(widths)
         for at, (j, _) in enumerate(jobs):
-            sends.setdefault((i, j), []).append(scatter(flat[at * n : (at + 1) * n]))
+            sends.setdefault((i, j), []).append(scatter(flat[at * n : (at + 1) * n], j))
 
     def forward_z(i, j):
-        parts[i, j] = gather_z(sends[i, j])
+        parts[i, j] = gather_z(sends[i, j], j)
 
     p_halo = []
 
@@ -681,7 +696,8 @@
                 jnp.where(first, es, 0.0),
                 jnp.where(last, ec, 1.0),
                 jnp.where(last, -es, 0.0),
-                jnp.zeros((3, wide), f32),
+                twice(jnp.where(own == 0, 1.0, 2.0).astype(f32)),
+                jnp.zeros((2, wide), f32),
             ],
             axis=0,
         )
@@ -700,10 +716,10 @@
             lax.ppermute(down, "gx", ring("gx", -1)),
         )
 
-    def solve(j, split):
+    def solve(j):
         vec, inv, mine, fl, fr = faces[j]
         q, p, groups = solve_call(
-            j, half, G, split, chained(vec), kz, inv, m_inv, mine, fl, fr,
+            j, half, G, ids, chained(vec), kz, inv, m_inv, mine, fl, fr,
             pressure_guess, p_halo[0], p_halo[1], q_old,
         )
         mark(q)
@@ -718,48 +734,43 @@
             out.append(got)
         return out
 
-    def back_matrix(j):
-        back_modes = modes_of(back_groups, j)
-        weights = jnp.where(back_modes == 0, 1.0, 2.0).astype(f32)
-        return y_matrix(NY, back_modes, weights)
-
     def guess_halo():
         guess = chained(pressure_guess)
         p_halo.append(lax.ppermute(guess[X - 3 :], "gx", ring("gx", 1)))
         p_halo.append(lax.ppermute(guess[:3], "gx", ring("gx", -1)))
 
     if J == 2:
+        spectra(0, (0, "uc"), us=6)
         vel_halo(0, 0, 1)
-        spectra(0, (0, "uc"), us=6)
         vel_halo(1, 1, 3)
         spectra(1, (0, "uc"), us=6)
         shear(0)
         spectra(0, (0, "w"))
         spectra(2, (0, "uc"), us=6)
-        guess_halo()
-        forward_z(0, 0)
         shear(1)
         spectra(1, (0, "w"))
         spectra(2, (0, "w"))
+        spectra(0, (1, "ucw"))
+        spectra(1, (1, "ucw"))
+        forward_z(0, 0)
+        spectra(2, (1, "ucw"))
+        guess_halo()
         forward_z(1, 0)
-        spectra(0, (1, "ucw"))
+        forward_z(0, 1)
         forward_z(2, 0)
-        spectra(1, (1, "ucw"))
-        forward_z(0, 1)
-        spectra(2, (1, "ucw"))
         prep(0)
         forward_z(1, 1)
-        solve(0, False)
+        solve(0)
         forward_z(2, 1)
+        prep(1)
         q, p, groups = solved[0]
         solved[0] = (q, p, [[chained(h) for h in hs] for hs in groups])
         got = give_back(0)
-        prep(1)
-        solve(1, False)
+        solve(1)
         got1 = give_back(1)
         base = chained(vel)
-        result = back_call(base, back_matrix(0), got[0], None)
-        result = back_call(result, back_matrix(1), got1[0], None)
+        result = back_call(base, f_pairs[0], ids, got[0])
+        result = back_call(result, f_pairs[1], ids, got1[0])
     else:
         if J > 2:
             raise NotImplementedError
@@ -774,8 +785,8 @@
                 spectra(i, (j, "ucw"))
                 forward_z(i, j)
             prep(j)
-            solve(j, False)
-            result = back_call(result, back_matrix(j), give_back(j)[0], None)
+            solve(j)
+            result = back_call(result, f_pairs[j], ids, give_back(j)[0])
     q_parts = [solved[j][0] for j in range(J)]
     p_parts = [solved[j][1] for j in range(J)]
     return result, pack_call(q_parts, half), pack_call(p_parts, half)

time: 380 us -> 379 us (level)
  the two profiles are of different devices: /device:TPU:8 before, /device:TPU:27 now
where the time goes in v1:
time: 379 us; the launch traced here: 378 us
  Pallas kernels  124 us (33%)
  waiting for transfers between devices  116 us (31%)
  starting transfers between devices  105 us (28%)
  local copies, waits for them, and re-layouts  25.1 us (7%)
  other arithmetic  5.95 us (2%)
    pallas_call x9, Pallas kernels, spectra_call(): pl.pallas_call(lambda *refs: spectra_body(comp, omega, half, jobs, comps,...  62.1 us
    ppermute x6, starting transfers between devices, give_back(): got.append(lax.ppermute(hs[s], 'yz', ring('yz', s)))  51.9 us
    ppermute x21, waiting for transfers between devices, scatter(): out[s] = lax.ppermute(pieces[s], 'yz', perms[s])  48.2 us
    ppermute x6, waiting for transfers between devices, give_back(): got.append(lax.ppermute(hs[s], 'yz', ring('yz', s)))  43.6 us
    ppermute x21, starting transfers between devices, scatter(): out[s] = lax.ppermute(pieces[s], 'yz', perms[s])  22.3 us
    unnamed x198, local copies, waits for them, and re-layouts  22.1 us
    pallas_call x6, Pallas kernels, z_call(): pl.pallas_call(lambda *refs: z_body(counts, first_id, n_t, half, *refs),...  19.8 us
    pallas_call x2, Pallas kernels, solve_call(): pl.pallas_call(lambda *refs: solve_body(chunk, half, n_slot, n, nb, *refs...  18.7 us
  transfers between devices with their start and end apart: 40, of which 13 were waited for; matrix products, arithmetic and copies ran while one was open for 2% of the time, Pallas kernels for 29%

profile of v1, /device:TPU:27, one launch (start us, length us, event | category | flops | bytes accessed | tf_op | source)
XLA Modules:
  0.0 377.9 jit_solution(9584473535723514077)
XLA Ops:
  3.9 5.1 %spectra.9 = (f32[2,6,48,128]{3,2,1,0:T(8,128)S(1)}, f32[2,6,48,128]{3,2,1,0:T(8,128)S(1)}, f32[2,6,48,128]{3,2,1,0:T(8,128)S(1)}, f32[2,6,48,128]{3,2,1,0:T(8,128)}) custom-call(s32[18]{0:T(128)S(1)} %concatenate.120.refs_0_, f32[6]{0:T(128)S(1)} %add_multiply_fusion.refs_1_, f32[3,6,48,1024]{3,2,1,0:T(8,128)} %refs_1_, f32[3,6,48,1024]{3,2,1,0:T(8,128)} %refs_1_, ...), custom_call_target="tpu_custom_call" | custom-call | flops 1500000000 | tf_op jit(solution)/shard_map/spectra/pallas_call | solution.py:198
  14.6 2.6 collective-permute-start.2
  21.6 5.2 %spectra.10 = (f32[2,6,48,128]{3,2,1,0:T(8,128)S(1)}, f32[2,6,48,128]{3,2,1,0:T(8,128)S(1)}, f32[2,6,48,128]{3,2,1,0:T(8,128)}, f32[2,6,48,128]{3,2,1,0:T(8,128)}) custom-call(s32[18]{0:T(128)S(1)} %concatenate.120.refs_0_, f32[6]{0:T(128)S(1)} %add_multiply_fusion.refs_1_, f32[3,6,48,1024]{3,2,1,0:T(8,128)} %refs_1_, f32[3,6,48,1024]{3,2,1,0:T(8,128)} %refs_1_, ...), custom_call_target="tpu_custom_call" | custom-call | flops 1500000000 | tf_op jit(solution)/shard_map/spectra/pallas_call | solution.py:198
  30.2 2.1 collective-permute-start.4
  32.7 2.2 shear.2
  34.9 7.0 %spectra.11 = (f32[1,6,48,128]{3,2,1,0:T(8,128)S(1)}, f32[1,6,48,128]{3,2,1,0:T(8,128)}, f32[1,6,48,128]{3,2,1,0:T(8,128)}, f32[1,6,48,128]{3,2,1,0:T(8,128)}) custom-call(s32[18]{0:T(128)S(1)} %concatenate.120.refs_0_, f32[6]{0:T(128)S(1)} %add_multiply_fusion.refs_1_, f32[3,6,48,1024]{3,2,1,0:T(8,128)} %refs_1_, f32[3,6,48,1024]{3,2,1,0:T(8,128)} %refs_1_, ...), custom_call_target="tpu_custom_call" | custom-call | flops 2000000000 | tf_op jit(solution)/shard_map/spectra/pallas_call | solution.py:198
  42.0 4.6 %spectra.12 = (f32[2,6,48,128]{3,2,1,0:T(8,128)S(1)}, f32[2,6,48,128]{3,2,1,0:T(8,128)}, f32[2,6,48,128]{3,2,1,0:T(8,128)S(1)}, f32[2,6,48,128]{3,2,1,0:T(8,128)S(1)}) custom-call(s32[18]{0:T(128)S(1)} %concatenate.120.refs_0_, f32[6]{0:T(128)S(1)} %add_multiply_fusion.refs_1_, f32[3,6,48,1024]{3,2,1,0:T(8,128)} %refs_1_, bf16[1024,512]{1,0:T(8,128)(2,1)S(1)} %copy-done.6, ...), custom_call_target="tpu_custom_call" | custom-call | flops 1500000000 | tf_op jit(solution)/shard_map/spectra/pallas_call | solution.py:198
  48.0 4.1 %collective-permute-done.3.down = f32[2,3,48,1024]{3,2,1,0:T(8,128)S(1)} collective-permute-done((f32[2,3,48,1024]{3,2,1,0:T(8,128)}, f32[2,3,48,1024]{3,2,1,0:T(8,128)S(1)}, u32[]{:S(2)}, u32[]{:S(2)}) %collective-permute-start.3) | collective-permute-done | bytes 1179680 | tf_op jit(solution)/shard_map/ppermute | solution.py:664
  52.1 2.0 collective-permute-start.10
  57.5 6.6 %spectra.13 = (f32[1,6,48,128]{3,2,1,0:T(8,128)S(1)}, f32[1,6,48,128]{3,2,1,0:T(8,128)S(1)}, f32[1,6,48,128]{3,2,1,0:T(8,128)S(1)}, f32[1,6,48,128]{3,2,1,0:T(8,128)S(1)}) custom-call(s32[18]{0:T(128)S(1)} %concatenate.120.refs_0_, f32[6]{0:T(128)S(1)} %add_multiply_fusion.refs_1_, f32[3,6,48,1024]{3,2,1,0:T(8,128)} %refs_1_, f32[3,6,48,1024]{3,2,1,0:T(8,128)} %refs_1_, ...), custom_call_target="tpu_custom_call" | custom-call | flops 2000000000 | tf_op jit(solution)/shard_map/spectra/pallas_call | solution.py:198
  65.5 7.0 %spectra.14 = (f32[1,6,48,128]{3,2,1,0:T(8,128)S(1)}, f32[1,6,48,128]{3,2,1,0:T(8,128)S(1)}, f32[1,6,48,128]{3,2,1,0:T(8,128)S(1)}, f32[1,6,48,128]{3,2,1,0:T(8,128)S(1)}) custom-call(s32[18]{0:T(128)S(1)} %concatenate.120.refs_0_, f32[6]{0:T(128)S(1)} %add_multiply_fusion.refs_1_, f32[3,6,48,1024]{3,2,1,0:T(8,128)} %refs_1_, f32[3,6,48,1024]{3,2,1,0:T(8,128)} %refs_1_, ...), custom_call_target="tpu_custom_call" | custom-call | flops 2000000000 | tf_op jit(solution)/shard_map/spectra/pallas_call | solution.py:198
  75.2 9.1 %spectra.15 = (f32[3,6,48,256]{3,2,1,0:T(8,128)S(1)}, f32[3,6,48,256]{3,2,1,0:T(8,128)}) custom-call(s32[18]{0:T(128)S(1)} %concatenate.120.refs_0_, f32[6]{0:T(128)S(1)} %add_multiply_fusion.refs_1_, f32[3,6,48,1024]{3,2,1,0:T(8,128)} %refs_1_, f32[3,6,48,1024]{3,2,1,0:T(8,128)} %refs_1_, f32[3,6,48,1024]{3,2,1,0:T(8,128)} %refs_1_, ...), custom_call_target="tpu_custom_call" | custom-call | flops 2000000000 | tf_op jit(solution)/shard_map/spectra/pallas_call | solution.py:198
  94.7 8.4 %collective-permute-done.7.refs_8_ = f32[1,6,48,128]{3,2,1,0:T(8,128)S(1)} collective-permute-done((f32[1,6,48,128]{3,2,1,0:T(8,128)}, f32[1,6,48,128]{3,2,1,0:T(8,128)S(1)}, u32[]{:S(2)}, u32[]{:S(2)}) %collective-permute-start.7) | collective-permute-done | bytes 147488 | tf_op jit(solution)/shard_map/ppermute | solution.py:634
  103.9 8.7 %spectra.16 = (f32[3,6,48,256]{3,2,1,0:T(8,128)S(1)}, f32[3,6,48,256]{3,2,1,0:T(8,128)S(1)}) custom-call(s32[18]{0:T(128)S(1)} %concatenate.120.refs_0_, f32[6]{0:T(128)S(1)} %add_multiply_fusion.refs_1_, f32[3,6,48,1024]{3,2,1,0:T(8,128)} %refs_1_, f32[3,6,48,1024]{3,2,1,0:T(8,128)} %refs_1_, f32[3,6,48,1024]{3,2,1,0:T(8,128)} %refs_1_, ...), custom_call_target="tpu_custom_call" | custom-call | flops 2000000000 | tf_op jit(solution)/shard_map/spectra/pallas_call | solution.py:198
  112.7 8.5 %collective-permute-done.9.refs_10_ = f32[1,6,48,128]{3,2,1,0:T(8,128)S(1)} collective-permute-done((f32[1,6,48,128]{3,2,1,0:T(8,128)}, f32[1,6,48,128]{3,2,1,0:T(8,128)S(1)}, u32[]{:S(2)}, u32[]{:S(2)}) %collective-permute-start.9) | collective-permute-done | bytes 147488 | tf_op jit(solution)/shard_map/ppermute | solution.py:634
  121.2 3.5 collective-permute-start.23
  124.7 2.8 zforward.6.refs_2_.refs_12_
  128.3 8.7 %spectra.17 = (f32[3,6,48,256]{3,2,1,0:T(8,128)S(1)}, f32[3,6,48,256]{3,2,1,0:T(8,128)S(1)}) custom-call(s32[18]{0:T(128)S(1)} %concatenate.120.refs_0_, f32[6]{0:T(128)S(1)} %add_multiply_fusion.refs_1_, f32[3,6,48,1024]{3,2,1,0:T(8,128)} %refs_1_, f32[3,6,48,1024]{3,2,1,0:T(8,128)} %refs_1_, f32[3,6,48,1024]{3,2,1,0:T(8,128)} %refs_1_, ...), custom_call_target="tpu_custom_call" | custom-call | flops 2000000000 | tf_op jit(solution)/shard_map/spectra/pallas_call | solution.py:198
  137.6 1.9 collective-permute-start.15
  139.5 19.6 %collective-permute-done.11.refs_6_ = f32[1,6,48,128]{3,2,1,0:T(8,128)S(1)} collective-permute-done((f32[1,6,48,128]{3,2,1,0:T(8,128)S(1)}, f32[1,6,48,128]{3,2,1,0:T(8,128)S(1)}, u32[]{:S(2)}, u32[]{:S(2)}) %collective-permute-start.11) | collective-permute-done | bytes 147488 | tf_op jit(solution)/shard_map/ppermute | solution.py:634
  159.3 10.6 %collective-permute-done.13.refs_8_ = f32[1,6,48,128]{3,2,1,0:T(8,128)S(1)} collective-permute-done((f32[1,6,48,128]{3,2,1,0:T(8,128)S(1)}, f32[1,6,48,128]{3,2,1,0:T(8,128)S(1)}, u32[]{:S(2)}, u32[]{:S(2)}) %collective-permute-start.13) | collective-permute-done | bytes 147488 | tf_op jit(solution)/shard_map/ppermute | solution.py:634
  170.8 1.9 collective-permute-start.18
  172.8 3.0 zforward.7.refs_3_.refs_13_
  175.9 4.3 %zforward.8 = (f32[6,192,128]{2,1,0:T(8,128)S(1)}, f32[6,192,128]{2,1,0:T(8,128)}) custom-call(s32[18]{0:T(128)S(1)} %concatenate.120.refs_0_, bf16[384,288]{1,0:T(8,128)(2,1)S(1)} %copy-done.27, bf16[384,288]{1,0:T(8,128)(2,1)S(1)} %copy-done.28, f32[3,6,48,256]{3,2,1,0:T(8,128)S(1)} %copy-done.37, f32[3,6,48,256]{3,2,1,0:T(8,128)} %collective-permute-done.16.refs_4_), custom_call_target="tpu_custom_call" | custom-call | flops 1000000000 | tf_op jit(solution)/shard_map/zforward/pallas_call | solution.py:246
  181.6 2.1 collective-permute-start.27
  183.7 2.3 collective-permute-start.26
  186.1 2.3 zforward.9.refs_4_.refs_14_
  188.6 2.2 prep.2
  192.2 3.7 zforward.10
  196.7 2.2 collective-permute-start.29
  200.0 7.6 %collective-permute-done.24.refs_6_ = f32[5,192,128]{2,1,0:T(8,128)S(1)} collective-permute-done((f32[5,192,128]{2,1,0:T(8,128)S(1)}, f32[5,192,128]{2,1,0:T(8,128)S(1)}, u32[]{:S(2)}, u32[]{:S(2)}) %collective-permute-start.24) | collective-permute-done | bytes 491552 | tf_op jit(solution)/shard_map/ppermute | solution.py:715
  207.6 9.2 %solve.2 = (f32[3,6,192,128]{3,2,1,0:T(8,128)S(1)}, f32[6,192,128]{2,1,0:T(8,128)S(1)}, f32[3,6,48,128]{3,2,1,0:T(8,128)S(1)}, f32[3,6,48,128]{3,2,1,0:T(8,128)S...) custom-call(s32[18]{0:T(128)S(1)} %concatenate.120.refs_0_, ...), custom_call_target="tpu_custom_call" | custom-call | flops 2500000000 | tf_op jit(solution)/shard_map/solve/pallas_call | solution.py:457
  217.6 3.7 zforward.11
  222.9 4.4 %collective-permute-done.30.refs_5_.refs_15_ = f32[6,192,128]{2,1,0:T(8,128)} collective-permute-done((f32[6,192,128]{2,1,0:T(8,128)}, f32[6,192,128]{2,1,0:T(8,128)}, u32[]{:S(2)}, u32[]{:S(2)}) %collective-permute-start.30) | collective-permute-done | bytes 589856 | tf_op jit(solution)/shard_map/ppermute | solution.py:654
  227.3 7.4 %collective-permute-done.31.refs_7_.refs_17_ = f32[6,192,128]{2,1,0:T(8,128)} collective-permute-done((f32[6,192,128]{2,1,0:T(8,128)}, f32[6,192,128]{2,1,0:T(8,128)}, u32[]{:S(2)}, u32[]{:S(2)}) %collective-permute-start.31) | collective-permute-done | bytes 589856 | tf_op jit(solution)/shard_map/ppermute | solution.py:654
  236.9 3.9 %prep.3 = (f32[5,192,128]{2,1,0:T(8,128)S(1)}, f32[5,192,128]{2,1,0:T(8,128)S(1)}) custom-call(f32[8,128]{1,0:T(8,128)S(1)} %concatenate.127.refs_0_.refs_1_, f32[192,128]{1,0:T(8,128)S(1)} %broadcast_in_dim.45.refs_1_.refs_2_, f32[6,192,128]{2,1,0:T(8,128)S(1)} %get-tuple-element.147.refs_2_.refs_12_, ...), custom_call_target="tpu_custom_call" | custom-call | flops 1000000000 | tf_op jit(solution)/shard_map/prep/pallas_call | solution.py:347
  240.8 8.6 %collective-permute-start.32 = (f32[5,192,128]{2,1,0:T(8,128)S(1)}, f32[5,192,128]{2,1,0:T(8,128)S(1)}, u32[]{:S(2)}, u32[]{:S(2)}) collective-permute-start(f32[5,192,128]{2,1,0:T(8,128)S(1)} %get-tuple-element.150), channel_id=1, source_target_pairs={{0,4},{4,8},{8,12},{12,16},{16,20},{20,24},{24,28},{28,0},{1,5},{5... | collective-permute-start | bytes 1474568 | tf_op jit(solution)/shard_map/ppermute | solution.py:715
  249.4 8.8 %collective-permute-start.33 = (f32[5,192,128]{2,1,0:T(8,128)S(1)}, f32[5,192,128]{2,1,0:T(8,128)S(1)}, u32[]{:S(2)}, u32[]{:S(2)}) collective-permute-start(f32[5,192,128]{2,1,0:T(8,128)S(1)} %get-tuple-element.151), channel_id=1, source_target_pairs={{0,28},{4,0},{8,4},{12,8},{16,12},{20,16},{24,20},{28,24},{1,29},{... | collective-permute-start | bytes 1474568 | tf_op jit(solution)/shard_map/ppermute | solution.py:716
  258.2 38.6 %collective-permute-start.35 = (f32[3,6,48,128]{3,2,1,0:T(8,128)S(1)}, f32[3,6,48,128]{3,2,1,0:T(8,128)S(1)}, u32[]{:S(2)}, u32[]{:S(2)}) collective-permute-start(f32[3,6,48,128]{3,2,1,0:T(8,128)S(1)} %copy-done.41), channel_id=1, source_target_pairs={{0,2},{1,3},{2,0},{3,1},{4,6},{5,7},{6,4},{7,5},{8,10},{9,11},{10,... | collective-permute-start | bytes 1327112 | tf_op jit(solution)/shard_map/ppermute | solution.py:733
  298.3 9.5 %solve.3 = (f32[3,6,192,128]{3,2,1,0:T(8,128)S(1)}, f32[6,192,128]{2,1,0:T(8,128)S(1)}, f32[3,6,48,128]{3,2,1,0:T(8,128)S(1)}, f32[3,6,48,128]{3,2,1,0:T(8,128)S...) custom-call(s32[18]{0:T(128)S(1)} %concatenate.120.refs_0_, ...), custom_call_target="tpu_custom_call" | custom-call | flops 2500000000 | tf_op jit(solution)/shard_map/solve/pallas_call | solution.py:457
  307.8 1.9 collective-permute-start.37
  309.8 8.6 %collective-permute-start.38 = (f32[3,6,48,128]{3,2,1,0:T(8,128)S(1)}, f32[3,6,48,128]{3,2,1,0:T(8,128)S(1)}, u32[]{:S(2)}, u32[]{:S(2)}) collective-permute-start(f32[3,6,48,128]{3,2,1,0:T(8,128)S(1)} %get-tuple-element.165), channel_id=1, source_target_pairs={{0,2},{1,3},{2,0},{3,1},{4,6},{5,7},{6,4},{7,5},{8,10},{9,11},{10,... | collective-permute-start | bytes 1327112 | tf_op jit(solution)/shard_map/ppermute | solution.py:733
  321.7 3.4 pack.2
  325.0 10.6 %collective-permute-done.35.refs_6_ = f32[3,6,48,128]{3,2,1,0:T(8,128)S(1)} collective-permute-done((f32[3,6,48,128]{3,2,1,0:T(8,128)S(1)}, f32[3,6,48,128]{3,2,1,0:T(8,128)S(1)}, u32[]{:S(2)}, u32[]{:S(2)}) %collective-permute-start.35) | collective-permute-done | bytes 442400 | tf_op jit(solution)/shard_map/ppermute | solution.py:733
  335.7 4.1 %back.2.refs_1_ = f32[3,6,48,1024]{3,2,1,0:T(8,128)S(1)} custom-call(s32[18]{0:T(128)S(1)} %concatenate.120.refs_0_, f32[3,6,48,1024]{3,2,1,0:T(8,128)S(1)} %copy-done.1, bf16[1024,512]{1,0:T(8,128)(2,1)S(1)} %copy-done.7, bf16[1024,512]{1,0:T(8,128)(2,1)S(1)} %copy-done.4, f32[3,6,48,128]{3,2,1,0:T(8,128)S(1)} %copy-done.25, ...), custom_call_target="tpu_custom_call" | custom-call | flops 1750000000 | tf_op jit(solution)/shard_map/back/pallas_call | solution.py:503
  339.8 2.5 collective-permute-done.37.refs_5_
  342.3 30.5 %collective-permute-done.38.refs_6_ = f32[3,6,48,128]{3,2,1,0:T(8,128)S(1)} collective-permute-done((f32[3,6,48,128]{3,2,1,0:T(8,128)S(1)}, f32[3,6,48,128]{3,2,1,0:T(8,128)S(1)}, u32[]{:S(2)}, u32[]{:S(2)}) %collective-permute-start.38) | collective-permute-done | bytes 442400 | tf_op jit(solution)/shard_map/ppermute | solution.py:733
  372.8 5.1 %back.3 = f32[3,6,48,1024]{3,2,1,0:T(8,128)} custom-call(s32[18]{0:T(128)S(1)} %concatenate.120.refs_0_, f32[3,6,48,1024]{3,2,1,0:T(8,128)S(1)} %back.2.refs_1_, bf16[1024,512]{1,0:T(8,128)(2,1)S(1)} %copy-done.11, bf16[1024,512]{1,0:T(8,128)(2,1)S(1)} %copy-done.10, f32[3,6,48,128]{3,2,1,0:T(8,128)S(1)} %get-tuple-element.163.refs_4_, ...), custom_call_target="tpu_custom_call" | custom-call | flops 1750000000 | tf_op jit(solution)/shard_map/back/pallas_call | solution.py:503
  (286 shorter events, 52.8 us)
Async XLA Ops:
  9.0 78.3 %collective-permute-start.8 = (f32[2,6,48,128]{3,2,1,0:T(8,128)}, f32[2,6,48,128]{3,2,1,0:T(8,128)}, u32[]{:S(2)}, u32[]{:S(2)}) collective-permute-start(f32[2,6,48,128]{3,2,1,0:T(8,128)} %get-tuple-element.86), channel_id=1, source_target_pairs={{0,2},{1,3},{2,0},{3,1},{4,6},{5,7},{6,4},{7,5},{8,10},{9,11},{10,... | collective-permute-start | bytes 884744 | tf_op jit(solution)/shard_map/ppermute | solution.py:634
  10.3 19.8 %collective-permute-start.1 = (f32[1,3,48,1024]{3,2,1,0:T(8,128)}, f32[1,3,48,1024]{3,2,1,0:T(8,128)}, u32[]{:S(2)}, u32[]{:S(2)}) collective-permute-start(f32[1,3,48,1024]{3,2,1,0:T(8,128)} %get-tuple-element.171), channel_id=1, source_target_pairs={{0,28},{4,0},{8,4},{12,8},{16,12},{20,16},{24,20},{28,24},{1,29},{... | collective-permute-start | bytes 1769480 | tf_op jit(solution)/shard_map/ppermute | solution.py:664
  11.3 21.0 %collective-permute-start = (f32[1,3,48,1024]{3,2,1,0:T(8,128)}, f32[1,3,48,1024]{3,2,1,0:T(8,128)}, u32[]{:S(2)}, u32[]{:S(2)}) collective-permute-start(f32[1,3,48,1024]{3,2,1,0:T(8,128)} %get-tuple-element.172), channel_id=1, source_target_pairs={{0,4},{4,8},{8,12},{12,16},{16,20},{20,24},{24,28},{28,0},{1,5},{5... | collective-permute-start | bytes 1769480 | tf_op jit(solution)/shard_map/ppermute | solution.py:663
  14.6 37.5 %collective-permute-start.3 = (f32[2,3,48,1024]{3,2,1,0:T(8,128)}, f32[2,3,48,1024]{3,2,1,0:T(8,128)S(1)}, u32[]{:S(2)}, u32[]{:S(2)}) collective-permute-start(f32[2,3,48,1024]{3,2,1,0:T(8,128)} %get-tuple-element.169), channel_id=1, source_target_pairs={{0,28},{4,0},{8,4},{12,8},{16,12},{20,16},{24,20},{28,24},{1,29},{... | collective-permute-start | bytes 3538952 | tf_op jit(solution)/shard_map/ppermute | solution.py:664
  14.6 39.5 %collective-permute-start.2 = (f32[2,3,48,1024]{3,2,1,0:T(8,128)}, f32[2,3,48,1024]{3,2,1,0:T(8,128)S(1)}, u32[]{:S(2)}, u32[]{:S(2)}) collective-permute-start(f32[2,3,48,1024]{3,2,1,0:T(8,128)} %get-tuple-element.170), channel_id=1, source_target_pairs={{0,4},{4,8},{8,12},{12,16},{16,20},{20,24},{24,28},{28,0},{1,5},{5... | collective-permute-start | bytes 3538952 | tf_op jit(solution)/shard_map/ppermute | solution.py:663
  30.2 54.2 %collective-permute-start.4 = (f32[2,6,48,128]{3,2,1,0:T(8,128)S(1)}, f32[2,6,48,128]{3,2,1,0:T(8,128)S(1)}, u32[]{:S(2)}, u32[]{:S(2)}) collective-permute-start(f32[2,6,48,128]{3,2,1,0:T(8,128)S(1)} %copy-done.60), channel_id=1, source_target_pairs={{0,3},{1,2},{2,1},{3,0},{4,7},{5,6},{6,5},{7,4},{8,11},{9,10},{10,... | collective-permute-start | bytes 884744 | tf_op jit(solution)/shard_map/ppermute | solution.py:634
  32.3 53.8 %collective-permute-start.6 = (f32[2,6,48,128]{3,2,1,0:T(8,128)S(1)}, f32[2,6,48,128]{3,2,1,0:T(8,128)S(1)}, u32[]{:S(2)}, u32[]{:S(2)}) collective-permute-start(f32[2,6,48,128]{3,2,1,0:T(8,128)S(1)} %copy-done.56), channel_id=1, source_target_pairs={{0,1},{1,0},{2,3},{3,2},{4,5},{5,4},{6,7},{7,6},{8,9},{9,8},{10,11... | collective-permute-start | bytes 884744 | tf_op jit(solution)/shard_map/ppermute | solution.py:634
  52.1 36.3 %collective-permute-start.10 = (f32[2,6,48,128]{3,2,1,0:T(8,128)S(1)}, f32[2,6,48,128]{3,2,1,0:T(8,128)S(1)}, u32[]{:S(2)}, u32[]{:S(2)}) collective-permute-start(f32[2,6,48,128]{3,2,1,0:T(8,128)S(1)} %get-tuple-element.120), channel_id=1, source_target_pairs={{0,3},{1,2},{2,1},{3,0},{4,7},{5,6},{6,5},{7,4},{8,11},{9,10},{10,... | collective-permute-start | bytes 884744 | tf_op jit(solution)/shard_map/ppermute | solution.py:634
  54.1 36.4 %collective-permute-start.12 = (f32[2,6,48,128]{3,2,1,0:T(8,128)}, f32[2,6,48,128]{3,2,1,0:T(8,128)}, u32[]{:S(2)}, u32[]{:S(2)}) collective-permute-start(f32[2,6,48,128]{3,2,1,0:T(8,128)} %get-tuple-element.122), channel_id=1, source_target_pairs={{0,1},{1,0},{2,3},{3,2},{4,5},{5,4},{6,7},{7,6},{8,9},{9,8},{10,11... | collective-permute-start | bytes 884744 | tf_op jit(solution)/shard_map/ppermute | solution.py:634
  85.2 7.6 %collective-permute-start.5 = (f32[1,6,48,128]{3,2,1,0:T(8,128)}, f32[1,6,48,128]{3,2,1,0:T(8,128)S(1)}, u32[]{:S(2)}, u32[]{:S(2)}) collective-permute-start(f32[1,6,48,128]{3,2,1,0:T(8,128)} %get-tuple-element.112), channel_id=1, source_target_pairs={{0,3},{1,2},{2,1},{3,0},{4,7},{5,6},{6,5},{7,4},{8,11},{9,10},{10,... | collective-permute-start | bytes 442376 | tf_op jit(solution)/shard_map/ppermute | solution.py:634
  86.9 16.2 %collective-permute-start.7 = (f32[1,6,48,128]{3,2,1,0:T(8,128)}, f32[1,6,48,128]{3,2,1,0:T(8,128)S(1)}, u32[]{:S(2)}, u32[]{:S(2)}) collective-permute-start(f32[1,6,48,128]{3,2,1,0:T(8,128)} %get-tuple-element.114), channel_id=1, source_target_pairs={{0,1},{1,0},{2,3},{3,2},{4,5},{5,4},{6,7},{7,6},{8,9},{9,8},{10,11... | collective-permute-start | bytes 442376 | tf_op jit(solution)/shard_map/ppermute | solution.py:634
  87.3 85.5 %collective-permute-start.16 = (f32[3,6,48,256]{3,2,1,0:T(8,128)}, f32[3,6,48,256]{3,2,1,0:T(8,128)}, u32[]{:S(2)}, u32[]{:S(2)}) collective-permute-start(f32[3,6,48,256]{3,2,1,0:T(8,128)} %get-tuple-element.105), channel_id=1, source_target_pairs={{0,1},{1,0},{2,3},{3,2},{4,5},{5,4},{6,7},{7,6},{8,9},{9,8},{10,11... | collective-permute-start | bytes 2654216 | tf_op jit(solution)/shard_map/ppermute | solution.py:634
  89.2 38.3 %collective-permute-start.14 = (f32[2,6,48,128]{3,2,1,0:T(8,128)}, f32[2,6,48,128]{3,2,1,0:T(8,128)}, u32[]{:S(2)}, u32[]{:S(2)}) collective-permute-start(f32[2,6,48,128]{3,2,1,0:T(8,128)} %get-tuple-element.88), channel_id=1, source_target_pairs={{0,2},{1,3},{2,0},{3,1},{4,6},{5,7},{6,4},{7,5},{8,10},{9,11},{10,... | collective-permute-start | bytes 884744 | tf_op jit(solution)/shard_map/ppermute | solution.py:634
  90.5 30.6 %collective-permute-start.9 = (f32[1,6,48,128]{3,2,1,0:T(8,128)}, f32[1,6,48,128]{3,2,1,0:T(8,128)S(1)}, u32[]{:S(2)}, u32[]{:S(2)}) collective-permute-start(f32[1,6,48,128]{3,2,1,0:T(8,128)} %get-tuple-element.94), channel_id=1, source_target_pairs={{0,2},{1,3},{2,0},{3,1},{4,6},{5,7},{6,4},{7,5},{8,10},{9,11},{10,... | collective-permute-start | bytes 442376 | tf_op jit(solution)/shard_map/ppermute | solution.py:634
  93.4 43.6 %collective-permute-start.17 = (f32[2,6,48,128]{3,2,1,0:T(8,128)}, f32[2,6,48,128]{3,2,1,0:T(8,128)S(1)}, u32[]{:S(2)}, u32[]{:S(2)}) collective-permute-start(f32[2,6,48,128]{3,2,1,0:T(8,128)} %get-tuple-element.130), channel_id=1, source_target_pairs={{0,3},{1,2},{2,1},{3,0},{4,7},{5,6},{6,5},{7,4},{8,11},{9,10},{10,... | collective-permute-start | bytes 884744 | tf_op jit(solution)/shard_map/ppermute | solution.py:634
  103.8 33.8 %collective-permute-start.19 = (f32[2,6,48,128]{3,2,1,0:T(8,128)}, f32[2,6,48,128]{3,2,1,0:T(8,128)S(1)}, u32[]{:S(2)}, u32[]{:S(2)}) collective-permute-start(f32[2,6,48,128]{3,2,1,0:T(8,128)} %copy-done.54), channel_id=1, source_target_pairs={{0,1},{1,0},{2,3},{3,2},{4,5},{5,4},{6,7},{7,6},{8,9},{9,8},{10,11... | collective-permute-start | bytes 884744 | tf_op jit(solution)/shard_map/ppermute | solution.py:634
  121.2 69.7 %collective-permute-start.23 = (f32[3,6,48,256]{3,2,1,0:T(8,128)S(1)}, f32[3,6,48,256]{3,2,1,0:T(8,128)S(1)}, u32[]{:S(2)}, u32[]{:S(2)}) collective-permute-start(f32[3,6,48,256]{3,2,1,0:T(8,128)S(1)} %get-tuple-element.107), channel_id=1, source_target_pairs={{0,1},{1,0},{2,3},{3,2},{4,5},{5,4},{6,7},{7,6},{8,9},{9,8},{10,11... | collective-permute-start | bytes 2654216 | tf_op jit(solution)/shard_map/ppermute | solution.py:634
  127.6 31.5 %collective-permute-start.11 = (f32[1,6,48,128]{3,2,1,0:T(8,128)S(1)}, f32[1,6,48,128]{3,2,1,0:T(8,128)S(1)}, u32[]{:S(2)}, u32[]{:S(2)}) collective-permute-start(f32[1,6,48,128]{3,2,1,0:T(8,128)S(1)} %copy-done.78), channel_id=1, source_target_pairs={{0,3},{1,2},{2,1},{3,0},{4,7},{5,6},{6,5},{7,4},{8,11},{9,10},{10,... | collective-permute-start | bytes 442376 | tf_op jit(solution)/shard_map/ppermute | solution.py:634
  137.0 43.2 %collective-permute-start.21 = (f32[2,6,48,128]{3,2,1,0:T(8,128)S(1)}, f32[2,6,48,128]{3,2,1,0:T(8,128)S(1)}, u32[]{:S(2)}, u32[]{:S(2)}) collective-permute-start(f32[2,6,48,128]{3,2,1,0:T(8,128)S(1)} %copy-done.51), channel_id=1, source_target_pairs={{0,2},{1,3},{2,0},{3,1},{4,6},{5,7},{6,4},{7,5},{8,10},{9,11},{10,... | collective-permute-start | bytes 884744 | tf_op jit(solution)/shard_map/ppermute | solution.py:634
  137.6 33.2 %collective-permute-start.15 = (f32[1,6,48,128]{3,2,1,0:T(8,128)S(1)}, f32[1,6,48,128]{3,2,1,0:T(8,128)S(1)}, u32[]{:S(2)}, u32[]{:S(2)}) collective-permute-start(f32[1,6,48,128]{3,2,1,0:T(8,128)S(1)} %copy-done.74), channel_id=1, source_target_pairs={{0,2},{1,3},{2,0},{3,1},{4,6},{5,7},{6,4},{7,5},{8,10},{9,11},{10,... | collective-permute-start | bytes 442376 | tf_op jit(solution)/shard_map/ppermute | solution.py:634
  159.1 10.7 %collective-permute-start.13 = (f32[1,6,48,128]{3,2,1,0:T(8,128)S(1)}, f32[1,6,48,128]{3,2,1,0:T(8,128)S(1)}, u32[]{:S(2)}, u32[]{:S(2)}) collective-permute-start(f32[1,6,48,128]{3,2,1,0:T(8,128)S(1)} %copy-done.76), channel_id=1, source_target_pairs={{0,1},{1,0},{2,3},{3,2},{4,5},{5,4},{6,7},{7,6},{8,9},{9,8},{10,11... | collective-permute-start | bytes 442376 | tf_op jit(solution)/shard_map/ppermute | solution.py:634
  169.9 16.2 %collective-permute-start.22 = (f32[1,6,48,128]{3,2,1,0:T(8,128)S(1)}, f32[1,6,48,128]{3,2,1,0:T(8,128)S(1)}, u32[]{:S(2)}, u32[]{:S(2)}) collective-permute-start(f32[1,6,48,128]{3,2,1,0:T(8,128)S(1)} %copy-done.66), channel_id=1, source_target_pairs={{0,2},{1,3},{2,0},{3,1},{4,6},{5,7},{6,4},{7,5},{8,10},{9,11},{10,... | collective-permute-start | bytes 442376 | tf_op jit(solution)/shard_map/ppermute | solution.py:634
  170.8 10.8 %collective-permute-start.18 = (f32[1,6,48,128]{3,2,1,0:T(8,128)S(1)}, f32[1,6,48,128]{3,2,1,0:T(8,128)S(1)}, u32[]{:S(2)}, u32[]{:S(2)}) collective-permute-start(f32[1,6,48,128]{3,2,1,0:T(8,128)S(1)} %copy-done.70), channel_id=1, source_target_pairs={{0,3},{1,2},{2,1},{3,0},{4,7},{5,6},{6,5},{7,4},{8,11},{9,10},{10,... | collective-permute-start | bytes 442376 | tf_op jit(solution)/shard_map/ppermute | solution.py:634
  172.8 11.0 %collective-permute-start.20 = (f32[1,6,48,128]{3,2,1,0:T(8,128)S(1)}, f32[1,6,48,128]{3,2,1,0:T(8,128)S(1)}, u32[]{:S(2)}, u32[]{:S(2)}) collective-permute-start(f32[1,6,48,128]{3,2,1,0:T(8,128)S(1)} %copy-done.68), channel_id=1, source_target_pairs={{0,1},{1,0},{2,3},{3,2},{4,5},{5,4},{6,7},{7,6},{8,9},{9,8},{10,11... | collective-permute-start | bytes 442376 | tf_op jit(solution)/shard_map/ppermute | solution.py:634
  180.2 37.4 %collective-permute-start.28 = (f32[3,6,48,256]{3,2,1,0:T(8,128)S(1)}, f32[3,6,48,256]{3,2,1,0:T(8,128)S(1)}, u32[]{:S(2)}, u32[]{:S(2)}) collective-permute-start(f32[3,6,48,256]{3,2,1,0:T(8,128)S(1)} %get-tuple-element.116), channel_id=1, source_target_pairs={{0,1},{1,0},{2,3},{3,2},{4,5},{5,4},{6,7},{7,6},{8,9},{9,8},{10,11... | collective-permute-start | bytes 2654216 | tf_op jit(solution)/shard_map/ppermute | solution.py:634
  181.6 15.0 %collective-permute-start.27 = (f32[3,192,256]{2,1,0:T(8,128)S(1)}, f32[3,192,256]{2,1,0:T(8,128)S(1)}, u32[]{:S(2)}, u32[]{:S(2)}) collective-permute-start(f32[3,192,256]{2,1,0:T(8,128)S(1)} %get-tuple-element.173), channel_id=1, source_target_pairs={{0,28},{4,0},{8,4},{12,8},{16,12},{20,16},{24,20},{28,24},{1,29},{... | collective-permute-start | bytes 1769480 | tf_op jit(solution)/shard_map/ppermute | solution.py:740
  183.7 15.5 %collective-permute-start.26 = (f32[3,192,256]{2,1,0:T(8,128)S(1)}, f32[3,192,256]{2,1,0:T(8,128)S(1)}, u32[]{:S(2)}, u32[]{:S(2)}) collective-permute-start(f32[3,192,256]{2,1,0:T(8,128)S(1)} %get-tuple-element.174), channel_id=1, source_target_pairs={{0,4},{4,8},{8,12},{12,16},{16,20},{20,24},{24,28},{28,0},{1,5},{5... | collective-permute-start | bytes 1769480 | tf_op jit(solution)/shard_map/ppermute | solution.py:739
  190.8 16.8 %collective-permute-start.24 = (f32[5,192,128]{2,1,0:T(8,128)S(1)}, f32[5,192,128]{2,1,0:T(8,128)S(1)}, u32[]{:S(2)}, u32[]{:S(2)}) collective-permute-start(f32[5,192,128]{2,1,0:T(8,128)S(1)} %get-tuple-element.135), channel_id=1, source_target_pairs={{0,4},{4,8},{8,12},{12,16},{16,20},{20,24},{24,28},{28,0},{1,5},{5... | collective-permute-start | bytes 1474568 | tf_op jit(solution)/shard_map/ppermute | solution.py:715
  190.9 16.8 %collective-permute-start.25 = (f32[5,192,128]{2,1,0:T(8,128)S(1)}, f32[5,192,128]{2,1,0:T(8,128)S(1)}, u32[]{:S(2)}, u32[]{:S(2)}) collective-permute-start(f32[5,192,128]{2,1,0:T(8,128)S(1)} %get-tuple-element.136), channel_id=1, source_target_pairs={{0,28},{4,0},{8,4},{12,8},{16,12},{20,16},{24,20},{28,24},{1,29},{... | collective-permute-start | bytes 1474568 | tf_op jit(solution)/shard_map/ppermute | solution.py:716
  196.7 26.2 %collective-permute-start.29 = (f32[6,192,128]{2,1,0:T(8,128)}, f32[6,192,128]{2,1,0:T(8,128)}, u32[]{:S(2)}, u32[]{:S(2)}) collective-permute-start(f32[6,192,128]{2,1,0:T(8,128)} %get-tuple-element.126), channel_id=1, source_target_pairs={{0,3},{1,2},{2,1},{3,0},{4,7},{5,6},{6,5},{7,4},{8,11},{9,10},{10,... | collective-permute-start | bytes 1769480 | tf_op jit(solution)/shard_map/ppermute | solution.py:654
  199.2 28.0 %collective-permute-start.30 = (f32[6,192,128]{2,1,0:T(8,128)}, f32[6,192,128]{2,1,0:T(8,128)}, u32[]{:S(2)}, u32[]{:S(2)}) collective-permute-start(f32[6,192,128]{2,1,0:T(8,128)} %get-tuple-element.139), channel_id=1, source_target_pairs={{0,3},{1,2},{2,1},{3,0},{4,7},{5,6},{6,5},{7,4},{8,11},{9,10},{10,... | collective-permute-start | bytes 1769480 | tf_op jit(solution)/shard_map/ppermute | solution.py:654
  222.2 12.5 %collective-permute-start.31 = (f32[6,192,128]{2,1,0:T(8,128)}, f32[6,192,128]{2,1,0:T(8,128)}, u32[]{:S(2)}, u32[]{:S(2)}) collective-permute-start(f32[6,192,128]{2,1,0:T(8,128)} %get-tuple-element.145), channel_id=1, source_target_pairs={{0,3},{1,2},{2,1},{3,0},{4,7},{5,6},{6,5},{7,4},{8,11},{9,10},{10,... | collective-permute-start | bytes 1769480 | tf_op jit(solution)/shard_map/ppermute | solution.py:654
  236.8 60.0 %copy-start.39 = (f32[3,6,48,128]{3,2,1,0:T(8,128)S(1)}, f32[3,6,48,128]{3,2,1,0:T(8,128)}, u32[]{:S(2)}) copy-start(f32[3,6,48,128]{3,2,1,0:T(8,128)} %copy-done.38) | copy-start | bytes 1327108
  236.8 61.4 %copy-start.17 = (f32[3,192,256]{2,1,0:T(8,128)S(1)}, f32[3,192,256]{2,1,0:T(8,128)}, u32[]{:S(2)}) copy-start(f32[3,192,256]{2,1,0:T(8,128)} %copy-done.16) | copy-start | bytes 1769476
  236.8 61.4 %copy-start.20 = (f32[6,192,128]{2,1,0:T(8,128)S(1)}, f32[6,192,128]{2,1,0:T(8,128)}, u32[]{:S(2)}) copy-start(f32[6,192,128]{2,1,0:T(8,128)} %copy-done.18) | copy-start | bytes 1769476
  236.8 61.4 %copy-start.23 = (f32[6,192,128]{2,1,0:T(8,128)S(1)}, f32[6,192,128]{2,1,0:T(8,128)}, u32[]{:S(2)}) copy-start(f32[6,192,128]{2,1,0:T(8,128)} %copy-done.21) | copy-start | bytes 1769476
  236.8 61.4 %copy-start.26 = (f32[192,128]{1,0:T(8,128)S(1)}, f32[192,128]{1,0:T(8,128)}, u32[]{:S(2)}) copy-start(f32[192,128]{1,0:T(8,128)} %get-tuple-element.175.refs_3_) | copy-start | bytes 294916
  236.8 61.4 %copy-start.30 = (bf16[384,192]{1,0:T(8,128)(2,1)S(1)}, bf16[384,192]{1,0:T(8,128)(2,1)}, u32[]{:S(2)}) copy-start(bf16[384,192]{1,0:T(8,128)(2,1)} %constant.132.clone.refs_5_) | copy-start | bytes 442372
  236.8 61.4 %copy-start.32 = (bf16[384,192]{1,0:T(8,128)(2,1)S(1)}, bf16[384,192]{1,0:T(8,128)(2,1)}, u32[]{:S(2)}) copy-start(bf16[384,192]{1,0:T(8,128)(2,1)} %constant.131.clone.refs_4_) | copy-start | bytes 442372
  240.8 57.4 %collective-permute-start.32 = (f32[5,192,128]{2,1,0:T(8,128)S(1)}, f32[5,192,128]{2,1,0:T(8,128)S(1)}, u32[]{:S(2)}, u32[]{:S(2)}) collective-permute-start(f32[5,192,128]{2,1,0:T(8,128)S(1)} %get-tuple-element.150), channel_id=1, source_target_pairs={{0,4},{4,8},{8,12},{12,16},{16,20},{20,24},{24,28},{28,0},{1,5},{5... | collective-permute-start | bytes 1474568 | tf_op jit(solution)/shard_map/ppermute | solution.py:715
  249.4 48.9 %collective-permute-start.33 = (f32[5,192,128]{2,1,0:T(8,128)S(1)}, f32[5,192,128]{2,1,0:T(8,128)S(1)}, u32[]{:S(2)}, u32[]{:S(2)}) collective-permute-start(f32[5,192,128]{2,1,0:T(8,128)S(1)} %get-tuple-element.151), channel_id=1, source_target_pairs={{0,28},{4,0},{8,4},{12,8},{16,12},{20,16},{24,20},{28,24},{1,29},{... | collective-permute-start | bytes 1474568 | tf_op jit(solution)/shard_map/ppermute | solution.py:716
  258.2 60.1 %collective-permute-start.34 = (f32[3,6,48,128]{3,2,1,0:T(8,128)S(1)}, f32[3,6,48,128]{3,2,1,0:T(8,128)S(1)}, u32[]{:S(2)}, u32[]{:S(2)}) collective-permute-start(f32[3,6,48,128]{3,2,1,0:T(8,128)S(1)} %copy-done.43), channel_id=1, source_target_pairs={{0,1},{1,2},{2,3},{3,0},{4,5},{5,6},{6,7},{7,4},{8,9},{9,10},{10,1... | collective-permute-start | bytes 1327112 | tf_op jit(solution)/shard_map/ppermute | solution.py:733
  258.2 77.4 %collective-permute-start.35 = (f32[3,6,48,128]{3,2,1,0:T(8,128)S(1)}, f32[3,6,48,128]{3,2,1,0:T(8,128)S(1)}, u32[]{:S(2)}, u32[]{:S(2)}) collective-permute-start(f32[3,6,48,128]{3,2,1,0:T(8,128)S(1)} %copy-done.41), channel_id=1, source_target_pairs={{0,2},{1,3},{2,0},{3,1},{4,6},{5,7},{6,4},{7,5},{8,10},{9,11},{10,... | collective-permute-start | bytes 1327112 | tf_op jit(solution)/shard_map/ppermute | solution.py:733
  296.8 38.8 %collective-permute-start.36 = (f32[3,6,48,128]{3,2,1,0:T(8,128)S(1)}, f32[3,6,48,128]{3,2,1,0:T(8,128)S(1)}, u32[]{:S(2)}, u32[]{:S(2)}) collective-permute-start(f32[3,6,48,128]{3,2,1,0:T(8,128)S(1)} %copy-done.39), channel_id=1, source_target_pairs={{0,3},{1,0},{2,1},{3,2},{4,7},{5,4},{6,5},{7,6},{8,11},{9,8},{10,9... | collective-permute-start | bytes 1327112 | tf_op jit(solution)/shard_map/ppermute | solution.py:733
  307.8 34.4 %collective-permute-start.37 = (f32[3,6,48,128]{3,2,1,0:T(8,128)S(1)}, f32[3,6,48,128]{3,2,1,0:T(8,128)S(1)}, u32[]{:S(2)}, u32[]{:S(2)}) collective-permute-start(f32[3,6,48,128]{3,2,1,0:T(8,128)S(1)} %get-tuple-element.164), channel_id=1, source_target_pairs={{0,1},{1,2},{2,3},{3,0},{4,5},{5,6},{6,7},{7,4},{8,9},{9,10},{10,1... | collective-permute-start | bytes 1327112 | tf_op jit(solution)/shard_map/ppermute | solution.py:733
  309.8 63.0 %collective-permute-start.38 = (f32[3,6,48,128]{3,2,1,0:T(8,128)S(1)}, f32[3,6,48,128]{3,2,1,0:T(8,128)S(1)}, u32[]{:S(2)}, u32[]{:S(2)}) collective-permute-start(f32[3,6,48,128]{3,2,1,0:T(8,128)S(1)} %get-tuple-element.165), channel_id=1, source_target_pairs={{0,2},{1,3},{2,0},{3,1},{4,6},{5,7},{6,4},{7,5},{8,10},{9,11},{10,... | collective-permute-start | bytes 1327112 | tf_op jit(solution)/shard_map/ppermute | solution.py:733
  318.4 54.4 %collective-permute-start.39 = (f32[3,6,48,128]{3,2,1,0:T(8,128)S(1)}, f32[3,6,48,128]{3,2,1,0:T(8,128)S(1)}, u32[]{:S(2)}, u32[]{:S(2)}) collective-permute-start(f32[3,6,48,128]{3,2,1,0:T(8,128)S(1)} %get-tuple-element.166), channel_id=1, source_target_pairs={{0,3},{1,0},{2,1},{3,2},{4,7},{5,4},{6,5},{7,6},{8,11},{9,8},{10,9... | collective-permute-start | bytes 1327112 | tf_op jit(solution)/shard_map/ppermute | solution.py:733
  325.0 47.8 %copy-start.10 = (bf16[1024,512]{1,0:T(8,128)(2,1)S(1)}, bf16[1024,512]{1,0:T(8,128)(2,1)}, u32[]{:S(2)}) copy-start(bf16[1024,512]{1,0:T(8,128)(2,1)} %constant.143.clone.refs_8_.refs_10_.refs_3_) | copy-start | bytes 3145732
  (91 other events, 782.6 us)

commit v2 on v1

--- a/solution.py
+++ b/solution.py
@@ -620,15 +620,15 @@
     else:
         slot_perms = [ring("yz", s) for s in range(G)]
 
-    def direct(j):
-        return not paired or j == 0
-
-    def widths_of(j):
-        return [wide] * G if direct(j) else [2 * wide] * 2
-
-    def scatter(pieces, j):
-        perms = slot_perms if direct(j) else [None, swap]
-        order = [2, 3, 1] if paired and direct(j) else range(1, len(pieces))
+    def direct(i, j):
+        return not paired or (i, j) in ((0, 0), (2, 0), (2, 1))
+
+    def widths_of(i, j):
+        return [wide] * G if direct(i, j) else [2 * wide] * 2
+
+    def scatter(pieces, i, j):
+        perms = slot_perms if direct(i, j) else [None, swap]
+        order = [2, 3, 1] if paired and direct(i, j) else range(1, len(pieces))
         out = [pieces[0]] + [None] * (len(pieces) - 1)
         for s in order:
             out[s] = lax.ppermute(pieces[s], "yz", perms[s])
@@ -642,9 +642,9 @@
     def mark(*arrays):
         token[:] = arrays
 
-    def gather_z(sent, j):
+    def gather_z(sent, i, j):
         ins = [list(source) for source in zip(*sent)]
-        whole_z = direct(j)
+        whole_z = direct(i, j)
         mats = m_direct if whole_z else m_pair
         first_id = G if whole_z else 2 * G
         got = z_call((chained(mats[0]), mats[1]), ids, first_id, ins, 1 if whole_z else 2, half)
@@ -669,7 +669,7 @@
         mark(*ghost[n])
 
     def spectra(i, *jobs, us=8):
-        widths = widths_of(jobs[0][0])
+        widths = widths_of(i, jobs[0][0])
         flat = spectra_call(
             i, [want for _, want in jobs], vel, ghost, ids, chained(background), omega,
             [f_pairs[j] + (kys[j],) for j, _ in jobs], widths, half, us,
@@ -677,10 +677,10 @@
         mark(flat[-1])
         n = len(widths)
         for at, (j, _) in enumerate(jobs):
-            sends.setdefault((i, j), []).append(scatter(flat[at * n : (at + 1) * n], j))
+            sends.setdefault((i, j), []).append(scatter(flat[at * n : (at + 1) * n], i, j))
 
     def forward_z(i, j):
-        parts[i, j] = gather_z(sends[i, j], j)
+        parts[i, j] = gather_z(sends[i, j], i, j)
 
     p_halo = []
 
@@ -751,21 +751,22 @@
         spectra(1, (0, "w"))
         spectra(2, (0, "w"))
         spectra(0, (1, "ucw"))
+        forward_z(1, 0)
         spectra(1, (1, "ucw"))
         forward_z(0, 0)
         spectra(2, (1, "ucw"))
         guess_halo()
-        forward_z(1, 0)
         forward_z(0, 1)
         forward_z(2, 0)
         prep(0)
         forward_z(1, 1)
         solve(0)
         forward_z(2, 1)
+        q, p, groups = solved[0]
+        arrived = parts[0, 1][1:] + parts[1, 1][1:]
+        solved[0] = (q, p, [[after(chained(h), *arrived) for h in hs] for hs in groups])
+        got = give_back(0)
         prep(1)
-        q, p, groups = solved[0]
-        solved[0] = (q, p, [[chained(h) for h in hs] for hs in groups])
-        got = give_back(0)
         solve(1)
         got1 = give_back(1)
         base = chained(vel)

time: 379 us -> 377 us (level)
  the two profiles are of different devices: /device:TPU:27 before, /device:TPU:26 now
where the time goes in v2:
time: 377 us; the launch traced here: 376 us
  Pallas kernels  125 us (33%)
  waiting for transfers between devices  125 us (33%)
  starting transfers between devices  87.3 us (23%)
  local copies, waits for them, and re-layouts  33.1 us (9%)
  other arithmetic  3.8 us (1%)
    ppermute x19, waiting for transfers between devices, scatter(): out[s] = lax.ppermute(pieces[s], 'yz', perms[s])  70.3 us
    pallas_call x9, Pallas kernels, spectra_call(): pl.pallas_call(lambda *refs: spectra_body(comp, omega, half, jobs, comps,...  60.9 us
    ppermute x19, starting transfers between devices, scatter(): out[s] = lax.ppermute(pieces[s], 'yz', perms[s])  53.2 us
    ppermute x6, waiting for transfers between devices, give_back(): got.append(lax.ppermute(hs[s], 'yz', ring('yz', s)))  47 us
    unnamed x178, local copies, waits for them, and re-layouts  28.7 us
    ppermute x6, starting transfers between devices, give_back(): got.append(lax.ppermute(hs[s], 'yz', ring('yz', s)))  23 us
    pallas_call x2, Pallas kernels, solve_call(): pl.pallas_call(lambda *refs: solve_body(chunk, half, n_slot, n, nb, *refs...  19 us
    pallas_call x6, Pallas kernels, z_call(): pl.pallas_call(lambda *refs: z_body(counts, first_id, n_t, half, *refs),...  18.5 us
  transfers between devices with their start and end apart: 38, of which 13 were waited for; matrix products, arithmetic and copies ran while one was open for 2% of the time, Pallas kernels for 29%

profile of v2, /device:TPU:26, one launch (start us, length us, event | category | flops | bytes accessed | tf_op | source)
XLA Modules:
  0.0 376.5 jit_solution(15742886287513560611)
XLA Ops:
  3.9 5.2 %spectra.9 = (f32[2,6,48,128]{3,2,1,0:T(8,128)S(1)}, f32[2,6,48,128]{3,2,1,0:T(8,128)S(1)}, f32[2,6,48,128]{3,2,1,0:T(8,128)}, f32[2,6,48,128]{3,2,1,0:T(8,128)}) custom-call(s32[18]{0:T(128)S(1)} %concatenate.120.refs_0_, f32[6]{0:T(128)S(1)} %add_multiply_fusion.refs_1_, f32[3,6,48,1024]{3,2,1,0:T(8,128)} %refs_1_, f32[3,6,48,1024]{3,2,1,0:T(8,128)} %refs_1_, ...), custom_call_target="tpu_custom_call" | custom-call | flops 1500000000 | tf_op jit(solution)/shard_map/spectra/pallas_call | solution.py:198
  18.9 4.3 %spectra.10 = (f32[2,6,48,256]{3,2,1,0:T(8,128)S(1)}, f32[2,6,48,256]{3,2,1,0:T(8,128)S(1)}) custom-call(s32[18]{0:T(128)S(1)} %concatenate.120.refs_0_, f32[6]{0:T(128)S(1)} %add_multiply_fusion.refs_1_, f32[3,6,48,1024]{3,2,1,0:T(8,128)} %refs_1_, f32[3,6,48,1024]{3,2,1,0:T(8,128)} %refs_1_, bf16[1024,512]{1,0:T(8,128)(2,1)S(1)} %copy-done.6, ...), custom_call_target="tpu_custom_call" | custom-call | flops 1500000000 | tf_op jit(solution)/shard_map/spectra/pallas_call | solution.py:198
  26.0 2.5 collective-permute-start.6
  28.5 2.2 shear.2
  30.7 7.0 %spectra.11 = (f32[1,6,48,128]{3,2,1,0:T(8,128)S(1)}, f32[1,6,48,128]{3,2,1,0:T(8,128)}, f32[1,6,48,128]{3,2,1,0:T(8,128)}, f32[1,6,48,128]{3,2,1,0:T(8,128)S(1)}) custom-call(s32[18]{0:T(128)S(1)} %concatenate.120.refs_0_, f32[6]{0:T(128)S(1)} %add_multiply_fusion.refs_1_, f32[3,6,48,1024]{3,2,1,0:T(8,128)} %refs_1_, f32[3,6,48,1024]{3,2,1,0:T(8,128)} %refs_1_, ...), custom_call_target="tpu_custom_call" | custom-call | flops 2000000000 | tf_op jit(solution)/shard_map/spectra/pallas_call | solution.py:198
  37.7 3.9 %spectra.12 = (f32[2,6,48,128]{3,2,1,0:T(8,128)S(1)}, f32[2,6,48,128]{3,2,1,0:T(8,128)S(1)}, f32[2,6,48,128]{3,2,1,0:T(8,128)S(1)}, f32[2,6,48,128]{3,2,1,0:T(8,128)S(1)}) custom-call(s32[18]{0:T(128)S(1)} %concatenate.120.refs_0_, f32[6]{0:T(128)S(1)} %add_multiply_fusion.refs_1_, f32[3,6,48,1024]{3,2,1,0:T(8,128)} %refs_1_, ...), custom_call_target="tpu_custom_call" | custom-call | flops 1500000000 | tf_op jit(solution)/shard_map/spectra/pallas_call | solution.py:198
  44.6 3.8 %collective-permute-done.3.down = f32[2,3,48,1024]{3,2,1,0:T(8,128)} collective-permute-done((f32[2,3,48,1024]{3,2,1,0:T(8,128)}, f32[2,3,48,1024]{3,2,1,0:T(8,128)}, u32[]{:S(2)}, u32[]{:S(2)}) %collective-permute-start.3) | collective-permute-done | bytes 1179680 | tf_op jit(solution)/shard_map/ppermute | solution.py:664
  48.4 2.9 collective-permute-done.2.up
  51.2 3.6 shear.3
  56.9 6.6 %spectra.13 = (f32[1,6,48,256]{3,2,1,0:T(8,128)S(1)}, f32[1,6,48,256]{3,2,1,0:T(8,128)S(1)}) custom-call(s32[18]{0:T(128)S(1)} %concatenate.120.refs_0_, f32[6]{0:T(128)S(1)} %add_multiply_fusion.refs_1_, f32[3,6,48,1024]{3,2,1,0:T(8,128)} %refs_1_, f32[3,6,48,1024]{3,2,1,0:T(8,128)} %refs_1_, f32[1,3,48,1024]{3,2,1,0:T(8,128)S(1)} %get-tuple-element.93.refs_4_.refs_5_, ...), custom_call_target="tpu_custom_call" | custom-call | flops 2000000000 | tf_op jit(solution)/shard_map/spectra/pallas_call | solution.py:198
  64.7 6.9 %spectra.14 = (f32[1,6,48,128]{3,2,1,0:T(8,128)S(1)}, f32[1,6,48,128]{3,2,1,0:T(8,128)S(1)}, f32[1,6,48,128]{3,2,1,0:T(8,128)S(1)}, f32[1,6,48,128]{3,2,1,0:T(8,128)S(1)}) custom-call(s32[18]{0:T(128)S(1)} %concatenate.120.refs_0_, f32[6]{0:T(128)S(1)} %add_multiply_fusion.refs_1_, f32[3,6,48,1024]{3,2,1,0:T(8,128)} %refs_1_, f32[3,6,48,1024]{3,2,1,0:T(8,128)} %refs_1_, ...), custom_call_target="tpu_custom_call" | custom-call | flops 2000000000 | tf_op jit(solution)/shard_map/spectra/pallas_call | solution.py:198
  72.9 9.2 %spectra.15 = (f32[3,6,48,256]{3,2,1,0:T(8,128)S(1)}, f32[3,6,48,256]{3,2,1,0:T(8,128)}) custom-call(s32[18]{0:T(128)S(1)} %concatenate.120.refs_0_, f32[6]{0:T(128)S(1)} %add_multiply_fusion.refs_1_, f32[3,6,48,1024]{3,2,1,0:T(8,128)} %refs_1_, f32[3,6,48,1024]{3,2,1,0:T(8,128)} %refs_1_, f32[3,6,48,1024]{3,2,1,0:T(8,128)} %refs_1_, ...), custom_call_target="tpu_custom_call" | custom-call | flops 2000000000 | tf_op jit(solution)/shard_map/spectra/pallas_call | solution.py:198
  87.4 3.6 collective-permute-start.7
  94.8 2.8 zforward.6
  97.7 14.6 %collective-permute-done.8.refs_7_ = f32[2,6,48,128]{3,2,1,0:T(8,128)} collective-permute-done((f32[2,6,48,128]{3,2,1,0:T(8,128)}, f32[2,6,48,128]{3,2,1,0:T(8,128)}, u32[]{:S(2)}, u32[]{:S(2)}) %collective-permute-start.8) | collective-permute-done | bytes 294944 | tf_op jit(solution)/shard_map/ppermute | solution.py:634
  112.3 7.3 %collective-permute-start.11 = (f32[1,6,48,128]{3,2,1,0:T(8,128)S(1)}, f32[1,6,48,128]{3,2,1,0:T(8,128)S(1)}, u32[]{:S(2)}, u32[]{:S(2)}) collective-permute-start(f32[1,6,48,128]{3,2,1,0:T(8,128)S(1)} %copy-done.75), channel_id=1, source_target_pairs={{0,2},{1,3},{2,0},{3,1},{4,6},{5,7},{6,4},{7,5},{8,10},{9,11},{10,... | collective-permute-start | bytes 442376 | tf_op jit(solution)/shard_map/ppermute | solution.py:634
  119.6 5.3 %collective-permute-start.13 = (f32[2,6,48,128]{3,2,1,0:T(8,128)S(1)}, f32[2,6,48,128]{3,2,1,0:T(8,128)S(1)}, u32[]{:S(2)}, u32[]{:S(2)}) collective-permute-start(f32[2,6,48,128]{3,2,1,0:T(8,128)S(1)} %copy-done.57), channel_id=1, source_target_pairs={{0,3},{1,2},{2,1},{3,0},{4,7},{5,6},{6,5},{7,4},{8,11},{9,10},{10,... | collective-permute-start | bytes 884744 | tf_op jit(solution)/shard_map/ppermute | solution.py:634
  125.0 8.9 %spectra.16 = (f32[3,6,48,256]{3,2,1,0:T(8,128)S(1)}, f32[3,6,48,256]{3,2,1,0:T(8,128)S(1)}) custom-call(s32[18]{0:T(128)S(1)} %concatenate.120.refs_0_, f32[6]{0:T(128)S(1)} %add_multiply_fusion.refs_1_, f32[3,6,48,1024]{3,2,1,0:T(8,128)} %refs_1_, f32[3,6,48,1024]{3,2,1,0:T(8,128)} %refs_1_, f32[3,6,48,1024]{3,2,1,0:T(8,128)} %refs_1_, ...), custom_call_target="tpu_custom_call" | custom-call | flops 2000000000 | tf_op jit(solution)/shard_map/spectra/pallas_call | solution.py:198
  133.9 5.6 %collective-permute-done.11.refs_10_ = f32[1,6,48,128]{3,2,1,0:T(8,128)S(1)} collective-permute-done((f32[1,6,48,128]{3,2,1,0:T(8,128)S(1)}, f32[1,6,48,128]{3,2,1,0:T(8,128)S(1)}, u32[]{:S(2)}, u32[]{:S(2)}) %collective-permute-start.11) | collective-permute-done | bytes 147488 | tf_op jit(solution)/shard_map/ppermute | solution.py:634
  141.0 3.0 zforward.7.refs_2_.refs_12_
  144.0 8.8 %spectra.17 = (f32[3,6,48,128]{3,2,1,0:T(8,128)S(1)}, f32[3,6,48,128]{3,2,1,0:T(8,128)S(1)}, f32[3,6,48,128]{3,2,1,0:T(8,128)S(1)}, f32[3,6,48,128]{3,2,1,0:T(8,128)S(1)}) custom-call(s32[18]{0:T(128)S(1)} %concatenate.120.refs_0_, f32[6]{0:T(128)S(1)} %add_multiply_fusion.refs_1_, f32[3,6,48,1024]{3,2,1,0:T(8,128)} %refs_1_, f32[3,6,48,1024]{3,2,1,0:T(8,128)} %refs_1_, ...), custom_call_target="tpu_custom_call" | custom-call | flops 2000000000 | tf_op jit(solution)/shard_map/spectra/pallas_call | solution.py:198
  152.9 15.1 %collective-permute-start.18 = (f32[1,6,48,128]{3,2,1,0:T(8,128)S(1)}, f32[1,6,48,128]{3,2,1,0:T(8,128)S(1)}, u32[]{:S(2)}, u32[]{:S(2)}) collective-permute-start(f32[1,6,48,128]{3,2,1,0:T(8,128)S(1)} %copy-done.67), channel_id=1, source_target_pairs={{0,2},{1,3},{2,0},{3,1},{4,6},{5,7},{6,4},{7,5},{8,10},{9,11},{10,... | collective-permute-start | bytes 442376 | tf_op jit(solution)/shard_map/ppermute | solution.py:634
  168.0 2.5 collective-permute-start.14
  170.7 2.1 collective-permute-start.20
  173.7 4.4 %zforward.8 = (f32[6,192,128]{2,1,0:T(8,128)S(1)}, f32[6,192,128]{2,1,0:T(8,128)}) custom-call(s32[18]{0:T(128)S(1)} %concatenate.120.refs_0_, bf16[384,288]{1,0:T(8,128)(2,1)S(1)} %copy-done.31, bf16[384,288]{1,0:T(8,128)(2,1)S(1)} %copy-done.33, f32[3,6,48,256]{3,2,1,0:T(8,128)S(1)} %copy-done.38, f32[3,6,48,256]{3,2,1,0:T(8,128)} %collective-permute-done.12.refs_4_), custom_call_target="tpu_custom_call" | custom-call | flops 1000000000 | tf_op jit(solution)/shard_map/zforward/pallas_call | solution.py:246
  180.2 4.8 %collective-permute-done.18.refs_10_ = f32[1,6,48,128]{3,2,1,0:T(8,128)S(1)} collective-permute-done((f32[1,6,48,128]{3,2,1,0:T(8,128)S(1)}, f32[1,6,48,128]{3,2,1,0:T(8,128)S(1)}, u32[]{:S(2)}, u32[]{:S(2)}) %collective-permute-start.18) | collective-permute-done | bytes 147488 | tf_op jit(solution)/shard_map/ppermute | solution.py:634
  185.0 2.3 zforward.9.refs_5_.refs_15_
  187.5 3.0 prep.2
  194.2 3.7 zforward.10
  198.7 2.2 collective-permute-start.29
  205.4 8.0 %collective-permute-start.26 = (f32[3,6,48,128]{3,2,1,0:T(8,128)}, f32[3,6,48,128]{3,2,1,0:T(8,128)S(1)}, u32[]{:S(2)}, u32[]{:S(2)}) collective-permute-start(f32[3,6,48,128]{3,2,1,0:T(8,128)} %copy-done.44), channel_id=1, source_target_pairs={{0,1},{1,0},{2,3},{3,2},{4,5},{5,4},{6,7},{7,6},{8,9},{9,8},{10,11... | collective-permute-start | bytes 1327112 | tf_op jit(solution)/shard_map/ppermute | solution.py:634
  213.6 2.0 copy-done.12
  221.7 9.6 %solve.2 = (f32[3,6,192,128]{3,2,1,0:T(8,128)S(1)}, f32[6,192,128]{2,1,0:T(8,128)S(1)}, f32[3,6,48,128]{3,2,1,0:T(8,128)S(1)}, f32[3,6,48,128]{3,2,1,0:T(8,128)S...) custom-call(s32[18]{0:T(128)S(1)} %concatenate.120.refs_0_, ...), custom_call_target="tpu_custom_call" | custom-call | flops 2500000000 | tf_op jit(solution)/shard_map/solve/pallas_call | solution.py:457
  231.3 11.2 %collective-permute-done.25.refs_4_ = f32[3,6,48,128]{3,2,1,0:T(8,128)S(1)} collective-permute-done((f32[3,6,48,128]{3,2,1,0:T(8,128)}, f32[3,6,48,128]{3,2,1,0:T(8,128)S(1)}, u32[]{:S(2)}, u32[]{:S(2)}) %collective-permute-start.25) | collective-permute-done | bytes 442400 | tf_op jit(solution)/shard_map/ppermute | solution.py:634
  242.5 4.8 %collective-permute-done.26.refs_5_ = f32[3,6,48,128]{3,2,1,0:T(8,128)S(1)} collective-permute-done((f32[3,6,48,128]{3,2,1,0:T(8,128)}, f32[3,6,48,128]{3,2,1,0:T(8,128)S(1)}, u32[]{:S(2)}, u32[]{:S(2)}) %collective-permute-start.26) | collective-permute-done | bytes 442400 | tf_op jit(solution)/shard_map/ppermute | solution.py:634
  247.2 27.9 %collective-permute-done.27.refs_6_ = f32[3,6,48,128]{3,2,1,0:T(8,128)S(1)} collective-permute-done((f32[3,6,48,128]{3,2,1,0:T(8,128)}, f32[3,6,48,128]{3,2,1,0:T(8,128)S(1)}, u32[]{:S(2)}, u32[]{:S(2)}) %collective-permute-start.27) | collective-permute-done | bytes 442400 | tf_op jit(solution)/shard_map/ppermute | solution.py:634
  275.2 2.3 zforward.11.refs_6_.refs_16_
  277.6 3.8 %prep.3 = (f32[5,192,128]{2,1,0:T(8,128)S(1)}, f32[5,192,128]{2,1,0:T(8,128)S(1)}) custom-call(f32[8,128]{1,0:T(8,128)S(1)} %concatenate.127.refs_0_.refs_1_, f32[192,128]{1,0:T(8,128)S(1)} %broadcast_in_dim.45.refs_1_.refs_2_, f32[6,192,128]{2,1,0:T(8,128)S(1)} %copy-done.21, f32[6,192,128]{2,1,0:T(8,128)} %collective-permute-done.28.refs_3_.refs_13_, ...), custom_call_target="tpu_custom_call" | custom-call | flops 1000000000 | tf_op jit(solution)/shard_map/prep/pallas_call | solution.py:347
  284.7 9.9 %collective-permute-start.33 = (f32[3,6,48,128]{3,2,1,0:T(8,128)S(1)}, f32[3,6,48,128]{3,2,1,0:T(8,128)S(1)}, u32[]{:S(2)}, u32[]{:S(2)}) collective-permute-start(f32[3,6,48,128]{3,2,1,0:T(8,128)S(1)} %get-tuple-element.163), channel_id=1, source_target_pairs={{0,2},{1,3},{2,0},{3,1},{4,6},{5,7},{6,4},{7,5},{8,10},{9,11},{10,... | collective-permute-start | bytes 1327112 | tf_op jit(solution)/shard_map/ppermute | solution.py:733
  295.3 9.4 %solve.3 = (f32[3,6,192,128]{3,2,1,0:T(8,128)S(1)}, f32[6,192,128]{2,1,0:T(8,128)S(1)}, f32[3,6,48,128]{3,2,1,0:T(8,128)S(1)}, f32[3,6,48,128]{3,2,1,0:T(8,128)S...) custom-call(s32[18]{0:T(128)S(1)} %concatenate.120.refs_0_, ...), custom_call_target="tpu_custom_call" | custom-call | flops 2500000000 | tf_op jit(solution)/shard_map/solve/pallas_call | solution.py:457
  304.7 3.2 collective-permute-start.35
  307.9 7.2 %collective-permute-start.36 = (f32[3,6,48,128]{3,2,1,0:T(8,128)S(1)}, f32[3,6,48,128]{3,2,1,0:T(8,128)S(1)}, u32[]{:S(2)}, u32[]{:S(2)}) collective-permute-start(f32[3,6,48,128]{3,2,1,0:T(8,128)S(1)} %get-tuple-element.169), channel_id=1, source_target_pairs={{0,2},{1,3},{2,0},{3,1},{4,6},{5,7},{6,4},{7,5},{8,10},{9,11},{10,... | collective-permute-start | bytes 1327112 | tf_op jit(solution)/shard_map/ppermute | solution.py:733
  316.9 3.3 pack.2
  320.2 14.0 %collective-permute-done.33.refs_6_ = f32[3,6,48,128]{3,2,1,0:T(8,128)S(1)} collective-permute-done((f32[3,6,48,128]{3,2,1,0:T(8,128)S(1)}, f32[3,6,48,128]{3,2,1,0:T(8,128)S(1)}, u32[]{:S(2)}, u32[]{:S(2)}) %collective-permute-start.33) | collective-permute-done | bytes 442400 | tf_op jit(solution)/shard_map/ppermute | solution.py:733
  334.3 4.1 %back.2.refs_1_ = f32[3,6,48,1024]{3,2,1,0:T(8,128)S(1)} custom-call(s32[18]{0:T(128)S(1)} %concatenate.120.refs_0_, f32[3,6,48,1024]{3,2,1,0:T(8,128)S(1)} %copy-done.1, bf16[1024,512]{1,0:T(8,128)(2,1)S(1)} %copy-done.7, bf16[1024,512]{1,0:T(8,128)(2,1)S(1)} %copy-done.4, f32[3,6,48,128]{3,2,1,0:T(8,128)S(1)} %get-tuple-element.157.refs_4_, ...), custom_call_target="tpu_custom_call" | custom-call | flops 1750000000 | tf_op jit(solution)/shard_map/back/pallas_call | solution.py:503
  338.4 3.8 %collective-permute-done.35.refs_5_ = f32[3,6,48,128]{3,2,1,0:T(8,128)S(1)} collective-permute-done((f32[3,6,48,128]{3,2,1,0:T(8,128)S(1)}, f32[3,6,48,128]{3,2,1,0:T(8,128)S(1)}, u32[]{:S(2)}, u32[]{:S(2)}) %collective-permute-start.35) | collective-permute-done | bytes 442400 | tf_op jit(solution)/shard_map/ppermute | solution.py:733
  342.2 29.1 %collective-permute-done.36.refs_6_ = f32[3,6,48,128]{3,2,1,0:T(8,128)S(1)} collective-permute-done((f32[3,6,48,128]{3,2,1,0:T(8,128)S(1)}, f32[3,6,48,128]{3,2,1,0:T(8,128)S(1)}, u32[]{:S(2)}, u32[]{:S(2)}) %collective-permute-start.36) | collective-permute-done | bytes 442400 | tf_op jit(solution)/shard_map/ppermute | solution.py:733
  371.3 5.1 %back.3 = f32[3,6,48,1024]{3,2,1,0:T(8,128)} custom-call(s32[18]{0:T(128)S(1)} %concatenate.120.refs_0_, f32[3,6,48,1024]{3,2,1,0:T(8,128)S(1)} %back.2.refs_1_, bf16[1024,512]{1,0:T(8,128)(2,1)S(1)} %copy-done.11, bf16[1024,512]{1,0:T(8,128)(2,1)S(1)} %copy-done.10, f32[3,6,48,128]{3,2,1,0:T(8,128)S(1)} %get-tuple-element.167.refs_4_, ...), custom_call_target="tpu_custom_call" | custom-call | flops 1750000000 | tf_op jit(solution)/shard_map/back/pallas_call | solution.py:503
  (262 shorter events, 57.4 us)
Async XLA Ops:
  9.2 110.4 %collective-permute-start.10 = (f32[2,6,48,128]{3,2,1,0:T(8,128)}, f32[2,6,48,128]{3,2,1,0:T(8,128)}, u32[]{:S(2)}, u32[]{:S(2)}) collective-permute-start(f32[2,6,48,128]{3,2,1,0:T(8,128)} %get-tuple-element.88), channel_id=1, source_target_pairs={{0,2},{1,3},{2,0},{3,1},{4,6},{5,7},{6,4},{7,5},{8,10},{9,11},{10,... | collective-permute-start | bytes 884744 | tf_op jit(solution)/shard_map/ppermute | solution.py:634
  10.6 13.5 %collective-permute-start.1 = (f32[1,3,48,1024]{3,2,1,0:T(8,128)}, f32[1,3,48,1024]{3,2,1,0:T(8,128)}, u32[]{:S(2)}, u32[]{:S(2)}) collective-permute-start(f32[1,3,48,1024]{3,2,1,0:T(8,128)} %get-tuple-element.175), channel_id=1, source_target_pairs={{0,28},{4,0},{8,4},{12,8},{16,12},{20,16},{24,20},{28,24},{1,29},{... | collective-permute-start | bytes 1769480 | tf_op jit(solution)/shard_map/ppermute | solution.py:664
  10.6 15.3 %collective-permute-start = (f32[1,3,48,1024]{3,2,1,0:T(8,128)}, f32[1,3,48,1024]{3,2,1,0:T(8,128)}, u32[]{:S(2)}, u32[]{:S(2)}) collective-permute-start(f32[1,3,48,1024]{3,2,1,0:T(8,128)} %get-tuple-element.176), channel_id=1, source_target_pairs={{0,4},{4,8},{8,12},{12,16},{16,20},{20,24},{24,28},{28,0},{1,5},{5... | collective-permute-start | bytes 1769480 | tf_op jit(solution)/shard_map/ppermute | solution.py:663
  12.7 35.7 %collective-permute-start.3 = (f32[2,3,48,1024]{3,2,1,0:T(8,128)}, f32[2,3,48,1024]{3,2,1,0:T(8,128)}, u32[]{:S(2)}, u32[]{:S(2)}) collective-permute-start(f32[2,3,48,1024]{3,2,1,0:T(8,128)} %get-tuple-element.173), channel_id=1, source_target_pairs={{0,28},{4,0},{8,4},{12,8},{16,12},{20,16},{24,20},{28,24},{1,29},{... | collective-permute-start | bytes 3538952 | tf_op jit(solution)/shard_map/ppermute | solution.py:664
  14.0 37.2 %collective-permute-start.2 = (f32[2,3,48,1024]{3,2,1,0:T(8,128)}, f32[2,3,48,1024]{3,2,1,0:T(8,128)}, u32[]{:S(2)}, u32[]{:S(2)}) collective-permute-start(f32[2,3,48,1024]{3,2,1,0:T(8,128)} %get-tuple-element.174), channel_id=1, source_target_pairs={{0,4},{4,8},{8,12},{12,16},{16,20},{20,24},{24,28},{28,0},{1,5},{5... | collective-permute-start | bytes 3538952 | tf_op jit(solution)/shard_map/ppermute | solution.py:663
  24.0 67.8 %copy-start.30 = (bf16[384,288]{1,0:T(8,128)(2,1)}, bf16[384,288]{1,0:T(8,128)(2,1)S(1)}, u32[]{:S(2)}) copy-start(bf16[384,288]{1,0:T(8,128)(2,1)S(1)} %broadcast_select_fusion.1.refs_1_) | copy-start | bytes 663556
  24.1 67.7 %copy-start.32 = (bf16[384,288]{1,0:T(8,128)(2,1)}, bf16[384,288]{1,0:T(8,128)(2,1)S(1)}, u32[]{:S(2)}) copy-start(bf16[384,288]{1,0:T(8,128)(2,1)S(1)} %broadcast_select_fusion.refs_2_) | copy-start | bytes 663556
  24.1 62.4 %collective-permute-start.4 = (f32[2,6,48,256]{3,2,1,0:T(8,128)S(1)}, f32[2,6,48,256]{3,2,1,0:T(8,128)S(1)}, u32[]{:S(2)}, u32[]{:S(2)}) collective-permute-start(f32[2,6,48,256]{3,2,1,0:T(8,128)S(1)} %get-tuple-element.90), channel_id=1, source_target_pairs={{0,1},{1,0},{2,3},{3,2},{4,5},{5,4},{6,7},{7,6},{8,9},{9,8},{10,11... | collective-permute-start | bytes 1769480 | tf_op jit(solution)/shard_map/ppermute | solution.py:634
  26.0 59.3 %collective-permute-start.6 = (f32[2,6,48,128]{3,2,1,0:T(8,128)S(1)}, f32[2,6,48,128]{3,2,1,0:T(8,128)S(1)}, u32[]{:S(2)}, u32[]{:S(2)}) collective-permute-start(f32[2,6,48,128]{3,2,1,0:T(8,128)S(1)} %copy-done.55), channel_id=1, source_target_pairs={{0,3},{1,2},{2,1},{3,0},{4,7},{5,6},{6,5},{7,4},{8,11},{9,10},{10,... | collective-permute-start | bytes 884744 | tf_op jit(solution)/shard_map/ppermute | solution.py:634
  64.3 26.7 %collective-permute-start.5 = (f32[1,6,48,256]{3,2,1,0:T(8,128)S(1)}, f32[1,6,48,256]{3,2,1,0:T(8,128)S(1)}, u32[]{:S(2)}, u32[]{:S(2)}) collective-permute-start(f32[1,6,48,256]{3,2,1,0:T(8,128)S(1)} %get-tuple-element.103), channel_id=1, source_target_pairs={{0,1},{1,0},{2,3},{3,2},{4,5},{5,4},{6,7},{7,6},{8,9},{9,8},{10,11... | collective-permute-start | bytes 884744 | tf_op jit(solution)/shard_map/ppermute | solution.py:634
  83.1 87.5 %collective-permute-start.12 = (f32[3,6,48,256]{3,2,1,0:T(8,128)}, f32[3,6,48,256]{3,2,1,0:T(8,128)}, u32[]{:S(2)}, u32[]{:S(2)}) collective-permute-start(f32[3,6,48,256]{3,2,1,0:T(8,128)} %get-tuple-element.107), channel_id=1, source_target_pairs={{0,1},{1,0},{2,3},{3,2},{4,5},{5,4},{6,7},{7,6},{8,9},{9,8},{10,11... | collective-permute-start | bytes 2654216 | tf_op jit(solution)/shard_map/ppermute | solution.py:634
  86.0 26.3 %collective-permute-start.8 = (f32[2,6,48,128]{3,2,1,0:T(8,128)}, f32[2,6,48,128]{3,2,1,0:T(8,128)}, u32[]{:S(2)}, u32[]{:S(2)}) collective-permute-start(f32[2,6,48,128]{3,2,1,0:T(8,128)} %get-tuple-element.119), channel_id=1, source_target_pairs={{0,1},{1,0},{2,3},{3,2},{4,5},{5,4},{6,7},{7,6},{8,9},{9,8},{10,11... | collective-permute-start | bytes 884744 | tf_op jit(solution)/shard_map/ppermute | solution.py:634
  87.4 32.3 %collective-permute-start.7 = (f32[1,6,48,128]{3,2,1,0:T(8,128)}, f32[1,6,48,128]{3,2,1,0:T(8,128)}, u32[]{:S(2)}, u32[]{:S(2)}) collective-permute-start(f32[1,6,48,128]{3,2,1,0:T(8,128)} %get-tuple-element.118), channel_id=1, source_target_pairs={{0,3},{1,2},{2,1},{3,0},{4,7},{5,6},{6,5},{7,4},{8,11},{9,10},{10,... | collective-permute-start | bytes 442376 | tf_op jit(solution)/shard_map/ppermute | solution.py:634
  91.7 33.2 %collective-permute-start.9 = (f32[1,6,48,128]{3,2,1,0:T(8,128)}, f32[1,6,48,128]{3,2,1,0:T(8,128)}, u32[]{:S(2)}, u32[]{:S(2)}) collective-permute-start(f32[1,6,48,128]{3,2,1,0:T(8,128)} %get-tuple-element.120), channel_id=1, source_target_pairs={{0,1},{1,0},{2,3},{3,2},{4,5},{5,4},{6,7},{7,6},{8,9},{9,8},{10,11... | collective-permute-start | bytes 442376 | tf_op jit(solution)/shard_map/ppermute | solution.py:634
  94.8 30.1 %copy-start.53 = (f32[2,6,48,128]{3,2,1,0:T(8,128)S(1)}, f32[2,6,48,128]{3,2,1,0:T(8,128)}, u32[]{:S(2)}) copy-start(f32[2,6,48,128]{3,2,1,0:T(8,128)} %copy-done.52) | copy-start | bytes 884740
  97.7 89.8 %copy-start.18 = (f32[6,192,128]{2,1,0:T(8,128)}, f32[6,192,128]{2,1,0:T(8,128)S(1)}, u32[]{:S(2)}) copy-start(f32[6,192,128]{2,1,0:T(8,128)S(1)} %get-tuple-element.134.refs_3_.refs_13_) | copy-start | bytes 1769476
  112.3 27.2 %collective-permute-start.11 = (f32[1,6,48,128]{3,2,1,0:T(8,128)S(1)}, f32[1,6,48,128]{3,2,1,0:T(8,128)S(1)}, u32[]{:S(2)}, u32[]{:S(2)}) collective-permute-start(f32[1,6,48,128]{3,2,1,0:T(8,128)S(1)} %copy-done.75), channel_id=1, source_target_pairs={{0,2},{1,3},{2,0},{3,1},{4,6},{5,7},{6,4},{7,5},{8,10},{9,11},{10,... | collective-permute-start | bytes 442376 | tf_op jit(solution)/shard_map/ppermute | solution.py:634
  119.6 51.0 %collective-permute-start.17 = (f32[2,6,48,128]{3,2,1,0:T(8,128)S(1)}, f32[2,6,48,128]{3,2,1,0:T(8,128)S(1)}, u32[]{:S(2)}, u32[]{:S(2)}) collective-permute-start(f32[2,6,48,128]{3,2,1,0:T(8,128)S(1)} %copy-done.51), channel_id=1, source_target_pairs={{0,2},{1,3},{2,0},{3,1},{4,6},{5,7},{6,4},{7,5},{8,10},{9,11},{10,... | collective-permute-start | bytes 884744 | tf_op jit(solution)/shard_map/ppermute | solution.py:634
  119.6 33.2 %collective-permute-start.13 = (f32[2,6,48,128]{3,2,1,0:T(8,128)S(1)}, f32[2,6,48,128]{3,2,1,0:T(8,128)S(1)}, u32[]{:S(2)}, u32[]{:S(2)}) collective-permute-start(f32[2,6,48,128]{3,2,1,0:T(8,128)S(1)} %copy-done.57), channel_id=1, source_target_pairs={{0,3},{1,2},{2,1},{3,0},{4,7},{5,6},{6,5},{7,4},{8,11},{9,10},{10,... | collective-permute-start | bytes 884744 | tf_op jit(solution)/shard_map/ppermute | solution.py:634
  125.0 43.1 %collective-permute-start.15 = (f32[2,6,48,128]{3,2,1,0:T(8,128)S(1)}, f32[2,6,48,128]{3,2,1,0:T(8,128)S(1)}, u32[]{:S(2)}, u32[]{:S(2)}) collective-permute-start(f32[2,6,48,128]{3,2,1,0:T(8,128)S(1)} %copy-done.53), channel_id=1, source_target_pairs={{0,1},{1,0},{2,3},{3,2},{4,5},{5,4},{6,7},{7,6},{8,9},{9,8},{10,11... | collective-permute-start | bytes 884744 | tf_op jit(solution)/shard_map/ppermute | solution.py:634
  139.5 47.9 %collective-permute-start.19 = (f32[6,192,128]{2,1,0:T(8,128)S(1)}, f32[6,192,128]{2,1,0:T(8,128)S(1)}, u32[]{:S(2)}, u32[]{:S(2)}) collective-permute-start(f32[6,192,128]{2,1,0:T(8,128)S(1)} %get-tuple-element.111), channel_id=1, source_target_pairs={{0,3},{1,2},{2,1},{3,0},{4,7},{5,6},{6,5},{7,4},{8,11},{9,10},{10,... | collective-permute-start | bytes 1769480 | tf_op jit(solution)/shard_map/ppermute | solution.py:654
  144.0 43.5 %copy-start.24 = (f32[6,192,128]{2,1,0:T(8,128)}, f32[6,192,128]{2,1,0:T(8,128)S(1)}, u32[]{:S(2)}) copy-start(f32[6,192,128]{2,1,0:T(8,128)S(1)} %zforward.7.refs_2_.refs_12_) | copy-start | bytes 1769476
  144.0 28.7 %copy-start.14 = (f32[6,192,256]{2,1,0:T(8,128)S(1)}, f32[6,192,256]{2,1,0:T(8,128)}, u32[]{:S(2)}) copy-start(f32[6,192,256]{2,1,0:T(8,128)} %refs_8_.6) | copy-start | bytes 3538948
  152.9 32.1 %collective-permute-start.18 = (f32[1,6,48,128]{3,2,1,0:T(8,128)S(1)}, f32[1,6,48,128]{3,2,1,0:T(8,128)S(1)}, u32[]{:S(2)}, u32[]{:S(2)}) collective-permute-start(f32[1,6,48,128]{3,2,1,0:T(8,128)S(1)} %copy-done.67), channel_id=1, source_target_pairs={{0,2},{1,3},{2,0},{3,1},{4,6},{5,7},{6,4},{7,5},{8,10},{9,11},{10,... | collective-permute-start | bytes 442376 | tf_op jit(solution)/shard_map/ppermute | solution.py:634
  168.0 10.8 %collective-permute-start.14 = (f32[1,6,48,128]{3,2,1,0:T(8,128)S(1)}, f32[1,6,48,128]{3,2,1,0:T(8,128)S(1)}, u32[]{:S(2)}, u32[]{:S(2)}) collective-permute-start(f32[1,6,48,128]{3,2,1,0:T(8,128)S(1)} %copy-done.71), channel_id=1, source_target_pairs={{0,3},{1,2},{2,1},{3,0},{4,7},{5,6},{6,5},{7,4},{8,11},{9,10},{10,... | collective-permute-start | bytes 442376 | tf_op jit(solution)/shard_map/ppermute | solution.py:634
  170.6 9.7 %collective-permute-start.16 = (f32[1,6,48,128]{3,2,1,0:T(8,128)S(1)}, f32[1,6,48,128]{3,2,1,0:T(8,128)S(1)}, u32[]{:S(2)}, u32[]{:S(2)}) collective-permute-start(f32[1,6,48,128]{3,2,1,0:T(8,128)S(1)} %copy-done.69), channel_id=1, source_target_pairs={{0,1},{1,0},{2,3},{3,2},{4,5},{5,4},{6,7},{7,6},{8,9},{9,8},{10,11... | collective-permute-start | bytes 442376 | tf_op jit(solution)/shard_map/ppermute | solution.py:634
  170.7 21.9 %collective-permute-start.20 = (f32[3,6,48,256]{3,2,1,0:T(8,128)S(1)}, f32[3,6,48,256]{3,2,1,0:T(8,128)S(1)}, u32[]{:S(2)}, u32[]{:S(2)}) collective-permute-start(f32[3,6,48,256]{3,2,1,0:T(8,128)S(1)} %get-tuple-element.113), channel_id=1, source_target_pairs={{0,1},{1,0},{2,3},{3,2},{4,5},{5,4},{6,7},{7,6},{8,9},{9,8},{10,11... | collective-permute-start | bytes 2654216 | tf_op jit(solution)/shard_map/ppermute | solution.py:634
  178.8 19.8 %collective-permute-start.24 = (f32[3,192,256]{2,1,0:T(8,128)S(1)}, f32[3,192,256]{2,1,0:T(8,128)S(1)}, u32[]{:S(2)}, u32[]{:S(2)}) collective-permute-start(f32[3,192,256]{2,1,0:T(8,128)S(1)} %get-tuple-element.177), channel_id=1, source_target_pairs={{0,28},{4,0},{8,4},{12,8},{16,12},{20,16},{24,20},{28,24},{1,29},{... | collective-permute-start | bytes 1769480 | tf_op jit(solution)/shard_map/ppermute | solution.py:740
  180.2 21.9 %collective-permute-start.23 = (f32[3,192,256]{2,1,0:T(8,128)}, f32[3,192,256]{2,1,0:T(8,128)S(1)}, u32[]{:S(2)}, u32[]{:S(2)}) collective-permute-start(f32[3,192,256]{2,1,0:T(8,128)} %get-tuple-element.178), channel_id=1, source_target_pairs={{0,4},{4,8},{8,12},{12,16},{16,20},{20,24},{24,28},{28,0},{1,5},{5... | collective-permute-start | bytes 1769480 | tf_op jit(solution)/shard_map/ppermute | solution.py:739
  190.6 13.0 %collective-permute-start.21 = (f32[5,192,128]{2,1,0:T(8,128)}, f32[5,192,128]{2,1,0:T(8,128)}, u32[]{:S(2)}, u32[]{:S(2)}) collective-permute-start(f32[5,192,128]{2,1,0:T(8,128)} %get-tuple-element.135), channel_id=1, source_target_pairs={{0,4},{4,8},{8,12},{12,16},{16,20},{20,24},{24,28},{28,0},{1,5},{5... | collective-permute-start | bytes 1474568 | tf_op jit(solution)/shard_map/ppermute | solution.py:715
  190.6 14.8 %collective-permute-start.22 = (f32[5,192,128]{2,1,0:T(8,128)}, f32[5,192,128]{2,1,0:T(8,128)}, u32[]{:S(2)}, u32[]{:S(2)}) collective-permute-start(f32[5,192,128]{2,1,0:T(8,128)} %get-tuple-element.136), channel_id=1, source_target_pairs={{0,28},{4,0},{8,4},{12,8},{16,12},{20,16},{24,20},{28,24},{1,29},{... | collective-permute-start | bytes 1474568 | tf_op jit(solution)/shard_map/ppermute | solution.py:716
  192.6 84.9 %collective-permute-start.28 = (f32[6,192,128]{2,1,0:T(8,128)}, f32[6,192,128]{2,1,0:T(8,128)}, u32[]{:S(2)}, u32[]{:S(2)}) collective-permute-start(f32[6,192,128]{2,1,0:T(8,128)} %get-tuple-element.125), channel_id=1, source_target_pairs={{0,3},{1,2},{2,1},{3,0},{4,7},{5,6},{6,5},{7,4},{8,11},{9,10},{10,... | collective-permute-start | bytes 1769480 | tf_op jit(solution)/shard_map/ppermute | solution.py:654
  198.7 78.8 %collective-permute-start.29 = (f32[6,192,128]{2,1,0:T(8,128)}, f32[6,192,128]{2,1,0:T(8,128)}, u32[]{:S(2)}, u32[]{:S(2)}) collective-permute-start(f32[6,192,128]{2,1,0:T(8,128)} %get-tuple-element.139), channel_id=1, source_target_pairs={{0,3},{1,2},{2,1},{3,0},{4,7},{5,6},{6,5},{7,4},{8,11},{9,10},{10,... | collective-permute-start | bytes 1769480 | tf_op jit(solution)/shard_map/ppermute | solution.py:654
  202.1 73.0 %collective-permute-start.27 = (f32[3,6,48,128]{3,2,1,0:T(8,128)}, f32[3,6,48,128]{3,2,1,0:T(8,128)S(1)}, u32[]{:S(2)}, u32[]{:S(2)}) collective-permute-start(f32[3,6,48,128]{3,2,1,0:T(8,128)} %copy-done.43), channel_id=1, source_target_pairs={{0,2},{1,3},{2,0},{3,1},{4,6},{5,7},{6,4},{7,5},{8,10},{9,11},{10,... | collective-permute-start | bytes 1327112 | tf_op jit(solution)/shard_map/ppermute | solution.py:634
  203.5 38.9 %collective-permute-start.25 = (f32[3,6,48,128]{3,2,1,0:T(8,128)}, f32[3,6,48,128]{3,2,1,0:T(8,128)S(1)}, u32[]{:S(2)}, u32[]{:S(2)}) collective-permute-start(f32[3,6,48,128]{3,2,1,0:T(8,128)} %copy-done.45), channel_id=1, source_target_pairs={{0,3},{1,2},{2,1},{3,0},{4,7},{5,6},{6,5},{7,4},{8,11},{9,10},{10,... | collective-permute-start | bytes 1327112 | tf_op jit(solution)/shard_map/ppermute | solution.py:634
  205.4 41.8 %collective-permute-start.26 = (f32[3,6,48,128]{3,2,1,0:T(8,128)}, f32[3,6,48,128]{3,2,1,0:T(8,128)S(1)}, u32[]{:S(2)}, u32[]{:S(2)}) collective-permute-start(f32[3,6,48,128]{3,2,1,0:T(8,128)} %copy-done.44), channel_id=1, source_target_pairs={{0,1},{1,0},{2,3},{3,2},{4,5},{5,4},{6,7},{7,6},{8,9},{9,8},{10,11... | collective-permute-start | bytes 1327112 | tf_op jit(solution)/shard_map/ppermute | solution.py:634
  221.7 53.5 %copy-start.42 = (f32[3,6,48,128]{3,2,1,0:T(8,128)S(1)}, f32[3,6,48,128]{3,2,1,0:T(8,128)}, u32[]{:S(2)}) copy-start(f32[3,6,48,128]{3,2,1,0:T(8,128)} %copy-done.41) | copy-start | bytes 1327108
  221.7 53.5 %copy-start.77 = (bf16[384,576]{1,0:T(8,128)(2,1)S(1)}, bf16[384,576]{1,0:T(8,128)(2,1)}, u32[]{:S(2)}) copy-start(bf16[384,576]{1,0:T(8,128)(2,1)} %constant.133.clone.refs_1_) | copy-start | bytes 1327108
  221.7 53.5 %copy-start.79 = (bf16[384,576]{1,0:T(8,128)(2,1)S(1)}, bf16[384,576]{1,0:T(8,128)(2,1)}, u32[]{:S(2)}) copy-start(bf16[384,576]{1,0:T(8,128)(2,1)} %constant.134.clone.refs_2_) | copy-start | bytes 1327108
  281.3 13.9 %collective-permute-start.30 = (f32[5,192,128]{2,1,0:T(8,128)S(1)}, f32[5,192,128]{2,1,0:T(8,128)S(1)}, u32[]{:S(2)}, u32[]{:S(2)}) collective-permute-start(f32[5,192,128]{2,1,0:T(8,128)S(1)} %get-tuple-element.150), channel_id=1, source_target_pairs={{0,4},{4,8},{8,12},{12,16},{16,20},{20,24},{24,28},{28,0},{1,5},{5... | collective-permute-start | bytes 1474568 | tf_op jit(solution)/shard_map/ppermute | solution.py:715
  281.4 13.9 %collective-permute-start.31 = (f32[5,192,128]{2,1,0:T(8,128)S(1)}, f32[5,192,128]{2,1,0:T(8,128)S(1)}, u32[]{:S(2)}, u32[]{:S(2)}) collective-permute-start(f32[5,192,128]{2,1,0:T(8,128)S(1)} %get-tuple-element.151), channel_id=1, source_target_pairs={{0,28},{4,0},{8,4},{12,8},{16,12},{20,16},{24,20},{28,24},{1,29},{... | collective-permute-start | bytes 1474568 | tf_op jit(solution)/shard_map/ppermute | solution.py:716
  283.1 32.0 %collective-permute-start.32 = (f32[3,6,48,128]{3,2,1,0:T(8,128)S(1)}, f32[3,6,48,128]{3,2,1,0:T(8,128)S(1)}, u32[]{:S(2)}, u32[]{:S(2)}) collective-permute-start(f32[3,6,48,128]{3,2,1,0:T(8,128)S(1)} %get-tuple-element.160), channel_id=1, source_target_pairs={{0,1},{1,2},{2,3},{3,0},{4,5},{5,6},{6,7},{7,4},{8,9},{9,10},{10,1... | collective-permute-start | bytes 1327112 | tf_op jit(solution)/shard_map/ppermute | solution.py:733
  284.7 49.6 %collective-permute-start.33 = (f32[3,6,48,128]{3,2,1,0:T(8,128)S(1)}, f32[3,6,48,128]{3,2,1,0:T(8,128)S(1)}, u32[]{:S(2)}, u32[]{:S(2)}) collective-permute-start(f32[3,6,48,128]{3,2,1,0:T(8,128)S(1)} %get-tuple-element.163), channel_id=1, source_target_pairs={{0,2},{1,3},{2,0},{3,1},{4,6},{5,7},{6,4},{7,5},{8,10},{9,11},{10,... | collective-permute-start | bytes 1327112 | tf_op jit(solution)/shard_map/ppermute | solution.py:733
  294.6 39.7 %collective-permute-start.34 = (f32[3,6,48,128]{3,2,1,0:T(8,128)S(1)}, f32[3,6,48,128]{3,2,1,0:T(8,128)S(1)}, u32[]{:S(2)}, u32[]{:S(2)}) collective-permute-start(f32[3,6,48,128]{3,2,1,0:T(8,128)S(1)} %get-tuple-element.166), channel_id=1, source_target_pairs={{0,3},{1,0},{2,1},{3,2},{4,7},{5,4},{6,5},{7,6},{8,11},{9,8},{10,9... | collective-permute-start | bytes 1327112 | tf_op jit(solution)/shard_map/ppermute | solution.py:733
  304.7 37.5 %collective-permute-start.35 = (f32[3,6,48,128]{3,2,1,0:T(8,128)S(1)}, f32[3,6,48,128]{3,2,1,0:T(8,128)S(1)}, u32[]{:S(2)}, u32[]{:S(2)}) collective-permute-start(f32[3,6,48,128]{3,2,1,0:T(8,128)S(1)} %get-tuple-element.168), channel_id=1, source_target_pairs={{0,1},{1,2},{2,3},{3,0},{4,5},{5,6},{6,7},{7,4},{8,9},{9,10},{10,1... | collective-permute-start | bytes 1327112 | tf_op jit(solution)/shard_map/ppermute | solution.py:733
  307.9 63.5 %collective-permute-start.36 = (f32[3,6,48,128]{3,2,1,0:T(8,128)S(1)}, f32[3,6,48,128]{3,2,1,0:T(8,128)S(1)}, u32[]{:S(2)}, u32[]{:S(2)}) collective-permute-start(f32[3,6,48,128]{3,2,1,0:T(8,128)S(1)} %get-tuple-element.169), channel_id=1, source_target_pairs={{0,2},{1,3},{2,0},{3,1},{4,6},{5,7},{6,4},{7,5},{8,10},{9,11},{10,... | collective-permute-start | bytes 1327112 | tf_op jit(solution)/shard_map/ppermute | solution.py:733
  315.1 56.2 %collective-permute-start.37 = (f32[3,6,48,128]{3,2,1,0:T(8,128)S(1)}, f32[3,6,48,128]{3,2,1,0:T(8,128)S(1)}, u32[]{:S(2)}, u32[]{:S(2)}) collective-permute-start(f32[3,6,48,128]{3,2,1,0:T(8,128)S(1)} %get-tuple-element.170), channel_id=1, source_target_pairs={{0,3},{1,0},{2,1},{3,2},{4,7},{5,4},{6,5},{7,6},{8,11},{9,8},{10,9... | collective-permute-start | bytes 1327112 | tf_op jit(solution)/shard_map/ppermute | solution.py:733
  320.2 51.1 %copy-start.10 = (bf16[1024,512]{1,0:T(8,128)(2,1)S(1)}, bf16[1024,512]{1,0:T(8,128)(2,1)}, u32[]{:S(2)}) copy-start(bf16[1024,512]{1,0:T(8,128)(2,1)} %constant.143.clone.refs_8_.refs_10_.refs_3_) | copy-start | bytes 3145732
  (79 other events, 547.6 us)
